TPU v7x, 256 devices: a whole 4x4x8 slice. The times are simulated.
256 devices in a mesh: seq: 64 (over y, z, core), frame: 4 (over x).
Axes of the slice: x: 4, y: 4, z: 8, core: 2. Of those that a mesh axis runs over, the one named last changes fastest.
Arguments:
- tokens: bfloat16 [4, 128, 128, 512], P('frame', 'seq'), may hold values from -6 to 6
- row_select: bfloat16 [4, 128, 128, 64], P('frame', 'seq'), may hold values from -2 to 2
- row_decay: float32 [4, 8, 128, 128], P('frame', None, 'seq'), may hold values from -1.5 to 0, as said below
- row_gain: float32 [512], replicated, may hold values from 0.25 to 1.75
- row_skip: float32 [8], replicated, may hold values from 0.5 to 1.5
- row_in: bfloat16 [512, 512], replicated, may hold values from -0.25 to 0.25
- row_out: bfloat16 [512, 512], replicated, may hold values from -0.25 to 0.25
- col_select: bfloat16 [4, 128, 128, 64], P('frame', 'seq'), may hold values from -2 to 2
- col_decay: float32 [4, 8, 128, 128], P('frame', None, 'seq'), may hold values from -1.5 to 0, as said below
- col_gain: float32 [512], replicated, may hold values from 0.25 to 1.75
- col_skip: float32 [8], replicated, may hold values from 0.5 to 1.5
- col_in: bfloat16 [512, 512], replicated, may hold values from -0.25 to 0.25
- col_out: bfloat16 [512, 512], replicated, may hold values from -0.25 to 0.25
- cotangent: bfloat16 [4, 128, 128, 512], P('frame', 'seq'), may hold values from -6 to 6
Outputs:
- mixed: bfloat16 [4, 128, 128, 512], P('frame', 'seq')
- grad_tokens: bfloat16 [4, 128, 128, 512], P('frame', 'seq')
Inputs may be any that keep to these rules, and one draw needn't show every extreme that they name: `row_decay`: every entry is below zero. `col_decay`: every entry is below zero.
All inputs are finite; a program needn't handle non-finite values.
Results may differ from a plain program's by a relative error of at most 0.013.
Values may be sent and summed in bfloat16 or wider, within the bound.
No kernel may reach another device: no remote copies, remote signals or barrier semaphores. Data moves between devices by JAX's collectives and lax.ppermute only.
A program may use at most 128 MiB of HBM per device.

v0:
```python
from functools import partial

import jax
import jax.numpy as jnp
from jax import lax
from jax.sharding import Mesh
from jax.sharding import PartitionSpec as P

SEQ = ("seq_0", "seq_1", "seq_2")


EPSILON = 1e-05
PRECISE = lax.Precision.HIGHEST


def filled_with(shard, identity):
    return jax.tree.map(
        lambda part, zero: jnp.zeros_like(part) + jnp.asarray(zero, part.dtype), shard, identity
    )


def collected_together(shard, axis):
    leaves = jax.tree.leaves(shard)
    turns = sorted(range(len(leaves)), key=lambda k: -leaves[k].size)
    width = (1, *leaves[turns[0]].shape)[-1]
    lines = [
        jnp.pad(leaves[k].reshape(-1), (0, -leaves[k].size % width)).reshape(-1, width)
        for k in turns
    ]
    both, at, found = (lax.all_gather(jnp.concatenate(lines), axis), 0, {})
    for k, line in zip(turns, lines):
        piece = both[:, at : at + len(line)].reshape(len(both), -1)
        found[k] = piece[:, : leaves[k].size].reshape(-1, *leaves[k].shape)
        at += len(line)
    numbers = iter(range(len(leaves)))
    return jax.tree.map(lambda _: found[next(numbers)], shard)


def prefix_by_axis(shard, axes, combine, identity, reverse):
    before = start = filled_with(shard, identity)
    subtotal = shard
    for axis in reversed(axes):
        peers, mine = (lax.axis_size(axis), lax.axis_index(axis))
        pieces = collected_together(subtotal, axis)
        inside, subtotal = (start, start)
        for k in reversed(range(peers)) if reverse else range(peers):
            passed = k > mine if reverse else k < mine
            subtotal = combine(subtotal, jax.tree.map(lambda part: part[k], pieces))
            inside = jax.tree.map(lambda new, old: jnp.where(passed, new, old), subtotal, inside)
        before = combine(inside, before)
    return before


def sent_to_all(shard, axis):
    copies = jnp.broadcast_to(shard, (lax.axis_size(axis), *shard.shape))
    return lax.all_to_all(copies, axis, split_axis=0, concat_axis=0, tiled=True)


def combined_pairwise(pieces, combine):
    while len(jax.tree.leaves(pieces)[0]) > 1:
        pieces = jax.vmap(combine)(*(pieces[side::2] for side in (0, 1)))
    return pieces[0]


def prefix(shard, axis, combine, identity, reverse):
    peers, mine = (lax.axis_size(axis), lax.axis_index(axis))
    passed = jnp.arange(peers) > mine if reverse else jnp.arange(peers) < mine

    def kept(part, zero, own):
        part = jnp.where(
            passed.reshape(-1, *(1 for _ in own.shape)), part, jnp.asarray(zero, own.dtype)
        )
        return part[::-1] if reverse else part

    pieces = sent_to_all(shard, axis)
    return combined_pairwise(kept(pieces, identity, shard), combine)


def over_pieces(shard, axis):
    blocks = lax.all_gather(shard, axis)
    return blocks.sum(axis=0)


def norm_rows(values, norm_gain):
    floats = values.astype(jnp.float32)
    factor = lax.rsqrt(jnp.mean(floats * floats, axis=-1, keepdims=True) + EPSILON)
    return (floats * factor * norm_gain).astype(jnp.bfloat16)


def block_terms(select_block, decay_block):
    extent = decay_block.shape[1]
    half_width = select_block.shape[1] // 2
    summed = jnp.cumsum(decay_block, axis=1)
    inward = jnp.sqrt(-jnp.expm1(2.0 * decay_block))
    target = lax.broadcasted_iota(jnp.int32, (extent, extent), 0)
    source = lax.broadcasted_iota(jnp.int32, (extent, extent), 1)
    causal = (target >= source).astype(jnp.float32)
    gap_sums = jnp.minimum(summed[:, :, None] - summed[:, None, :], 0.0)
    affinity = lax.dot_general(
        select_block[:, half_width:],
        select_block[:, :half_width],
        (((1,), (1,)), ((), ())),
        preferred_element_type=jnp.float32,
    )
    mixing = (jnp.exp(gap_sums) * causal * affinity[None] * inward[:, None, :]).astype(jnp.bfloat16)
    opening = jnp.exp(summed)
    ending = jnp.exp(summed[:, -1:] - summed) * inward
    return (mixing, opening, ending, jnp.exp(summed[:, -1]))


def forward_block(memory, block_piece, skip_gain):
    values, select_block, decay_block = block_piece
    half_width = select_block.shape[1] // 2
    mixing, opening, ending, through = block_terms(select_block, decay_block)
    floats = values.astype(jnp.float32)
    readout = select_block[:, half_width:].astype(jnp.float32)
    within = jnp.einsum("hts,shp->thp", mixing, values, preferred_element_type=jnp.float32)
    carried = jnp.einsum("tn,hpn->thp", readout, memory, precision=PRECISE) * opening.T[:, :, None]
    output = within + carried + skip_gain[None, :, None] * floats
    weighted = (floats * ending.T[:, :, None]).astype(jnp.bfloat16)
    memory = through[:, None, None] * memory + jnp.einsum(
        "shp,sn->hpn", weighted, select_block[:, :half_width], preferred_element_type=jnp.float32
    )
    return (memory, output)


def backward_block(memory, block_piece, skip_gain):
    values, select_block, decay_block = block_piece
    half_width = select_block.shape[1] // 2
    mixing, opening, ending, through = block_terms(select_block, decay_block)
    floats = values.astype(jnp.float32)
    writein = select_block[:, :half_width].astype(jnp.float32)
    within = jnp.einsum("hts,thp->shp", mixing, values, preferred_element_type=jnp.float32)
    carried = jnp.einsum("sn,hpn->shp", writein, memory, precision=PRECISE) * ending.T[:, :, None]
    output = within + carried + skip_gain[None, :, None] * floats
    weighted = (floats * opening.T[:, :, None]).astype(jnp.bfloat16)
    memory = through[:, None, None] * memory + jnp.einsum(
        "thp,tn->hpn", weighted, select_block[:, half_width:], preferred_element_type=jnp.float32
    )
    return (memory, output)


def local_pass(values, select, decay, skip_gain, backward):
    series_extent, model_width = values.shape
    head_count = decay.shape[0]
    half_width = select.shape[1] // 2
    block_size = min(512, series_extent)
    block_count = series_extent // block_size
    pieces = (
        values.reshape(block_count, block_size, head_count, model_width // head_count),
        select.reshape(block_count, block_size, select.shape[1]),
        decay.reshape(head_count, block_count, block_size).transpose(1, 0, 2),
    )
    zero_state = jnp.zeros((head_count, model_width // head_count, half_width), jnp.float32)
    advance = partial(backward_block if backward else forward_block, skip_gain=skip_gain)
    last_state, results = lax.scan(advance, zero_state, pieces, reverse=backward)
    summed = jnp.cumsum(decay, axis=1)
    return (results.reshape(series_extent, head_count, -1), last_state, summed)


def combine(earlier, later):
    return (earlier[0] * later[0], later[0][:, None, None] * earlier[1] + later[1])


def add_logs(earlier, later):
    return earlier + later


def frames_from_all(every_through, every_state, identity, backward):
    position = lax.axis_index("frame")
    frame_count = every_through.shape[0]
    earlier = identity
    ordering = range(frame_count - 1, -1, -1) if backward else range(frame_count)
    for other in ordering:
        keeping = other > position if backward else other < position
        taken = (
            jnp.where(keeping, every_through[other], 1.0),
            jnp.where(keeping, every_state[other], 0.0),
        )
        earlier = combine(earlier, taken)
    return earlier


def carry_chain(device_pair, spent, backward):
    identity = (jnp.ones_like(device_pair[0]), jnp.zeros_like(device_pair[1]))
    before = prefix_by_axis(device_pair, SEQ, combine, identity, backward)
    outside = prefix(spent, SEQ, add_logs, jnp.zeros_like(spent), not backward)
    decayed = jnp.exp(outside)[:, None, None] * device_pair[1]
    group_state, group_spent = (over_pieces(decayed, SEQ), over_pieces(spent, SEQ))
    group = (jnp.exp(group_spent), group_state)
    every_through, every_state = (
        lax.all_gather(group[0][None].astype(jnp.bfloat16), "frame", axis=0, tiled=True).astype(
            jnp.float32
        ),
        lax.all_gather(group[1][None].astype(jnp.bfloat16), "frame", axis=0, tiled=True).astype(
            jnp.float32
        ),
    )
    earlier = frames_from_all(every_through, every_state, identity, backward)
    return combine(earlier, before)[1]


def forward_start(inputs, select, decay, norm_gain, skip_gain, weight_in):
    normed = norm_rows(inputs, norm_gain)
    projected = jnp.dot(normed, weight_in, preferred_element_type=jnp.float32).astype(jnp.bfloat16)
    return local_pass(projected, select, decay, skip_gain, False)


def forward_finish(inputs, select, results, summed, entering, weight_out):
    series_extent, model_width = inputs.shape
    half_width = select.shape[1] // 2
    readout = select[:, half_width:].astype(jnp.float32)
    carried = (
        jnp.einsum("tn,hpn->thp", readout, entering, precision=PRECISE)
        * jnp.exp(summed).T[:, :, None]
    )
    scanned = (results + carried).reshape(series_extent, model_width).astype(jnp.bfloat16)
    total = inputs.astype(jnp.float32) + jnp.dot(
        scanned, weight_out, preferred_element_type=jnp.float32
    )
    return total.astype(jnp.bfloat16)


def backward_start(incoming, select, decay, skip_gain, weight_out):
    pulled = lax.dot_general(
        incoming, weight_out, (((1,), (1,)), ((), ())), preferred_element_type=jnp.float32
    ).astype(jnp.bfloat16)
    return local_pass(pulled, select, decay, skip_gain, True)


def backward_finish(
    inputs, incoming, select, decay, results, summed, entering, norm_gain, weight_in
):
    series_extent, model_width = inputs.shape
    half_width = select.shape[1] // 2
    inward = jnp.sqrt(-jnp.expm1(2.0 * decay))
    ending = jnp.exp(summed[:, -1:] - summed) * inward
    writein = select[:, :half_width].astype(jnp.float32)
    carried = jnp.einsum("sn,hpn->shp", writein, entering, precision=PRECISE) * ending.T[:, :, None]
    scanned = (results + carried).reshape(series_extent, model_width).astype(jnp.bfloat16)
    returned = lax.dot_general(
        scanned, weight_in, (((1,), (1,)), ((), ())), preferred_element_type=jnp.float32
    )
    floats = inputs.astype(jnp.float32)
    factor = lax.rsqrt(jnp.mean(floats * floats, axis=-1, keepdims=True) + EPSILON)
    scaled = norm_gain * returned
    result = (
        incoming.astype(jnp.float32)
        + factor * scaled
        - floats * factor**3 * jnp.mean(scaled * floats, axis=-1, keepdims=True)
    )
    return result.astype(jnp.bfloat16)


def mixer_forward(inputs, select, decay, norm_gain, skip_gain, weight_in, weight_out):
    results, last_state, summed = forward_start(
        inputs, select, decay, norm_gain, skip_gain, weight_in
    )
    spent = summed[:, -1]
    entering = carry_chain((jnp.exp(spent), last_state), spent, False)
    return forward_finish(inputs, select, results, summed, entering, weight_out)


def mixer_backward(inputs, incoming, select, decay, norm_gain, skip_gain, weight_in, weight_out):
    results, last_state, summed = backward_start(incoming, select, decay, skip_gain, weight_out)
    spent = summed[:, -1]
    entering = carry_chain((jnp.exp(spent), last_state), spent, True)
    return backward_finish(
        inputs, incoming, select, decay, results, summed, entering, norm_gain, weight_in
    )


def body(
    tokens,
    row_select,
    row_decay,
    row_gain,
    row_skip,
    row_in,
    row_out,
    col_select,
    col_decay,
    col_gain,
    col_skip,
    col_in,
    col_out,
    cotangent,
):
    model_width = tokens.shape[-1]
    head_count = row_decay.shape[1]
    doubled = row_select.shape[-1]
    row_share = row_decay.shape[2]
    col_share = col_decay.shape[2]
    seq_count = lax.axis_size(SEQ)
    row_inputs = tokens.reshape(-1, model_width)
    row_lam = row_decay.reshape(head_count, -1)
    col_lam = col_decay.reshape(head_count, -1)
    row_vectors = row_select.reshape(-1, doubled)
    col_vectors = col_select.reshape(-1, doubled)
    row_mixed = mixer_forward(row_inputs, row_vectors, row_lam, row_gain, row_skip, row_in, row_out)
    sending = row_mixed.reshape(row_share, seq_count, col_share, model_width).transpose(2, 1, 0, 3)
    arrived = lax.all_to_all(sending, SEQ, split_axis=1, concat_axis=1, tiled=True)
    col_tokens = arrived.reshape(-1, model_width)
    incoming = cotangent.reshape(-1, model_width)
    mixed = mixer_forward(col_tokens, col_vectors, col_lam, col_gain, col_skip, col_in, col_out)
    col_grad = mixer_backward(
        col_tokens, incoming, col_vectors, col_lam, col_gain, col_skip, col_in, col_out
    )
    returning = col_grad.reshape(col_share, seq_count, row_share, model_width)
    landed = lax.all_to_all(returning, SEQ, split_axis=1, concat_axis=1, tiled=True)
    row_grad = landed.transpose(2, 1, 0, 3).reshape(-1, model_width)
    grad_tokens = mixer_backward(
        row_inputs, row_grad, row_vectors, row_lam, row_gain, row_skip, row_in, row_out
    )
    return (mixed.reshape(cotangent.shape), grad_tokens.reshape(tokens.shape))


def solution(mesh):
    torus = Mesh(
        mesh.devices.reshape(4, 8, 2, mesh.shape["frame"]), ("seq_0", "seq_1", "seq_2", "frame")
    )
    in_specs = (
        P("frame", SEQ, None, None),
        P("frame", SEQ, None, None),
        P("frame", None, SEQ, None),
        P(),
        P(),
        P(),
        P(),
        P("frame", SEQ, None, None),
        P("frame", None, SEQ, None),
        P(),
        P(),
        P(),
        P(),
        P("frame", SEQ, None, None),
    )
    out_specs = (P("frame", SEQ, None, None), P("frame", SEQ, None, None))
    return jax.shard_map(body, mesh=torus, in_specs=in_specs, out_specs=out_specs, check_vma=False)
```

profile of v0, /device:TPU:8, one launch (start us, length us, event | category | flops | bytes accessed | tf_op | source)
XLA Modules:
  0.0 566.3 jit_solution(14886705953455302298)
XLA Ops:
  9.6 12.2 %all-to-all-start.2 = ((f32[64,1,8]{2,1,0:T(1,128)}), f32[64,1,8]{2,1,0:T(1,128)S(1)}, u32[]{:S(2)}, u32[]{:S(2)}) async-start(f32[64,1,8]{2,1,0:T(1,128)} %broadcast_in_dim.206), calls=%async_computation.2 | async-start | bytes 65536 | tf_op jit(solution)/shard_map/all_to_all | solution.py:56
  24.4 1.1 fusion.36
  25.5 1.1 fusion.31
  26.6 1.3 convolution_convert_fusion.3
  28.0 2.4 all-to-all-done.2
  31.1 7.9 %all-to-all-start = ((f32[64,1,8]{2,1,0:T(1,128)}), f32[64,1,8]{2,1,0:T(1,128)S(1)}, u32[]{:S(2)}, u32[]{:S(2)}) async-start(f32[64,1,8]{2,1,0:T(1,128)} %broadcast_in_dim.204), calls=%async_computation | async-start | bytes 65536 | tf_op jit(solution)/shard_map/all_to_all | solution.py:56
  39.3 8.3 %all-to-all-done = f32[64,1,8]{2,1,0:T(1,128)S(1)} async-done(((f32[64,1,8]{2,1,0:T(1,128)}), f32[64,1,8]{2,1,0:T(1,128)S(1)}, u32[]{:S(2)}, u32[]{:S(2)}) %all-to-all-start) | async-done | bytes 2080 | tf_op jit(solution)/shard_map/all_to_all | solution.py:56
  48.5 0.9 broadcast_multiply_fusion.3
  51.9 106.3 %all-reduce.14 = (f32[512]{0:T(512)S(1)}, f32[512]{0:T(512)S(1)}) all-reduce(f32[512]{0:T(512)S(1)} %dynamic-update-slice, f32[512]{0:T(512)S(1)} %dynamic-update-slice.2), channel_id=5, replica_groups=mesh['seq_0'=4,'seq_1'=8,'seq_2'=2,'frame'=4] {'seq_0','seq_1','seq_2'}, use_global_device_ids=true, to_apply=%add.10 | all-reduce | flops 1024 | bytes 8192
  159.8 1.0 broadcast_multiply_fusion.1
  162.7 10.4 %all-reduce.15 = (bf16[32]{0:T(256)(128)(2,1)S(1)}, bf16[32]{0:T(256)(128)(2,1)S(1)}) all-reduce(bf16[32]{0:T(256)(128)(2,1)S(1)} %dynamic-update-slice.1, bf16[32]{0:T(256)(128)(2,1)S(1)} %dynamic-update-slice.3), channel_id=6, replica_groups=mesh['seq_0'=4,'seq_1'=8,'seq_2'=2,'frame'=4] {'frame'}, use_global_device_ids=true, to_apply=%add.11 | all-reduce | flops 64 | bytes 256
  176.4 0.9 fusion.152
  177.3 1.1 fusion.13
  178.7 1.9 all-gather.24
  182.3 25.8 %all-gather.25 = f32[8,513,32]{1,2,0:T(8,128)S(1)} all-gather(f32[1,513,32]{1,2,0:T(8,128)S(1)} %maximum_bitcast_fusion), channel_id=3, replica_groups=mesh['seq_0'=4,'seq_1'=8,'seq_2'=2,'frame'=4] {'seq_1'}, dimensions={0}, use_global_device_ids=true | all-gather | bytes 590976 | tf_op jit(solution)/shard_map/all_gather | solution.py:30
  210.9 31.8 %all-gather.26 = f32[4,513,32]{1,2,0:T(8,128)S(1)} all-gather(f32[1,513,32]{1,2,0:T(8,128)S(1)} %maximum_bitcast_fusion.1), channel_id=4, replica_groups=mesh['seq_0'=4,'seq_1'=8,'seq_2'=2,'frame'=4] {'seq_0'}, dimensions={0}, use_global_device_ids=true | all-gather | bytes 328320 | tf_op jit(solution)/shard_map/all_gather | solution.py:30
  243.8 1.0 fusion.158
  245.0 4.5 reduce_sum.91
  249.6 12.4 %all-gather.6 = bf16[32,64,32]{1,2,0:T(8,128)(2,1)S(1)} all-gather(bf16[8,64,32]{1,2,0:T(8,128)(2,1)S(1)} %reduce_sum.91), channel_id=8, replica_groups=mesh['seq_0'=4,'seq_1'=8,'seq_2'=2,'frame'=4] {'frame'}, dimensions={0}, use_global_device_ids=true | all-gather | bytes 163840 | tf_op jit(solution)/shard_map/all_gather | solution.py:195
  264.6 0.9 copy.528
  265.5 7.6 %all-to-all-start.1 = ((bf16[2,64,2,512]{3,0,2,1:T(2,128)(2,1)}), bf16[2,64,2,512]{3,0,2,1:T(2,128)(2,1)S(1)}, u32[]{:S(2)}, u32[]{:S(2)}) async-start(bf16[2,64,2,512]{3,0,2,1:T(2,128)(2,1)} %bitcast.997), calls=%async_computation.1 | async-start | bytes 524288 | tf_op jit(solution)/shard_map/all_to_all | solution.py:302
  273.9 0.9 fusion.143
  275.7 9.0 %all-to-all-done.1 = bf16[2,64,2,512]{3,0,2,1:T(2,128)(2,1)S(1)} async-done(((bf16[2,64,2,512]{3,0,2,1:T(2,128)(2,1)}), bf16[2,64,2,512]{3,0,2,1:T(2,128)(2,1)S(1)}, u32[]{:S(2)}, u32[]{:S(2)}) %all-to-all-start.1) | async-done | bytes 262176 | tf_op jit(solution)/shard_map/all_to_all | solution.py:302
  286.5 1.6 broadcast_multiply_fusion.2
  288.7 1.1 fusion.9
  289.9 1.1 fusion.5
  291.0 1.1 fusion.1
  293.1 4.5 reduce_sum.112
  297.6 12.4 %all-gather.18 = bf16[32,64,32]{1,2,0:T(8,128)(2,1)S(1)} all-gather(bf16[8,64,32]{1,2,0:T(8,128)(2,1)S(1)} %reduce_sum.112), channel_id=20, replica_groups=mesh['seq_0'=4,'seq_1'=8,'seq_2'=2,'frame'=4] {'frame'}, dimensions={0}, use_global_device_ids=true | all-gather | bytes 163840 | tf_op jit(solution)/shard_map/all_gather | solution.py:195
  310.0 0.9 copy_convert_fusion.1
  311.7 1.9 all-gather.30
  315.4 26.5 %all-gather.31 = f32[8,513,32]{1,2,0:T(8,128)S(1)} all-gather(f32[1,513,32]{1,2,0:T(8,128)S(1)} %maximum_bitcast_fusion.4), channel_id=17, replica_groups=mesh['seq_0'=4,'seq_1'=8,'seq_2'=2,'frame'=4] {'seq_1'}, dimensions={0}, use_global_device_ids=true | all-gather | bytes 590976 | tf_op jit(solution)/shard_map/all_gather | solution.py:30
  342.6 0.8 fusion.191
  343.5 1.6 squeeze.515
  345.0 1.6 squeeze.514
  346.6 1.6 squeeze.513
  348.2 1.6 squeeze.512
  349.7 1.6 squeeze.511
  351.3 1.6 squeeze.510
  352.9 1.6 squeeze.509
  355.2 1.0 copy.474
  362.9 12.6 %all-gather.32 = f32[4,513,32]{1,2,0:T(8,128)S(1)} all-gather(f32[1,513,32]{1,2,0:T(8,128)S(1)} %maximum_bitcast_fusion.5), channel_id=18, replica_groups=mesh['seq_0'=4,'seq_1'=8,'seq_2'=2,'frame'=4] {'seq_0'}, dimensions={0}, use_global_device_ids=true | all-gather | bytes 328320 | tf_op jit(solution)/shard_map/all_gather | solution.py:30
  376.2 1.6 squeeze.507
  377.8 1.6 squeeze.506
  381.8 2.1 fusion.59
  384.4 1.5 fusion.23
  386.7 1.0 copy.460
  387.7 6.2 %all-to-all-start.3 = ((bf16[2,64,2,512]{3,0,2,1:T(2,128)(2,1)}), bf16[2,64,2,512]{3,0,2,1:T(2,128)(2,1)S(1)}, u32[]{:S(2)}, u32[]{:S(2)}) async-start(bf16[2,64,2,512]{3,0,2,1:T(2,128)(2,1)} %copy.460), calls=%async_computation.3 | async-start | bytes 524288 | tf_op jit(solution)/shard_map/all_to_all | solution.py:310
  394.0 2.1 all-gather.27
  398.5 7.0 %all-to-all-done.3 = bf16[2,64,2,512]{3,0,2,1:T(2,128)(2,1)S(1)} async-done(((bf16[2,64,2,512]{3,0,2,1:T(2,128)(2,1)}), bf16[2,64,2,512]{3,0,2,1:T(2,128)(2,1)S(1)}, u32[]{:S(2)}, u32[]{:S(2)}) %all-to-all-start.3) | async-done | bytes 262176 | tf_op jit(solution)/shard_map/all_to_all | solution.py:310
  406.3 0.9 broadcast_multiply_fusion
  407.4 26.2 %all-gather.28 = f32[8,513,32]{1,2,0:T(8,128)S(1)} all-gather(f32[1,513,32]{1,2,0:T(8,128)S(1)} %maximum_bitcast_fusion.2), channel_id=10, replica_groups=mesh['seq_0'=4,'seq_1'=8,'seq_2'=2,'frame'=4] {'seq_1'}, dimensions={0}, use_global_device_ids=true | all-gather | bytes 590976 | tf_op jit(solution)/shard_map/all_gather | solution.py:30
  441.9 13.0 %all-gather.29 = f32[4,513,32]{1,2,0:T(8,128)S(1)} all-gather(f32[1,513,32]{1,2,0:T(8,128)S(1)} %maximum_bitcast_fusion.3), channel_id=11, replica_groups=mesh['seq_0'=4,'seq_1'=8,'seq_2'=2,'frame'=4] {'seq_0'}, dimensions={0}, use_global_device_ids=true | all-gather | bytes 328320 | tf_op jit(solution)/shard_map/all_gather | solution.py:30
  459.8 1.9 all-gather.33
  464.1 26.8 %all-gather.34 = f32[8,513,32]{1,2,0:T(8,128)S(1)} all-gather(f32[1,513,32]{1,2,0:T(8,128)S(1)} %maximum_bitcast_fusion.6), channel_id=22, replica_groups=mesh['seq_0'=4,'seq_1'=8,'seq_2'=2,'frame'=4] {'seq_1'}, dimensions={0}, use_global_device_ids=true | all-gather | bytes 590976 | tf_op jit(solution)/shard_map/all_gather | solution.py:30
  499.0 13.0 %all-gather.35 = f32[4,513,32]{1,2,0:T(8,128)S(1)} all-gather(f32[1,513,32]{1,2,0:T(8,128)S(1)} %maximum_bitcast_fusion.7), channel_id=23, replica_groups=mesh['seq_0'=4,'seq_1'=8,'seq_2'=2,'frame'=4] {'seq_0'}, dimensions={0}, use_global_device_ids=true | all-gather | bytes 328320 | tf_op jit(solution)/shard_map/all_gather | solution.py:30
  516.8 4.5 reduce_sum.97
  521.5 12.4 %all-gather.13 = bf16[32,64,32]{1,2,0:T(8,128)(2,1)S(1)} all-gather(bf16[8,64,32]{1,2,0:T(8,128)(2,1)S(1)} %reduce_sum.97), channel_id=15, replica_groups=mesh['seq_0'=4,'seq_1'=8,'seq_2'=2,'frame'=4] {'frame'}, dimensions={0}, use_global_device_ids=true | all-gather | bytes 163840 | tf_op jit(solution)/shard_map/all_gather | solution.py:195
  534.1 1.8 fusion.68
  537.2 1.0 fusion.21
  538.4 4.6 reduce_sum.114
  543.0 12.4 %all-gather.23 = bf16[32,64,32]{1,2,0:T(8,128)(2,1)S(1)} all-gather(bf16[8,64,32]{1,2,0:T(8,128)(2,1)S(1)} %reduce_sum.114), channel_id=25, replica_groups=mesh['seq_0'=4,'seq_1'=8,'seq_2'=2,'frame'=4] {'frame'}, dimensions={0}, use_global_device_ids=true | all-gather | bytes 163840 | tf_op jit(solution)/shard_map/all_gather | solution.py:195
  555.7 1.1 fusion.50
  558.8 0.9 fusion.34
  (728 shorter events, 77.4 us)
Async XLA Ops:
  7.2 278.8 %copy-start = (bf16[512,512]{1,0:T(8,128)(2,1)S(1)}, bf16[512,512]{1,0:T(8,128)(2,1)}, u32[]{:S(2)}) copy-start(bf16[512,512]{1,0:T(8,128)(2,1)} %param.25) | copy-start | bytes 1572868
  7.2 31.9 %copy-start.67 = (bf16[1,2,128,64]{2,3,1,0:T(8,128)(2,1)S(1)}, bf16[1,2,128,64]{2,3,1,0:T(8,128)(2,1)}, u32[]{:S(2)}) copy-start(bf16[1,2,128,64]{2,3,1,0:T(8,128)(2,1)} %param.15) | copy-start | bytes 98308
  8.0 42.2 %copy-start.164 = (u32[256]{0:T(256)S(1)}, u32[256]{0:T(256)}, u32[]{:S(2)}) copy-start(u32[256]{0:T(256)} %constant.145) | copy-start | bytes 3076
  8.8 151.0 %copy-start.50 = (f32[256,8]{0,1:T(8,128)}, f32[256,8]{0,1:T(8,128)S(1)}, u32[]{:S(2)}) copy-start(f32[256,8]{0,1:T(8,128)S(1)} %get-tuple-element.85) | copy-start | bytes 24580
  8.8 167.0 %copy-start.65 = (f32[8,256]{1,0:T(8,128)}, f32[8,256]{1,0:T(8,128)S(1)}, u32[]{:S(2)}) copy-start(f32[8,256]{1,0:T(8,128)S(1)} %get-tuple-element.86) | copy-start | bytes 24580
  9.6 148.7 %copy-start.68 = (bf16[1,2,128,64]{2,3,1,0:T(8,128)(2,1)S(1)}, bf16[1,2,128,64]{2,3,1,0:T(8,128)(2,1)}, u32[]{:S(2)}) copy-start(bf16[1,2,128,64]{2,3,1,0:T(8,128)(2,1)} %param.21) | copy-start | bytes 98308
  9.6 20.8 %all-to-all-start.2 = ((f32[64,1,8]{2,1,0:T(1,128)}), f32[64,1,8]{2,1,0:T(1,128)S(1)}, u32[]{:S(2)}, u32[]{:S(2)}) async-start(f32[64,1,8]{2,1,0:T(1,128)} %broadcast_in_dim.206), calls=%async_computation.2 | async-start | bytes 65536 | tf_op jit(solution)/shard_map/all_to_all | solution.py:56
  24.1 134.3 %copy-start.3 = (bf16[512,512]{1,0:T(8,128)(2,1)S(1)}, bf16[512,512]{1,0:T(8,128)(2,1)}, u32[]{:S(2)}) copy-start(bf16[512,512]{1,0:T(8,128)(2,1)} %param.26) | copy-start | bytes 1572868
  24.1 134.3 %copy-start.8 = (bf16[1,2,128,512]{3,2,1,0:T(8,128)(2,1)S(1)}, bf16[1,2,128,512]{3,2,1,0:T(8,128)(2,1)}, u32[]{:S(2)}) copy-start(bf16[1,2,128,512]{3,2,1,0:T(8,128)(2,1)} %param.27) | copy-start | bytes 786436
  24.2 24.1 %copy-start.62 = (f32[8,256]{1,0:T(8,128)}, f32[8,256]{1,0:T(8,128)S(1)}, u32[]{:S(2)}) copy-start(f32[8,256]{1,0:T(8,128)S(1)} %get-tuple-element.98) | copy-start | bytes 24580
  24.2 153.2 %copy-start.53 = (f32[256,8]{0,1:T(8,128)}, f32[256,8]{0,1:T(8,128)S(1)}, u32[]{:S(2)}) copy-start(f32[256,8]{0,1:T(8,128)S(1)} %get-tuple-element.90) | copy-start | bytes 24580
  27.9 131.6 %copy-start.69 = (f32[1,8,2,128]{3,2,1,0:T(2,128)S(1)}, f32[1,8,2,128]{3,2,1,0:T(2,128)}, u32[]{:S(2)}) copy-start(f32[1,8,2,128]{3,2,1,0:T(2,128)} %param.22) | copy-start | bytes 24580
  28.0 130.4 %copy-start.47 = (f32[256,8]{0,1:T(8,128)}, f32[256,8]{0,1:T(8,128)S(1)}, u32[]{:S(2)}) copy-start(f32[256,8]{0,1:T(8,128)S(1)} %multiply_bitcast_fusion.1) | copy-start | bytes 24580
  28.0 130.2 %copy-start.156 = (f32[8]{0:T(128)}, f32[8]{0:T(128)S(1)}, u32[]{:S(2)}) copy-start(f32[8]{0:T(128)S(1)} %get-tuple-element.245) | copy-start | bytes 100
  31.1 16.5 %all-to-all-start = ((f32[64,1,8]{2,1,0:T(1,128)}), f32[64,1,8]{2,1,0:T(1,128)S(1)}, u32[]{:S(2)}, u32[]{:S(2)}) async-start(f32[64,1,8]{2,1,0:T(1,128)} %broadcast_in_dim.204), calls=%async_computation | async-start | bytes 65536 | tf_op jit(solution)/shard_map/all_to_all | solution.py:56
  39.0 205.8 %all-gather.41.cloned.1.call-start = ((), (), s32[]{:S(2)}) async-start(), calls=%async_computation.4 | async-start | bytes 8519680 | tf_op jit(solution)/shard_map/all_gather | solution.py:80
  39.1 251.8 %copy-start.10 = (bf16[8,8,2,128]{3,1,2,0:T(8,128)(2,1)}, bf16[8,8,2,128]{3,1,2,0:T(8,128)(2,1)S(1)}, u32[]{:S(2)}) copy-start(bf16[8,8,2,128]{3,1,2,0:T(8,128)(2,1)S(1)} %copy.530) | copy-start | bytes 98308
  39.3 121.6 %copy-start.163 = (u32[256]{0:T(256)S(1)}, u32[256]{0:T(256)}, u32[]{:S(2)}) copy-start(u32[256]{0:T(256)} %constant.150) | copy-start | bytes 3076
  49.5 243.7 %all-gather.45.cloned.1.call-start = ((), (), s32[]{:S(2)}) async-start(), calls=%async_computation.6 | async-start | bytes 8519680 | tf_op jit(solution)/shard_map/all_gather | solution.py:80
  158.4 225.5 %copy-start.13 = (bf16[8,8,2,128]{3,1,2,0:T(8,128)(2,1)}, bf16[8,8,2,128]{3,1,2,0:T(8,128)(2,1)S(1)}, u32[]{:S(2)}) copy-start(bf16[8,8,2,128]{3,1,2,0:T(8,128)(2,1)S(1)} %copy.529) | copy-start | bytes 98308
  158.9 19.7 %copy-start.6 = (bf16[256,512]{0,1:T(8,128)(2,1)}, bf16[256,512]{0,1:T(8,128)(2,1)S(1)}, u32[]{:S(2)}) copy-start(bf16[256,512]{0,1:T(8,128)(2,1)S(1)} %copy.451) | copy-start | bytes 786436
  159.6 18.9 %copy-start.158 = (f32[8]{0:T(128)}, f32[8]{0:T(128)S(1)}, u32[]{:S(2)}) copy-start(f32[8]{0:T(128)S(1)} %get-tuple-element.243) | copy-start | bytes 100
  244.8 17.2 %copy-start.33 = (f32[8,64,32]{1,0,2:T(8,128)S(1)}, f32[8,64,32]{1,0,2:T(8,128)}, u32[]{:S(2)}) copy-start(f32[8,64,32]{1,0,2:T(8,128)} %squeeze.444) | copy-start | bytes 196612
  244.8 17.2 %copy-start.109 = (f32[8]{0:T(128)S(1)}, f32[8]{0:T(128)}, u32[]{:S(2)}) copy-start(f32[8]{0:T(128)} %copy-done.108) | copy-start | bytes 100
  244.9 17.2 %copy-start.111 = (f32[8]{0:T(128)S(1)}, f32[8]{0:T(128)}, u32[]{:S(2)}) copy-start(f32[8]{0:T(128)} %copy-done.110) | copy-start | bytes 100
  244.9 17.2 %copy-start.113 = (f32[8]{0:T(128)S(1)}, f32[8]{0:T(128)}, u32[]{:S(2)}) copy-start(f32[8]{0:T(128)} %copy-done.112) | copy-start | bytes 100
  244.9 17.2 %copy-start.115 = (f32[8]{0:T(128)S(1)}, f32[8]{0:T(128)}, u32[]{:S(2)}) copy-start(f32[8]{0:T(128)} %copy-done.114) | copy-start | bytes 100
  244.9 17.2 %copy-start.117 = (f32[8]{0:T(128)S(1)}, f32[8]{0:T(128)}, u32[]{:S(2)}) copy-start(f32[8]{0:T(128)} %copy-done.116) | copy-start | bytes 100
  244.9 17.2 %copy-start.119 = (f32[8]{0:T(128)S(1)}, f32[8]{0:T(128)}, u32[]{:S(2)}) copy-start(f32[8]{0:T(128)} %copy-done.118) | copy-start | bytes 100
  265.5 20.5 %copy-start.81 = (f32[512]{0:T(512)S(1)}, f32[512]{0:T(512)}, u32[]{:S(2)}) copy-start(f32[512]{0:T(512)} %param.23) | copy-start | bytes 6148
  265.5 19.2 %all-to-all-start.1 = ((bf16[2,64,2,512]{3,0,2,1:T(2,128)(2,1)}), bf16[2,64,2,512]{3,0,2,1:T(2,128)(2,1)S(1)}, u32[]{:S(2)}, u32[]{:S(2)}) async-start(bf16[2,64,2,512]{3,0,2,1:T(2,128)(2,1)} %bitcast.997), calls=%async_computation.1 | async-start | bytes 524288 | tf_op jit(solution)/shard_map/all_to_all | solution.py:302
  273.1 243.6 %all-gather.43.cloned.1.call-start = ((), (), s32[]{:S(2)}) async-start(), calls=%async_computation.5 | async-start | bytes 8519680 | tf_op jit(solution)/shard_map/all_gather | solution.py:80
  293.1 17.9 %copy-start.60 = (f32[1,32]{0,1:T(8,128)S(1)}, f32[1,32]{0,1:T(8,128)}, u32[]{:S(2)}) copy-start(f32[1,32]{0,1:T(8,128)} %copy.445) | copy-start | bytes 388
  315.2 40.9 %copy-start.148 = (f32[8]{0:T(128)}, f32[8]{0:T(128)S(1)}, u32[]{:S(2)}) copy-start(f32[8]{0:T(128)S(1)} %slice_bitcast_fusion.21) | copy-start | bytes 100
  345.0 35.9 %copy-start.71 = (f32[256]{0:T(256)S(1)}, f32[256]{0:T(256)}, u32[]{:S(2)}) copy-start(f32[256]{0:T(256)} %copy-done.70) | copy-start | bytes 3076
  362.9 21.0 %copy-start.57 = (f32[256,8]{0,1:T(8,128)S(1)}, f32[256,8]{0,1:T(8,128)}, u32[]{:S(2)}) copy-start(f32[256,8]{0,1:T(8,128)} %multiply_bitcast_fusion) | copy-start | bytes 24580
  387.6 18.6 %copy-start.11 = (bf16[8,8,2,128]{3,1,2,0:T(8,128)(2,1)S(1)}, bf16[8,8,2,128]{3,1,2,0:T(8,128)(2,1)}, u32[]{:S(2)}) copy-start(bf16[8,8,2,128]{3,1,2,0:T(8,128)(2,1)} %copy-done.10) | copy-start | bytes 98308
  387.7 18.6 %copy-start.55 = (f32[256,8]{0,1:T(8,128)S(1)}, f32[256,8]{0,1:T(8,128)}, u32[]{:S(2)}) copy-start(f32[256,8]{0,1:T(8,128)} %copy-done.53) | copy-start | bytes 24580
  387.7 18.6 %copy-start.157 = (f32[8]{0:T(128)S(1)}, f32[8]{0:T(128)}, u32[]{:S(2)}) copy-start(f32[8]{0:T(128)} %copy-done.156) | copy-start | bytes 100
  387.7 18.6 %copy-start.159 = (f32[8]{0:T(128)S(1)}, f32[8]{0:T(128)}, u32[]{:S(2)}) copy-start(f32[8]{0:T(128)} %exponential_bitcast_fusion.2) | copy-start | bytes 100
  387.7 17.8 %all-to-all-start.3 = ((bf16[2,64,2,512]{3,0,2,1:T(2,128)(2,1)}), bf16[2,64,2,512]{3,0,2,1:T(2,128)(2,1)S(1)}, u32[]{:S(2)}, u32[]{:S(2)}) async-start(bf16[2,64,2,512]{3,0,2,1:T(2,128)(2,1)} %copy.460), calls=%async_computation.3 | async-start | bytes 524288 | tf_op jit(solution)/shard_map/all_to_all | solution.py:310
  393.9 144.3 %all-gather.47.cloned.1.call-start = ((), (), s32[]{:S(2)}) async-start(), calls=%async_computation.7 | async-start | bytes 8519680 | tf_op jit(solution)/shard_map/all_gather | solution.py:80
  407.2 26.3 %copy-start.140 = (f32[8]{0:T(128)}, f32[8]{0:T(128)S(1)}, u32[]{:S(2)}) copy-start(f32[8]{0:T(128)S(1)} %slice_bitcast_fusion.32) | copy-start | bytes 100
  434.4 24.7 %copy-start.84 = (f32[2,32]{1,0:T(2,128)S(1)}, f32[2,32]{1,0:T(2,128)}, u32[]{:S(2)}) copy-start(f32[2,32]{1,0:T(2,128)} %copy-done.83) | copy-start | bytes 772
  434.4 24.7 %copy-start.152 = (f32[8]{0:T(128)S(1)}, f32[8]{0:T(128)}, u32[]{:S(2)}) copy-start(f32[8]{0:T(128)} %copy-done.151) | copy-start | bytes 100
  463.3 27.6 %copy-start.135 = (f32[8]{0:T(128)}, f32[8]{0:T(128)S(1)}, u32[]{:S(2)}) copy-start(f32[8]{0:T(128)S(1)} %get-tuple-element.218) | copy-start | bytes 100
  463.9 27.0 %copy-start.141 = (f32[8]{0:T(128)}, f32[8]{0:T(128)S(1)}, u32[]{:S(2)}) copy-start(f32[8]{0:T(128)S(1)} %slice_bitcast_fusion.10) | copy-start | bytes 100
  538.2 17.3 %copy-start.19 = (f32[8,64,32]{1,0,2:T(8,128)S(1)}, f32[8,64,32]{1,0,2:T(8,128)}, u32[]{:S(2)}) copy-start(f32[8,64,32]{1,0,2:T(8,128)} %squeeze.546) | copy-start | bytes 196612
  538.2 17.3 %copy-start.20 = (f32[8,64,32]{1,0,2:T(8,128)S(1)}, f32[8,64,32]{1,0,2:T(8,128)}, u32[]{:S(2)}) copy-start(f32[8,64,32]{1,0,2:T(8,128)} %squeeze.545) | copy-start | bytes 196612
  538.2 17.3 %copy-start.21 = (f32[8,64,32]{1,0,2:T(8,128)S(1)}, f32[8,64,32]{1,0,2:T(8,128)}, u32[]{:S(2)}) copy-start(f32[8,64,32]{1,0,2:T(8,128)} %squeeze.544) | copy-start | bytes 196612
  538.2 17.3 %copy-start.22 = (f32[8,64,32]{1,0,2:T(8,128)S(1)}, f32[8,64,32]{1,0,2:T(8,128)}, u32[]{:S(2)}) copy-start(f32[8,64,32]{1,0,2:T(8,128)} %squeeze.543) | copy-start | bytes 196612
  538.2 17.3 %copy-start.23 = (f32[8,64,32]{1,0,2:T(8,128)S(1)}, f32[8,64,32]{1,0,2:T(8,128)}, u32[]{:S(2)}) copy-start(f32[8,64,32]{1,0,2:T(8,128)} %squeeze.542) | copy-start | bytes 196612
  538.3 17.3 %copy-start.24 = (f32[8,64,32]{1,0,2:T(8,128)S(1)}, f32[8,64,32]{1,0,2:T(8,128)}, u32[]{:S(2)}) copy-start(f32[8,64,32]{1,0,2:T(8,128)} %squeeze.541) | copy-start | bytes 196612
  538.3 17.3 %copy-start.25 = (f32[8,64,32]{1,0,2:T(8,128)S(1)}, f32[8,64,32]{1,0,2:T(8,128)}, u32[]{:S(2)}) copy-start(f32[8,64,32]{1,0,2:T(8,128)} %squeeze.540) | copy-start | bytes 196612
  538.3 17.3 %copy-start.26 = (f32[8,64,32]{1,0,2:T(8,128)S(1)}, f32[8,64,32]{1,0,2:T(8,128)}, u32[]{:S(2)}) copy-start(f32[8,64,32]{1,0,2:T(8,128)} %squeeze.539) | copy-start | bytes 196612
  538.3 17.3 %copy-start.27 = (f32[8,64,32]{1,0,2:T(8,128)S(1)}, f32[8,64,32]{1,0,2:T(8,128)}, u32[]{:S(2)}) copy-start(f32[8,64,32]{1,0,2:T(8,128)} %squeeze.538) | copy-start | bytes 196612
  538.3 17.3 %copy-start.28 = (f32[8,64,32]{1,0,2:T(8,128)S(1)}, f32[8,64,32]{1,0,2:T(8,128)}, u32[]{:S(2)}) copy-start(f32[8,64,32]{1,0,2:T(8,128)} %squeeze.537) | copy-start | bytes 196612
  538.3 17.3 %copy-start.29 = (f32[8,64,32]{1,0,2:T(8,128)S(1)}, f32[8,64,32]{1,0,2:T(8,128)}, u32[]{:S(2)}) copy-start(f32[8,64,32]{1,0,2:T(8,128)} %squeeze.536) | copy-start | bytes 196612
  538.3 17.3 %copy-start.30 = (f32[8,64,32]{1,0,2:T(8,128)S(1)}, f32[8,64,32]{1,0,2:T(8,128)}, u32[]{:S(2)}) copy-start(f32[8,64,32]{1,0,2:T(8,128)} %squeeze.535) | copy-start | bytes 196612
  538.3 17.3 %copy-start.31 = (f32[8,64,32]{1,0,2:T(8,128)S(1)}, f32[8,64,32]{1,0,2:T(8,128)}, u32[]{:S(2)}) copy-start(f32[8,64,32]{1,0,2:T(8,128)} %squeeze.534) | copy-start | bytes 196612
  538.3 17.3 %copy-start.32 = (f32[8,64,32]{1,0,2:T(8,128)S(1)}, f32[8,64,32]{1,0,2:T(8,128)}, u32[]{:S(2)}) copy-start(f32[8,64,32]{1,0,2:T(8,128)} %squeeze.533) | copy-start | bytes 196612
  538.3 17.3 %copy-start.102 = (f32[8]{0:T(128)S(1)}, f32[8]{0:T(128)}, u32[]{:S(2)}) copy-start(f32[8]{0:T(128)} %copy-done.101) | copy-start | bytes 100
  538.4 17.3 %copy-start.104 = (f32[8]{0:T(128)S(1)}, f32[8]{0:T(128)}, u32[]{:S(2)}) copy-start(f32[8]{0:T(128)} %copy-done.103) | copy-start | bytes 100
  538.4 17.3 %copy-start.106 = (f32[8]{0:T(128)S(1)}, f32[8]{0:T(128)}, u32[]{:S(2)}) copy-start(f32[8]{0:T(128)} %copy-done.105) | copy-start | bytes 100
  (110 other events, 808.2 us)
Sparse Core Ops, SparseCore 0:
  49.6 77.4 all-gather.40
  161.0 96.4 all-gather.44
  288.3 77.5 all-gather.42
  407.3 81.1 all-gather.46
where the time goes:
time: 568 us; the launch traced here: 566 us
  blocking collectives  350 us (62%)
  local copies, waits for them, and re-layouts  74.8 us (13%)
  other arithmetic  42.1 us (7%)
  starting transfers between devices  34.2 us (6%)
  waiting for transfers between devices  26.7 us (5%)
  matrix products  20.8 us (4%)
  between operations  17.9 us (3%)
    all_gather x12, blocking collectives, collected_together(): both, at, found = (lax.all_gather(jnp.concatenate(lines), axis), 0, {})  184 us
    unnamed x2, blocking collectives  117 us
    all_gather x4, blocking collectives, carry_chain(): lax.all_gather(group[1][None].astype(jnp.bfloat16), 'frame', axis=0, tile...  49.6 us
    squeeze x60, local copies, waits for them, and re-layouts, prefix_by_axis(): subtotal = combine(subtotal, jax.tree.map(lambda part: part[k], pieces))  40.8 us
    all_to_all x2, starting transfers between devices, sent_to_all(): return lax.all_to_all(copies, axis, split_axis=0, concat_axis=0, tiled=True)  20.2 us
    reduce_sum x6, other arithmetic, over_pieces(): return blocks.sum(axis=0)  18.2 us
  transfers between devices with their start and end apart: 8, of which 4 were waited for; matrix products, arithmetic and copies ran while one was open for 21% of the time, Pallas kernels for 0%

commit v1 on v0

v1 whole, which is shorter than its diff:
```python
from functools import partial

import jax
import jax.numpy as jnp
from jax import lax
from jax.experimental import pallas as pl
from jax.experimental.pallas import tpu as pltpu
from jax.sharding import Mesh
from jax.sharding import PartitionSpec as P

SEQ = ("seq_0", "seq_1", "seq_2")
INNER = ("seq_1", "seq_2")
OUTER = ("frame", "seq_0")

EPSILON = 1e-05
LOG2E = 1.4426950408889634

TOK = 256
WIDTH = 512
HEADS = 8
PART = 64
STATE = 32
GROUP = 16
ROWS8 = 8
HALF = 256

F32 = jnp.float32
BF16 = jnp.bfloat16


def iota(shape, axis):
    return lax.broadcasted_iota(jnp.int32, shape, axis)


def nn(left, right):
    return lax.dot_general(left, right, (((1,), (0,)), ((), ())), preferred_element_type=F32)


def nt(left, right):
    return lax.dot_general(left, right, (((1,), (1,)), ((), ())), preferred_element_type=F32)


def pieces(values, count):
    out = []
    rest = values
    for _ in range(count):
        piece = rest.astype(BF16)
        out.append(piece)
        rest = rest - piece.astype(F32)
    return out


def one_minus_exp(v):
    series = 1.0 - v * (1.0 / 9.0)
    for k in range(8, 1, -1):
        series = 1.0 - v * (1.0 / k) * series
    return jnp.where(v < 0.5, v * series, 1.0 - jnp.exp(-v))


def decay_terms(lam_ref):
    lam = jnp.concatenate([lam_ref[:, 0, :], lam_ref[:, 1, :]], axis=1)
    parts = pieces(lam, 3)
    first = iota((TOK, TOK), 0)
    second = iota((TOK, TOK), 1)
    upto = (second <= first).astype(F32).astype(BF16)
    same = (second == first).astype(F32).astype(BF16)
    cum_col = sum(nt(upto, p) for p in reversed(parts))
    cum_row = sum(nt(p, upto) for p in reversed(parts))
    lam_col = sum(nt(same, p) for p in reversed(parts))
    square_col = one_minus_exp(-2.0 * lam_col)
    square_row = one_minus_exp(-2.0 * lam)
    return cum_col, cum_row, square_col, square_row


def cum_of(lam_ref):
    lam = jnp.concatenate([lam_ref[:, 0, :], lam_ref[:, 1, :]], axis=1)
    parts = pieces(lam, 3)
    first = iota((TOK, TOK), 0)
    second = iota((TOK, TOK), 1)
    upto = (second <= first).astype(F32).astype(BF16)
    same = (second == first).astype(F32).astype(BF16)
    cum_col = sum(nt(upto, p) for p in reversed(parts))
    lam_col = sum(nt(same, p) for p in reversed(parts))
    return cum_col, lam_col


def spread_heads(values, count):
    spread = (iota((HEADS, WIDTH), 1) // PART == iota((HEADS, WIDTH), 0)).astype(F32).astype(BF16)
    return sum(nn(p, spread) for p in reversed(pieces(values, count)))


def opening_of(cum_col):
    return spread_heads(jnp.exp(cum_col), 2)


def ending_of(cum_col, lam_col):
    last = cum_col[TOK - 1 : TOK, :]
    return spread_heads(jnp.exp(last - cum_col) * jnp.sqrt(one_minus_exp(-2.0 * lam_col)), 2)


def placed(select, offset, slot, copies):
    at = iota((2 * STATE, GROUP * ROWS8), 0)
    col = iota((2 * STATE, GROUP * ROWS8), 1)
    k = col % ROWS8 - slot
    hit = (at == offset + 2 * (col // ROWS8) + k % 2) & (k >= 0) & (k < copies)
    return nn(select, hit.astype(F32).astype(BF16)).astype(BF16)


def placed_rows(select, offset, slot):
    at = iota((GROUP * ROWS8, 2 * STATE), 1)
    row = iota((GROUP * ROWS8, 2 * STATE), 0)
    k = row % ROWS8 - slot
    hit = (at == offset + 2 * (row // ROWS8) + k) & (k >= 0) & (k < 2)
    return nt(hit.astype(F32).astype(BF16), select).astype(BF16)


def spent_rows(cum_col):
    tail = spread_heads(cum_col[TOK - 8 :, :], 3)[7:8, :]
    high = tail.astype(BF16).astype(F32)
    return high, tail - high


def message_part(weighted, select, offset, slot, cum_col):
    state = nn(placed_rows(select, offset, slot), weighted)
    high, low = spent_rows(cum_col)
    row = iota((GROUP * ROWS8, WIDTH), 0) % ROWS8
    return jnp.where(row == slot + 2, high, jnp.where(row == slot + 3, low, state))


def normalized(x, gain):
    factor = lax.rsqrt(jnp.mean(x * x, axis=-1, keepdims=True) + EPSILON)
    return (x * factor * gain).astype(BF16)


def local_scan(values, select, lam_ref, skip_ref, out_ref, backward):
    cum_col, cum_row, square_col, square_row = decay_terms(lam_ref)
    source = select[:, :STATE]
    target = select[:, STATE:]
    if backward:
        affinity = nt(source, target)
        left = (0.5 * jnp.log2(square_col)) - cum_col * LOG2E
        right = cum_row * LOG2E
    else:
        affinity = nt(target, source)
        left = cum_col * LOG2E
        right = (0.5 * jnp.log2(square_row)) - cum_row * LOG2E
    first = iota((128, 128), 0)
    second = iota((128, 128), 1)
    keep = second >= first if backward else second <= first
    for h in range(HEADS):
        span = slice(h * PART, (h + 1) * PART)
        v = values[:, span]
        lo, hi = slice(0, 128), slice(128, 256)
        lc = left[:, h : h + 1]
        rr = right[h : h + 1, :]

        def tile(a, b, masked):
            m = jnp.exp2(lc[a] + rr[:, b]) * affinity[a, b]
            return (jnp.where(keep, m, 0.0) if masked else m).astype(BF16)

        skip = skip_ref[h]
        if backward:
            top = nn(tile(lo, lo, True), v[lo]) + nn(tile(lo, hi, False), v[hi])
            low = nn(tile(hi, hi, True), v[hi])
        else:
            top = nn(tile(lo, lo, True), v[lo])
            low = nn(tile(hi, lo, False), v[lo]) + nn(tile(hi, hi, True), v[hi])
        out_ref[lo, span] = top + skip * v[lo].astype(F32)
        out_ref[hi, span] = low + skip * v[hi].astype(F32)


def start_kernel(
    x_ref, rsel_ref, rlam_ref, gain_ref, win_ref, y_ref, csel_ref, clam_ref, wout_ref,
    value_ref, pulled_ref, message_ref,
):
    value = nn(normalized(x_ref[...].astype(F32), gain_ref[...]), win_ref[...]).astype(BF16)
    value_ref[...] = value
    rcum, rlam = cum_of(rlam_ref)
    weighted = (value.astype(F32) * ending_of(rcum, rlam)).astype(BF16)
    first = message_part(weighted, rsel_ref[...], 0, 0, rcum)
    pulled = nt(y_ref[...], wout_ref[...]).astype(BF16)
    pulled_ref[...] = pulled
    ccum, _ = cum_of(clam_ref)
    weighted = (pulled.astype(F32) * opening_of(ccum)).astype(BF16)
    second = message_part(weighted, csel_ref[...], STATE, 4, ccum)
    row = iota((GROUP * ROWS8, WIDTH), 0) % ROWS8
    message_ref[...] = jnp.where(row < 4, first, second).astype(BF16)


def scan_kernel(value_ref, select_ref, lam_ref, skip_ref, out_ref, *, backward):
    local_scan(value_ref[...], select_ref[...], lam_ref, skip_ref, out_ref, backward)


def inner_kernel(got_ref, before_ref, total_ref):
    row = iota((ROWS8, WIDTH), 0)

    def tile(j):
        return got_ref[j * ROWS8 : (j + 1) * ROWS8, :].astype(F32)

    def spent(t, slot):
        return t[slot + 2 : slot + 3, :] + t[slot + 3 : slot + 4, :]

    gone = jnp.zeros((1, WIDTH), F32)
    state = jnp.zeros((ROWS8, WIDTH), F32)
    for j in range(GROUP):
        t = tile(j)
        before_ref[j * ROWS8 : (j + 1) * ROWS8, :] = jnp.where(row < 2, state, jnp.exp(gone))
        step = spent(t, 0)
        state = jnp.exp(step) * state + t
        gone = gone + step
    forward_state, forward_gone = state, gone
    gone = jnp.zeros((1, WIDTH), F32)
    state = jnp.zeros((ROWS8, WIDTH), F32)
    for j in reversed(range(GROUP)):
        t = tile(j)
        at = slice(j * ROWS8, (j + 1) * ROWS8)
        before_ref[at, :] = jnp.where(
            row < 4, before_ref[at, :], jnp.where(row < 6, state, jnp.exp(gone))
        )
        step = spent(t, 4)
        state = jnp.exp(step) * state + t
        gone = gone + step
    total = jnp.where(row < 2, forward_state, state)
    spent_both = jnp.where(row < 4, forward_gone, gone)
    high = spent_both.astype(BF16).astype(F32)
    total = jnp.where(row % 4 < 2, total, jnp.where(row % 4 == 2, high, spent_both - high))
    total = total.astype(BF16)
    for j in range(GROUP):
        total_ref[j * ROWS8 : (j + 1) * ROWS8, :] = total


def outer_kernel(mine_ref, got_ref, before_ref, out_ref):
    mine = mine_ref[0]
    row = iota((ROWS8, WIDTH), 0)

    def tile(j):
        return got_ref[j * ROWS8 : (j + 1) * ROWS8, :].astype(F32)

    def entering(slot, order, passed):
        state = jnp.zeros((ROWS8, WIDTH), F32)
        for j in order:
            t = tile(j)
            step = t[slot + 2 : slot + 3, :] + t[slot + 3 : slot + 4, :]
            state = jnp.where(passed(j), jnp.exp(step) * state + t, state)
        return state

    first = entering(0, range(GROUP), lambda j: j < mine)
    second = entering(4, reversed(range(GROUP)), lambda j: j > mine)
    both = jnp.where(row < 4, first, second)
    for j in range(GROUP):
        at = slice(j * ROWS8, (j + 1) * ROWS8)
        t = before_ref[at, :]
        through = jnp.where(row < 4, t[2:3, :], t[6:7, :])
        full = through * both + t
        high = full.astype(BF16).astype(F32)
        low = pltpu.roll(full - high, 2, 0)
        out_ref[at, :] = jnp.where(row % 4 < 2, high, low).astype(BF16)


def row_target(token, half):
    column = token % 128
    return (column // 2) * 8 + half * 4 + (column % 2) * 2 + token // 128


def column_target(token, half):
    row = token % 128
    return (row // 2) * 8 + half * 4 + (token // 128) * 2 + row % 2


def to_message(tokens, target):
    at = iota((2 * TOK, TOK), 0)
    token = iota((1, TOK), 1)
    out = None
    for half in (0, 1):
        hot = (at == target(token, half)).astype(F32).astype(BF16)
        part = nn(hot, tokens[:, half * HALF : (half + 1) * HALF])
        out = part if out is None else out + part
    return out.astype(BF16)


def from_message(message, target):
    at = iota((2 * TOK, TOK), 0)
    token = iota((1, TOK), 1)
    out = []
    for half in (0, 1):
        hot = (at == target(token, half)).astype(F32).astype(BF16)
        out.append(
            lax.dot_general(hot, message, (((0,), (0,)), ((), ())), preferred_element_type=F32)
        )
    return jnp.concatenate(out, axis=1)


def row_finish_kernel(x_ref, sel_ref, lam_ref, local_ref, got_ref, wout_ref, message_ref):
    cum, _ = cum_of(lam_ref)
    carried = nn(placed(sel_ref[...], STATE, 0, 4), got_ref[...]) * opening_of(cum)
    scanned = (local_ref[...] + carried).astype(BF16)
    mixed = (x_ref[...].astype(F32) + nn(scanned, wout_ref[...])).astype(BF16)
    message_ref[...] = to_message(mixed, row_target)


def col_returned_kernel(sel_ref, lam_ref, local_ref, got_ref, win_ref, gain_ref, out_ref):
    cum, lam = cum_of(lam_ref)
    carried = nn(placed(sel_ref[...], 0, 4, 4), got_ref[...]) * ending_of(cum, lam)
    scanned = (local_ref[...] + carried).astype(BF16)
    out_ref[...] = gain_ref[...] * nt(scanned, win_ref[...])


def input_gradient(x, y, scaled):
    factor = lax.rsqrt(jnp.mean(x * x, axis=-1, keepdims=True) + EPSILON)
    inner = jnp.mean(scaled * x, axis=-1, keepdims=True)
    return (y + factor * scaled - x * (factor * factor * factor) * inner).astype(BF16)


def col_grad_kernel(got_ref, y_ref, scaled_ref, x_ref, message_ref):
    x = from_message(got_ref[...], column_target)
    x_ref[...] = x.astype(BF16)
    grad = input_gradient(x, y_ref[...].astype(F32), scaled_ref[...])
    message_ref[...] = to_message(grad, column_target)


def col_value_kernel(x_ref, sel_ref, lam_ref, gain_ref, win_ref, value_ref, part_ref):
    value = nn(normalized(x_ref[...].astype(F32), gain_ref[...]), win_ref[...]).astype(BF16)
    value_ref[...] = value
    cum, lam = cum_of(lam_ref)
    weighted = (value.astype(F32) * ending_of(cum, lam)).astype(BF16)
    part_ref[...] = message_part(weighted, sel_ref[...], 0, 0, cum).astype(BF16)


def row_pull_kernel(
    got_ref, sel_ref, lam_ref, wout_ref, part_ref, y_ref, pulled_ref, message_ref
):
    y = from_message(got_ref[...], row_target).astype(BF16)
    y_ref[...] = y
    pulled = nt(y, wout_ref[...]).astype(BF16)
    pulled_ref[...] = pulled
    cum, _ = cum_of(lam_ref)
    weighted = (pulled.astype(F32) * opening_of(cum)).astype(BF16)
    second = message_part(weighted, sel_ref[...], STATE, 4, cum)
    row = iota((GROUP * ROWS8, WIDTH), 0) % ROWS8
    message_ref[...] = jnp.where(row < 4, part_ref[...].astype(F32), second).astype(BF16)


def end_kernel(
    got_ref, cx_ref, csel_ref, clam_ref, clocal_ref, cwout_ref,
    x_ref, y_ref, rsel_ref, rlam_ref, rlocal_ref, rwin_ref, gain_ref,
    mixed_ref, grad_ref,
):
    got = got_ref[...]
    cum, _ = cum_of(clam_ref)
    carried = nn(placed(csel_ref[...], STATE, 0, 4), got) * opening_of(cum)
    scanned = (clocal_ref[...] + carried).astype(BF16)
    mixed_ref[...] = (cx_ref[...].astype(F32) + nn(scanned, cwout_ref[...])).astype(BF16)
    cum, lam = cum_of(rlam_ref)
    carried = nn(placed(rsel_ref[...], 0, 4, 4), got) * ending_of(cum, lam)
    scanned = (rlocal_ref[...] + carried).astype(BF16)
    scaled = gain_ref[...] * nt(scanned, rwin_ref[...])
    grad_ref[...] = input_gradient(x_ref[...].astype(F32), y_ref[...].astype(F32), scaled)


VM = pl.BlockSpec(memory_space=pltpu.VMEM)
SM = pl.BlockSpec(memory_space=pltpu.SMEM)


def call(kernel, name, outs, args, scalars=(), flops=4e8):
    return pl.pallas_call(
        kernel,
        name=name,
        out_shape=[jax.ShapeDtypeStruct(s, d) for s, d in outs],
        in_specs=[SM if i in scalars else VM for i in range(len(args))],
        out_specs=[VM] * len(outs),
        cost_estimate=pl.CostEstimate(flops=int(flops), bytes_accessed=1 << 20, transcendentals=0),
    )(*args)


TOKS = (TOK, WIDTH)
MSG = (GROUP * ROWS8, WIDTH)
BIG = (2 * TOK, HALF)


def swapped(array, axes):
    count = 1
    for axis in axes:
        count *= lax.axis_size(axis)
    split = array.reshape(count, array.shape[0] // count, array.shape[1])
    return lax.all_to_all(split, axes, split_axis=0, concat_axis=0, tiled=True).reshape(array.shape)


def carry(message, mine):
    got = swapped(message, INNER)
    before, total = call(inner_kernel, "inner", [(MSG, F32), (MSG, BF16)], [got], flops=1e6)
    groups = swapped(total, OUTER)
    (down,) = call(outer_kernel, "outer", [(MSG, BF16)], [mine, groups, before], (0,), flops=1e6)
    return swapped(down, INNER)


def local(value, select, lam, skip, backward, name):
    (out,) = call(
        partial(scan_kernel, backward=backward), name, [(TOKS, F32)],
        [value, select, lam, skip], (3,), flops=2e9,
    )
    return out


def body(
    tokens, row_select, row_decay, row_gain, row_skip, row_in, row_out,
    col_select, col_decay, col_gain, col_skip, col_in, col_out, cotangent,
):
    mine = (lax.axis_index("frame") * lax.axis_size("seq_0") + lax.axis_index("seq_0")).reshape(1)
    x = tokens.reshape(TOKS)
    y = cotangent.reshape(TOKS)
    rsel = row_select.reshape(TOK, 2 * STATE)
    csel = col_select.reshape(TOK, 2 * STATE)
    rlam = row_decay.reshape(HEADS, 2, 128)
    clam = col_decay.reshape(HEADS, 2, 128)
    rgain = row_gain.reshape(1, WIDTH)
    cgain = col_gain.reshape(1, WIDTH)

    rvalue, cpulled, message = call(
        start_kernel, "start", [(TOKS, BF16), (TOKS, BF16), (MSG, BF16)],
        [x, rsel, rlam, rgain, row_in, y, csel, clam, col_out],
    )
    rlocal = local(rvalue, rsel, rlam, row_skip, False, "row_scan")
    clocal = local(cpulled, csel, clam, col_skip, True, "col_scan_back")
    got = carry(message, mine)
    (sending,) = call(
        row_finish_kernel, "row_finish", [(BIG, BF16)], [x, rsel, rlam, rlocal, got, row_out]
    )
    (scaled,) = call(
        col_returned_kernel, "col_returned", [(TOKS, F32)],
        [csel, clam, clocal, got, col_in, cgain],
    )
    arrived = swapped(sending, SEQ)
    cx, returning = call(
        col_grad_kernel, "col_grad", [(TOKS, BF16), (BIG, BF16)], [arrived, y, scaled]
    )
    landed = swapped(returning, SEQ)
    cvalue, part = call(
        col_value_kernel, "col_value", [(TOKS, BF16), (MSG, BF16)], [cx, csel, clam, cgain, col_in]
    )
    clocal2 = local(cvalue, csel, clam, col_skip, False, "col_scan")
    ry, rpulled, message = call(
        row_pull_kernel, "row_pull", [(TOKS, BF16), (TOKS, BF16), (MSG, BF16)],
        [landed, rsel, rlam, row_out, part],
    )
    rlocal2 = local(rpulled, rsel, rlam, row_skip, True, "row_scan_back")
    got = carry(message, mine)
    mixed, grad = call(
        end_kernel, "end", [(TOKS, BF16), (TOKS, BF16)],
        [got, cx, csel, clam, clocal2, col_out, x, ry, rsel, rlam, rlocal2, row_in, rgain],
    )
    return mixed.reshape(cotangent.shape), grad.reshape(tokens.shape)


def solution(mesh):
    torus = Mesh(
        mesh.devices.reshape(4, 8, 2, mesh.shape["frame"]), ("seq_0", "seq_1", "seq_2", "frame")
    )
    tall = P("frame", SEQ, None, None)
    flat = P("frame", None, SEQ, None)
    in_specs = (tall, tall, flat, P(), P(), P(), P(), tall, flat, P(), P(), P(), P(), tall)
    return jax.shard_map(
        body, mesh=torus, in_specs=in_specs, out_specs=(tall, tall), check_vma=False
    )
```

time: 568 us -> 151 us (0.27)
  the two profiles are of different devices: /device:TPU:8 before, /device:TPU:1 now
where the time goes in v1:
time: 151 us; the launch traced here: 150 us
  blocking collectives  44.3 us (29%)
  Pallas kernels  42.7 us (28%)
  waiting for transfers between devices  31.1 us (21%)
  starting transfers between devices  26 us (17%)
  local copies, waits for them, and re-layouts  5.61 us (4%)
    all_to_all x3, blocking collectives, swapped(): lax.all_to_all(split, axes, split_axis=0, concat_axis=0, tiled=True)  44.3 us
    pallas_call x15, Pallas kernels, call(): pl.pallas_call(kernel, name=name, out_shape=[jax.ShapeDtypeStruct(s, d) f...  42.7 us
    all_to_all x5, waiting for transfers between devices, swapped(): lax.all_to_all(split, axes, split_axis=0, concat_axis=0, tiled=True)  31.1 us
    all_to_all x5, starting transfers between devices, swapped(): lax.all_to_all(split, axes, split_axis=0, concat_axis=0, tiled=True)  26 us
    unnamed x14, local copies, waits for them, and re-layouts  5.61 us
  transfers between devices with their start and end apart: 5, of which 5 were waited for; matrix products, arithmetic and copies ran while one was open for 0% of the time, Pallas kernels for 12%

profile of v1, /device:TPU:1, one launch (start us, length us, event | category | flops | bytes accessed | tf_op | source)
XLA Modules:
  0.0 150.4 jit_solution(3389684672507830831)
XLA Ops:
  0.6 0.0 copy-start.5
  0.6 1.5 copy.16
  2.1 0.0 copy-done.5
  2.1 0.7 copy.17
  2.9 4.1 %start.1 = (bf16[256,512]{1,0:T(8,128)(2,1)}, bf16[256,512]{1,0:T(8,128)(2,1)}, bf16[128,512]{1,0:T(8,128)(2,1)}) custom-call(bf16[256,512]{1,0:T(8,128)(2,1)} %bitcast.27, bf16[256,64]{1,0:T(8,128)(2,1)} %bitcast.32, f32[8,2,128]{2,1,0:T(2,128)} %bitcast.61, f32[1,512]{1,0:T(1,128)} %bitcast.73, bf16[512,512]{1,0:T(8,128)(2,1)} %rwin_ref.1, ...), custom_call_target="tpu_custom_call" | custom-call | flops 400000000 | bytes 1048576 | tf_op jit(solution)/shard_map/start/pallas_call | solution.py:365
  7.0 19.0 %all_to_all.40 = bf16[16,8,512]{2,1,0:T(8,128)(2,1)} all-to-all(bf16[16,8,512]{2,1,0:T(8,128)(2,1)} %bitcast.59), channel_id=1, replica_groups=mesh['seq_0'=4,'seq_1'=8,'seq_2'=2,'frame'=4] {'seq_1','seq_2'}, dimensions={0} | all-to-all | bytes 262144 | tf_op jit(solution)/shard_map/all_to_all | solution.py:385
  25.9 1.9 %inner.2 = (f32[128,512]{1,0:T(8,128)}, bf16[128,512]{1,0:T(8,128)(2,1)}) custom-call(bf16[128,512]{1,0:T(8,128)(2,1)} %bitcast.50), custom_call_target="tpu_custom_call" | custom-call | flops 1000000 | bytes 1048576 | tf_op jit(solution)/shard_map/inner/pallas_call | solution.py:365
  27.8 6.8 %all-to-all-start.1 = ((bf16[16,8,512]{2,1,0:T(8,128)(2,1)}), bf16[16,8,512]{2,1,0:T(8,128)(2,1)S(1)}, u32[]{:S(2)}, u32[]{:S(2)}) async-start(bf16[16,8,512]{2,1,0:T(8,128)(2,1)} %bitcast.57), calls=%async_computation.1 | async-start | bytes 262144 | tf_op jit(solution)/shard_map/all_to_all | solution.py:385
  34.6 6.8 %all-to-all-done.1 = bf16[16,8,512]{2,1,0:T(8,128)(2,1)S(1)} async-done(((bf16[16,8,512]{2,1,0:T(8,128)(2,1)}), bf16[16,8,512]{2,1,0:T(8,128)(2,1)S(1)}, u32[]{:S(2)}, u32[]{:S(2)}) %all-to-all-start.1) | async-done | bytes 131104 | tf_op jit(solution)/shard_map/all_to_all | solution.py:385
  41.3 0.0 copy-start.1
  41.3 0.6 copy-done.1
  42.0 1.9 %outer.2 = bf16[128,512]{1,0:T(8,128)(2,1)} custom-call(s32[1]{0:T(128)} %bitcast.mine_ref, bf16[128,512]{1,0:T(8,128)(2,1)} %bitcast.45, f32[128,512]{1,0:T(8,128)} %get-tuple-element.21.before_ref), custom_call_target="tpu_custom_call" | custom-call | flops 1000000 | bytes 1048576 | tf_op jit(solution)/shard_map/outer/pallas_call | solution.py:365
  43.9 4.6 %all-to-all-start.2 = ((bf16[16,8,512]{2,1,0:T(8,128)(2,1)}), bf16[16,8,512]{2,1,0:T(8,128)(2,1)S(1)}, u32[]{:S(2)}, u32[]{:S(2)}) async-start(bf16[16,8,512]{2,1,0:T(8,128)(2,1)} %bitcast.48), calls=%async_computation.2 | async-start | bytes 262144 | tf_op jit(solution)/shard_map/all_to_all | solution.py:385
  48.5 2.8 %row_scan.1.local_ref = f32[256,512]{1,0:T(8,128)} custom-call(bf16[256,512]{1,0:T(8,128)(2,1)} %get-tuple-element.18.value_ref, bf16[256,64]{1,0:T(8,128)(2,1)} %bitcast.33, f32[8,2,128]{2,1,0:T(2,128)} %bitcast.62, f32[8]{0:T(128)} %skip_ref.7), custom_call_target="tpu_custom_call" | custom-call | flops 2000000000 | bytes 1048576 | tf_op jit(solution)/shard_map/row_scan/pallas_call | solution.py:365
  51.3 6.4 %all-to-all-done.2 = bf16[16,8,512]{2,1,0:T(8,128)(2,1)S(1)} async-done(((bf16[16,8,512]{2,1,0:T(8,128)(2,1)}), bf16[16,8,512]{2,1,0:T(8,128)(2,1)S(1)}, u32[]{:S(2)}, u32[]{:S(2)}) %all-to-all-start.2) | async-done | bytes 131104 | tf_op jit(solution)/shard_map/all_to_all | solution.py:385
  57.7 0.0 copy-start
  57.7 0.7 copy-done
  58.4 3.1 %row_finish.1 = bf16[512,256]{1,0:T(8,128)(2,1)} custom-call(bf16[256,512]{1,0:T(8,128)(2,1)} %bitcast.28, bf16[256,64]{1,0:T(8,128)(2,1)} %bitcast.34, f32[8,2,128]{2,1,0:T(2,128)} %bitcast.63, f32[256,512]{1,0:T(8,128)} %row_scan.1.local_ref, bf16[128,512]{1,0:T(8,128)(2,1)} %bitcast.30, bf16[512,512]{1,0:T(8,128)(2,1)} %wout_ref.5), custom_call_target="tpu_custom_call" | custom-call | flops 400000000 | bytes 1048576 | tf_op jit(solution)/shard_map/row_finish/pallas_call | solution.py:365
  61.5 4.2 %all-to-all-start.3 = ((bf16[64,8,256]{2,1,0:T(8,128)(2,1)}), bf16[64,8,256]{2,1,0:T(8,128)(2,1)S(1)}, u32[]{:S(2)}, u32[]{:S(2)}) async-start(bf16[64,8,256]{2,1,0:T(8,128)(2,1)} %bitcast.38), calls=%async_computation.3 | async-start | bytes 524288 | tf_op jit(solution)/shard_map/all_to_all | solution.py:385
  65.7 3.1 %col_scan_back.1.local_ref = f32[256,512]{1,0:T(8,128)} custom-call(bf16[256,512]{1,0:T(8,128)(2,1)} %get-tuple-element.22.value_ref, bf16[256,64]{1,0:T(8,128)(2,1)} %bitcast.40, f32[8,2,128]{2,1,0:T(2,128)} %bitcast.68, f32[8]{0:T(128)} %skip_ref.6), custom_call_target="tpu_custom_call" | custom-call | flops 2000000000 | bytes 1048576 | tf_op jit(solution)/shard_map/col_scan_back/pallas_call | solution.py:365
  68.8 3.1 %col_returned.1.scaled_ref = f32[256,512]{1,0:T(8,128)} custom-call(bf16[256,64]{1,0:T(8,128)(2,1)} %bitcast.41, f32[8,2,128]{2,1,0:T(2,128)} %bitcast.69, f32[256,512]{1,0:T(8,128)} %col_scan_back.1.local_ref, bf16[128,512]{1,0:T(8,128)(2,1)} %bitcast.31, bf16[512,512]{1,0:T(8,128)(2,1)} %win_ref.5, f32[1,512]{1,0:T(1,128)} %bitcast.75), custom_call_target="tpu_custom_call" | custom-call | flops 400000000 | bytes 1048576 | tf_op jit(solution)/shard_map/col_returned/pallas_call | solution.py:365
  71.9 5.7 %all-to-all-done.3 = bf16[64,8,256]{2,1,0:T(8,128)(2,1)S(1)} async-done(((bf16[64,8,256]{2,1,0:T(8,128)(2,1)}), bf16[64,8,256]{2,1,0:T(8,128)(2,1)S(1)}, u32[]{:S(2)}, u32[]{:S(2)}) %all-to-all-start.3) | async-done | bytes 262176 | tf_op jit(solution)/shard_map/all_to_all | solution.py:385
  77.6 0.0 copy-start.3
  77.6 0.7 copy-done.3
  78.3 2.7 %col_grad.1 = (bf16[256,512]{1,0:T(8,128)(2,1)}, bf16[512,256]{1,0:T(8,128)(2,1)}) custom-call(bf16[512,256]{1,0:T(8,128)(2,1)} %bitcast.52, bf16[256,512]{1,0:T(8,128)(2,1)} %bitcast.56, f32[256,512]{1,0:T(8,128)} %col_returned.1.scaled_ref), custom_call_target="tpu_custom_call" | custom-call | flops 400000000 | bytes 1048576 | tf_op jit(solution)/shard_map/col_grad/pallas_call | solution.py:365
  81.0 6.0 %all-to-all-start.4 = ((bf16[64,8,256]{2,1,0:T(8,128)(2,1)}), bf16[64,8,256]{2,1,0:T(8,128)(2,1)S(1)}, u32[]{:S(2)}, u32[]{:S(2)}) async-start(bf16[64,8,256]{2,1,0:T(8,128)(2,1)} %bitcast.54), calls=%async_computation.4 | async-start | bytes 524288 | tf_op jit(solution)/shard_map/all_to_all | solution.py:385
  87.0 3.0 %col_value.1 = (bf16[256,512]{1,0:T(8,128)(2,1)}, bf16[128,512]{1,0:T(8,128)(2,1)}) custom-call(bf16[256,512]{1,0:T(8,128)(2,1)} %get-tuple-element.24.x_ref.cx_ref, bf16[256,64]{1,0:T(8,128)(2,1)} %bitcast.42, f32[8,2,128]{2,1,0:T(2,128)} %bitcast.70, f32[1,512]{1,0:T(1,128)} %bitcast.76, bf16[512,512]{1,0:T(8,128)(2,1)} %win_ref.5), custom_call_target="tpu_custom_call" | custom-call | flops 400000000 | bytes 1048576 | tf_op jit(solution)/shard_map/col_value/pallas_call | solution.py:365
  90.0 8.9 %all-to-all-done.4 = bf16[64,8,256]{2,1,0:T(8,128)(2,1)S(1)} async-done(((bf16[64,8,256]{2,1,0:T(8,128)(2,1)}), bf16[64,8,256]{2,1,0:T(8,128)(2,1)S(1)}, u32[]{:S(2)}, u32[]{:S(2)}) %all-to-all-start.4) | async-done | bytes 262176 | tf_op jit(solution)/shard_map/all_to_all | solution.py:385
  99.0 0.0 copy-start.4
  99.0 0.7 copy-done.4
  99.7 3.0 %row_pull.1 = (bf16[256,512]{1,0:T(8,128)(2,1)}, bf16[256,512]{1,0:T(8,128)(2,1)}, bf16[128,512]{1,0:T(8,128)(2,1)}) custom-call(bf16[512,256]{1,0:T(8,128)(2,1)} %bitcast.53, bf16[256,64]{1,0:T(8,128)(2,1)} %bitcast.35, f32[8,2,128]{2,1,0:T(2,128)} %bitcast.64, bf16[512,512]{1,0:T(8,128)(2,1)} %wout_ref.5, bf16[128,512]{1,0:T(8,128)(2,1)} %get-tuple-element.25.part_ref), custom_call_target="tpu_custom_call" | custom-call | flops 400000000 | bytes 1048576 | tf_op jit(solution)/shard_map/row_pull/pallas_call | solution.py:365
  102.7 13.5 %all_to_all.41 = bf16[16,8,512]{2,1,0:T(8,128)(2,1)} all-to-all(bf16[16,8,512]{2,1,0:T(8,128)(2,1)} %bitcast.58), channel_id=1, replica_groups=mesh['seq_0'=4,'seq_1'=8,'seq_2'=2,'frame'=4] {'seq_1','seq_2'}, dimensions={0} | all-to-all | bytes 262144 | tf_op jit(solution)/shard_map/all_to_all | solution.py:385
  116.3 1.9 %inner.3 = (f32[128,512]{1,0:T(8,128)}, bf16[128,512]{1,0:T(8,128)(2,1)}) custom-call(bf16[128,512]{1,0:T(8,128)(2,1)} %bitcast.51), custom_call_target="tpu_custom_call" | custom-call | flops 1000000 | bytes 1048576 | tf_op jit(solution)/shard_map/inner/pallas_call | solution.py:365
  118.1 11.8 %all_to_all.42 = bf16[16,8,512]{2,1,0:T(8,128)(2,1)} all-to-all(bf16[16,8,512]{2,1,0:T(8,128)(2,1)} %bitcast.60), channel_id=1, replica_groups=mesh['seq_0'=4,'seq_1'=8,'seq_2'=2,'frame'=4] {'frame','seq_0'}, dimensions={0} | all-to-all | bytes 262144 | tf_op jit(solution)/shard_map/all_to_all | solution.py:385
  129.9 1.9 %outer.3 = bf16[128,512]{1,0:T(8,128)(2,1)} custom-call(s32[1]{0:T(128)} %bitcast.mine_ref, bf16[128,512]{1,0:T(8,128)(2,1)} %bitcast.49, f32[128,512]{1,0:T(8,128)} %get-tuple-element.28.before_ref), custom_call_target="tpu_custom_call" | custom-call | flops 1000000 | bytes 1048576 | tf_op jit(solution)/shard_map/outer/pallas_call | solution.py:365
  131.8 4.3 %all-to-all-start.7 = ((bf16[16,8,512]{2,1,0:T(8,128)(2,1)}), bf16[16,8,512]{2,1,0:T(8,128)(2,1)S(1)}, u32[]{:S(2)}, u32[]{:S(2)}) async-start(bf16[16,8,512]{2,1,0:T(8,128)(2,1)} %bitcast.47), calls=%async_computation.7 | async-start | bytes 262144 | tf_op jit(solution)/shard_map/all_to_all | solution.py:385
  136.2 2.8 %col_scan.1.clocal_ref = f32[256,512]{1,0:T(8,128)} custom-call(bf16[256,512]{1,0:T(8,128)(2,1)} %get-tuple-element.29.value_ref, bf16[256,64]{1,0:T(8,128)(2,1)} %bitcast.43, f32[8,2,128]{2,1,0:T(2,128)} %bitcast.71, f32[8]{0:T(128)} %skip_ref.6), custom_call_target="tpu_custom_call" | custom-call | flops 2000000000 | bytes 1048576 | tf_op jit(solution)/shard_map/col_scan/pallas_call | solution.py:365
  139.0 3.1 %row_scan_back.1.rlocal_ref = f32[256,512]{1,0:T(8,128)} custom-call(bf16[256,512]{1,0:T(8,128)(2,1)} %get-tuple-element.31.value_ref, bf16[256,64]{1,0:T(8,128)(2,1)} %bitcast.36, f32[8,2,128]{2,1,0:T(2,128)} %bitcast.65, f32[8]{0:T(128)} %skip_ref.7), custom_call_target="tpu_custom_call" | custom-call | flops 2000000000 | bytes 1048576 | tf_op jit(solution)/shard_map/row_scan_back/pallas_call | solution.py:365
  142.1 3.3 %all-to-all-done.7 = bf16[16,8,512]{2,1,0:T(8,128)(2,1)S(1)} async-done(((bf16[16,8,512]{2,1,0:T(8,128)(2,1)}), bf16[16,8,512]{2,1,0:T(8,128)(2,1)S(1)}, u32[]{:S(2)}, u32[]{:S(2)}) %all-to-all-start.7) | async-done | bytes 131104 | tf_op jit(solution)/shard_map/all_to_all | solution.py:385
  145.4 0.0 copy-start.2
  145.4 0.7 copy-done.2
  146.0 4.3 %end.1 = (bf16[256,512]{1,0:T(8,128)(2,1)}, bf16[256,512]{1,0:T(8,128)(2,1)}) custom-call(bf16[128,512]{1,0:T(8,128)(2,1)} %bitcast.46, bf16[256,512]{1,0:T(8,128)(2,1)} %get-tuple-element.24.x_ref.cx_ref, bf16[256,64]{1,0:T(8,128)(2,1)} %bitcast.44, f32[8,2,128]{2,1,0:T(2,128)} %bitcast.72, f32[256,512]{1,0:T(8,128)} %col_scan.1.clocal_ref, ...), custom_call_target="tpu_custom_call" | custom-call | flops 400000000 | bytes 1048576 | tf_op jit(solution)/shard_map/end/pallas_call | solution.py:365
Async XLA Ops:
  0.6 1.5 %copy-start.5 = (bf16[1,2,128,64]{2,3,1,0:T(8,128)(2,1)S(1)}, bf16[1,2,128,64]{2,3,1,0:T(8,128)(2,1)}, u32[]{:S(2)}) copy-start(bf16[1,2,128,64]{2,3,1,0:T(8,128)(2,1)} %param.21) | copy-start | bytes 98308
  27.8 13.5 %all-to-all-start.1 = ((bf16[16,8,512]{2,1,0:T(8,128)(2,1)}), bf16[16,8,512]{2,1,0:T(8,128)(2,1)S(1)}, u32[]{:S(2)}, u32[]{:S(2)}) async-start(bf16[16,8,512]{2,1,0:T(8,128)(2,1)} %bitcast.57), calls=%async_computation.1 | async-start | bytes 262144 | tf_op jit(solution)/shard_map/all_to_all | solution.py:385
  41.3 0.6 copy-start.1
  43.9 13.8 %all-to-all-start.2 = ((bf16[16,8,512]{2,1,0:T(8,128)(2,1)}), bf16[16,8,512]{2,1,0:T(8,128)(2,1)S(1)}, u32[]{:S(2)}, u32[]{:S(2)}) async-start(bf16[16,8,512]{2,1,0:T(8,128)(2,1)} %bitcast.48), calls=%async_computation.2 | async-start | bytes 262144 | tf_op jit(solution)/shard_map/all_to_all | solution.py:385
  57.7 0.7 copy-start
  61.5 16.1 %all-to-all-start.3 = ((bf16[64,8,256]{2,1,0:T(8,128)(2,1)}), bf16[64,8,256]{2,1,0:T(8,128)(2,1)S(1)}, u32[]{:S(2)}, u32[]{:S(2)}) async-start(bf16[64,8,256]{2,1,0:T(8,128)(2,1)} %bitcast.38), calls=%async_computation.3 | async-start | bytes 524288 | tf_op jit(solution)/shard_map/all_to_all | solution.py:385
  77.6 0.7 copy-start.3
  81.0 18.0 %all-to-all-start.4 = ((bf16[64,8,256]{2,1,0:T(8,128)(2,1)}), bf16[64,8,256]{2,1,0:T(8,128)(2,1)S(1)}, u32[]{:S(2)}, u32[]{:S(2)}) async-start(bf16[64,8,256]{2,1,0:T(8,128)(2,1)} %bitcast.54), calls=%async_computation.4 | async-start | bytes 524288 | tf_op jit(solution)/shard_map/all_to_all | solution.py:385
  99.0 0.7 copy-start.4
  131.8 13.5 %all-to-all-start.7 = ((bf16[16,8,512]{2,1,0:T(8,128)(2,1)}), bf16[16,8,512]{2,1,0:T(8,128)(2,1)S(1)}, u32[]{:S(2)}, u32[]{:S(2)}) async-start(bf16[16,8,512]{2,1,0:T(8,128)(2,1)} %bitcast.47), calls=%async_computation.7 | async-start | bytes 262144 | tf_op jit(solution)/shard_map/all_to_all | solution.py:385
  145.4 0.7 copy-start.2

commit v2 on v1

v2 whole, which is shorter than its diff:
```python
from functools import partial

import jax
import jax.numpy as jnp
from jax import lax
from jax.experimental import pallas as pl
from jax.experimental.pallas import tpu as pltpu
from jax.sharding import Mesh
from jax.sharding import PartitionSpec as P

SEQ = ("seq_0", "seq_1", "seq_2")
INNER = ("seq_2", "seq_1")
OUTER = ("seq_0", "frame")

EPSILON = 1e-05
LOG2E = 1.4426950408889634

TOK = 256
WIDTH = 512
HEADS = 8
PART = 64
STATE = 32
GROUP = 16
HALF = 256
LINES = GROUP * 8
LOGS = 128

F32 = jnp.float32
BF16 = jnp.bfloat16


def iota(shape, axis):
    return lax.broadcasted_iota(jnp.int32, shape, axis)


def onehot(mask):
    return mask.astype(F32).astype(BF16)


def dot(left, right, left_axis, right_axis):
    return lax.dot_general(
        left, right, (((left_axis,), (right_axis,)), ((), ())), preferred_element_type=F32
    )


def nn(left, right):
    return dot(left, right, 1, 0)


def nt(left, right):
    return dot(left, right, 1, 1)


def tn(left, right):
    return dot(left, right, 0, 0)


def parts_of(values, count):
    out = []
    rest = values
    for _ in range(count):
        piece = rest.astype(BF16)
        out.append(piece)
        rest = rest - piece.astype(F32)
    return out


def one_minus_exp(v):
    series = 1.0 - v * (1.0 / 9.0)
    for k in range(8, 1, -1):
        series = 1.0 - v * (1.0 / k) * series
    return jnp.where(v < 0.5, v * series, 1.0 - jnp.exp(-v))


def lam_of(lam_ref):
    return jnp.concatenate([lam_ref[:, 0, :], lam_ref[:, 1, :]], axis=1)


def turned_select(select_ref):
    return jnp.concatenate([select_ref[0], select_ref[1]], axis=1)


def triangle():
    return onehot(iota((TOK, TOK), 1) <= iota((TOK, TOK), 0))


def cum_columns(lam):
    upto = triangle()
    return sum(nt(upto, p) for p in reversed(parts_of(lam, 3)))


def cum_rows(lam):
    upto = triangle()
    return sum(nt(p, upto) for p in reversed(parts_of(lam, 3)))


def columns(lam):
    same = onehot(iota((TOK, TOK), 1) == iota((TOK, TOK), 0))
    return sum(nt(same, p) for p in reversed(parts_of(lam, 3)))


def spread_heads(values):
    spread = onehot(iota((HEADS, WIDTH), 1) // PART == iota((HEADS, WIDTH), 0))
    return sum(nn(p, spread) for p in reversed(parts_of(values, 2)))


def opening_of(cum_col):
    return jnp.exp(cum_col)


def ending_of(cum_col, lam_col):
    last = cum_col[TOK - 1 : TOK, :]
    return jnp.exp(last - cum_col) * jnp.sqrt(one_minus_exp(-2.0 * lam_col))


def placed(select, offset, stream):
    at = iota((2 * STATE, 2 * LINES), 0)
    col = iota((2 * STATE, 2 * LINES), 1)
    row = col % LINES
    hit = (at == offset + 2 * (row // 8) + row % 2) & (row % 8 // 2 == col // LINES * 2 + stream)
    return tn(select, onehot(hit)).astype(BF16)


def carried_of(placed_pair, got):
    return jnp.concatenate(
        [nn(placed_pair[:, half * LINES : (half + 1) * LINES], got) for half in (0, 1)], axis=1
    )


def state_rows(weighted, select, offset, stream):
    at = iota((LINES, 2 * STATE), 1)
    row = iota((LINES, 2 * STATE), 0)
    out = None
    for half in (0, 1):
        hit = (at == offset + 2 * (row // 8) + row % 2) & (row % 8 // 2 == half * 2 + stream)
        rows = nn(onehot(hit), select).astype(BF16)
        part = nn(rows, weighted[:, half * HALF : (half + 1) * HALF])
        out = part if out is None else out + part
    return out


def normalized(x, gain):
    factor = lax.rsqrt(jnp.mean(x * x, axis=-1, keepdims=True) + EPSILON)
    return (x * factor * gain).astype(BF16)


def input_gradient(x, y, scaled):
    factor = lax.rsqrt(jnp.mean(x * x, axis=-1, keepdims=True) + EPSILON)
    inner = jnp.mean(scaled * x, axis=-1, keepdims=True)
    return (y + factor * scaled - x * (factor * factor * factor) * inner).astype(BF16)


def local_scan(values_ref, select, lam, cum_col, lam_col, skip_ref, out_ref, backward):
    cum_row = cum_rows(lam)
    source = select[:STATE]
    target = select[STATE:]
    if backward:
        affinity = tn(source, target)
        left = 0.5 * jnp.log2(one_minus_exp(-2.0 * lam_col)) - cum_col * LOG2E
        right = cum_row * LOG2E
    else:
        affinity = tn(target, source)
        left = cum_col * LOG2E
        right = 0.5 * jnp.log2(one_minus_exp(-2.0 * lam)) - cum_row * LOG2E
    first = iota((128, 128), 0)
    second = iota((128, 128), 1)
    keep = second >= first if backward else second <= first
    lo, hi = slice(0, 128), slice(128, 256)
    for h in range(HEADS):
        span = slice(h * PART, (h + 1) * PART)
        lc = left[:, h : h + 1]
        rr = right[h : h + 1, :]

        def tile(a, b, masked):
            m = jnp.exp2(lc[a] + rr[:, b]) * affinity[a, b]
            return (jnp.where(keep, m, 0.0) if masked else m).astype(BF16)

        v_lo = values_ref[lo, span]
        v_hi = values_ref[hi, span]
        skip = skip_ref[0:1, h : h + 1]
        if backward:
            top = nn(tile(lo, lo, True), v_lo) + nn(tile(lo, hi, False), v_hi)
            low = nn(tile(hi, hi, True), v_hi)
        else:
            top = nn(tile(lo, lo, True), v_lo)
            low = nn(tile(hi, lo, False), v_lo) + nn(tile(hi, hi, True), v_hi)
        out_ref[lo, span] = top + skip * v_lo.astype(F32)
        out_ref[hi, span] = low + skip * v_hi.astype(F32)


def row_target(token):
    column = token % 128
    return column // 2 * 8 + column % 2 * 2 + token // 128


def column_target(token):
    row = token % 128
    return row // 2 * 8 + token // 128 * 2 + row % 2


def to_message(tokens, target):
    off = iota((2 * TOK, TOK), 0) - target(iota((1, TOK), 1))
    left = nn(onehot(off == 0), tokens[:, :HALF])
    return (left + nn(onehot(off == 4), tokens[:, HALF:])).astype(BF16)


def from_message(message, target):
    off = iota((TOK, 2 * TOK), 1) - target(iota((TOK, 1), 0))
    return jnp.concatenate([nn(onehot(off == 0), message), nn(onehot(off == 4), message)], axis=1)


def start_kernel(
    x_hbm, rsel_hbm, rlam_hbm, gain_hbm, win_hbm, y_hbm, csel_hbm, clam_hbm, wout_hbm,
    value_hbm, pulled_hbm, message_ref,
    x_ref, rsel_ref, rlam_ref, gain_ref, win_ref, y_ref, csel_ref, clam_ref, wout_ref,
    value_ref, pulled_ref, sem,
):
    def copy(a, b, i):
        return pltpu.make_async_copy(a, b, sem.at[i])

    rlam_in, clam_in = copy(rlam_hbm, rlam_ref, 0), copy(clam_hbm, clam_ref, 1)
    gain_in, x_in = copy(gain_hbm, gain_ref, 2), copy(x_hbm, x_ref, 3)
    win_in, rsel_in = copy(win_hbm, win_ref, 4), copy(rsel_hbm, rsel_ref, 5)
    y_in, wout_in = copy(y_hbm, y_ref, 6), copy(wout_hbm, wout_ref, 7)
    csel_in = copy(csel_hbm, csel_ref, 8)
    for one in (rlam_in, clam_in, gain_in, x_in, win_in, rsel_in, y_in, wout_in, csel_in):
        one.start()
    rlam_in.wait()
    rlam = lam_of(rlam_ref)
    rcum = cum_columns(rlam)
    ending = spread_heads(ending_of(rcum, columns(rlam)))
    clam_in.wait()
    clam = lam_of(clam_ref)
    ccum = cum_columns(clam)
    opening = spread_heads(opening_of(ccum))
    row = iota((8, HEADS), 0)
    head = iota((8, HEADS), 1)
    logs = jnp.where(row % 4 < 2, rcum[TOK - 1 : TOK, :], ccum[TOK - 1 : TOK, :])
    logs = jnp.where(head // 4 == row // 4, logs, 0.0)
    tile = None
    for k, piece in enumerate(parts_of(logs, 3)):
        place = onehot(iota((HEADS, LOGS), 1) == 4 * k + iota((HEADS, LOGS), 0) % 4)
        part = nn(piece, place)
        tile = part if tile is None else tile + part
    tile = tile.astype(BF16)
    for j in range(GROUP):
        message_ref[j * 8 : (j + 1) * 8, HALF:] = tile
    gain_in.wait()
    x_in.wait()
    normed = normalized(x_ref[...].astype(F32), gain_ref[...])
    win_in.wait()
    value = nn(normed, win_ref[...]).astype(BF16)
    value_ref[...] = value
    value_out = copy(value_ref, value_hbm, 9)
    value_out.start()
    rsel_in.wait()
    weighted = (value.astype(F32) * ending).astype(BF16)
    first = state_rows(weighted, turned_select(rsel_ref), 0, 0)
    y_in.wait()
    wout_in.wait()
    pulled = nt(y_ref[...], wout_ref[...]).astype(BF16)
    pulled_ref[...] = pulled
    pulled_out = copy(pulled_ref, pulled_hbm, 10)
    pulled_out.start()
    csel_in.wait()
    weighted = (pulled.astype(F32) * opening).astype(BF16)
    second = state_rows(weighted, turned_select(csel_ref), STATE, 1)
    message_ref[:, :HALF] = (first + second).astype(BF16)
    value_out.wait()
    pulled_out.wait()


def logs_spread(tiles):
    spread = onehot(
        (iota((LOGS, HALF), 0) % 4 == iota((LOGS, HALF), 1) // PART) & (iota((LOGS, HALF), 0) < 12)
    )
    return nn(tiles, spread)


def inner_order(j):
    return j % 2 * 8 + j // 2


def outer_order(j):
    return j % 4 * 4 + j // 4


def tile_at(j):
    return slice(j * 8, (j + 1) * 8)


def stream_mask():
    return iota((8, HALF), 0) % 4 < 2


def pick(a_forward, forward, backward):
    first = stream_mask()
    return jnp.where(first, forward, backward) if a_forward else jnp.where(first, backward, forward)


def inner_scan(tile, decay, a_forward, before_ref):
    spots = [inner_order(j) for j in range(GROUP)]
    state = jnp.zeros((8, HALF), F32)
    forward = {}
    for j in spots:
        forward[j] = state
        state = decay(j) * state + tile(j)
    ahead = state
    state = jnp.zeros((8, HALF), F32)
    for j in reversed(spots):
        before_ref[tile_at(j), :] = pick(a_forward, forward[j], state)
        state = decay(j) * state + tile(j)
    return pick(a_forward, ahead, state).astype(BF16)


def inner_first_kernel(got_ref, before_ref, decay_ref, through_ref, later_ref, total_ref):
    logs = logs_spread(got_ref[:, HALF:])
    decay_ref[...] = jnp.exp(logs)
    total = inner_scan(
        lambda j: got_ref[tile_at(j), :HALF].astype(F32),
        lambda j: decay_ref[tile_at(j), :], True, before_ref,
    )
    compact = jnp.zeros((8, LOGS), F32)
    for j in range(GROUP):
        compact = compact + got_ref[tile_at(j), HALF:].astype(F32)
    compact = compact + pltpu.roll(compact, LOGS - 4, 1) + pltpu.roll(compact, LOGS - 8, 1)
    compact = jnp.where(iota((8, LOGS), 1) < 4, compact, 0.0)
    high = compact.astype(BF16).astype(F32)
    middle = (compact - high).astype(BF16).astype(F32)
    low = compact - high - middle
    compact = (high + pltpu.roll(middle, 4, 1) + pltpu.roll(low, 8, 1)).astype(BF16)
    for j in range(GROUP):
        total_ref[tile_at(j), :HALF] = total
        total_ref[tile_at(j), HALF:] = compact
    spots = [inner_order(j) for j in range(GROUP)]
    gone = jnp.zeros((8, HALF), F32)
    earlier = {}
    for j in spots:
        earlier[j] = gone
        gone = gone + logs[tile_at(j), :]
    gone = jnp.zeros((8, HALF), F32)
    for j in reversed(spots):
        ahead, behind = jnp.exp(earlier[j]), jnp.exp(gone)
        through_ref[tile_at(j), :] = pick(True, ahead, behind)
        later_ref[tile_at(j), :] = pick(False, ahead, behind)
        gone = gone + logs[tile_at(j), :]


def inner_second_kernel(got_ref, decay_ref, before_ref, total_ref):
    total = inner_scan(
        lambda j: got_ref[tile_at(j), :].astype(F32),
        lambda j: decay_ref[tile_at(j), :], False, before_ref,
    )
    for j in range(GROUP):
        total_ref[tile_at(j), :] = total


def outer_scan(mine, tile, decay, a_forward, before_ref, through_ref, out_ref):
    state = jnp.zeros((8, HALF), F32)
    for j in range(GROUP):
        at = outer_order(j)
        state = jnp.where(j < mine, decay(at) * state + tile(at), state)
    ahead = state
    state = jnp.zeros((8, HALF), F32)
    for j in reversed(range(GROUP)):
        at = outer_order(j)
        state = jnp.where(j > mine, decay(at) * state + tile(at), state)
    both = pick(a_forward, ahead, state)
    for j in range(GROUP):
        at = tile_at(j)
        out_ref[at, :] = (through_ref[at, :] * both + before_ref[at, :]).astype(BF16)


def outer_first_kernel(mine_ref, got_ref, before_ref, through_ref, decay_ref, out_ref):
    decay_ref[...] = jnp.exp(logs_spread(got_ref[:, HALF:]))
    outer_scan(
        mine_ref[0], lambda j: got_ref[tile_at(j), :HALF].astype(F32),
        lambda j: decay_ref[tile_at(j), :], True, before_ref, through_ref, out_ref,
    )


def outer_second_kernel(mine_ref, got_ref, before_ref, through_ref, decay_ref, out_ref):
    outer_scan(
        mine_ref[0], lambda j: got_ref[tile_at(j), :].astype(F32),
        lambda j: decay_ref[tile_at(j), :], False, before_ref, through_ref, out_ref,
    )


def row_scan_kernel(value_ref, sel_ref, lam_ref, skip_ref, local_ref, opening_ref, placed_ref):
    lam = lam_of(lam_ref)
    cum_col = cum_columns(lam)
    select = turned_select(sel_ref)
    opening_ref[...] = opening_of(cum_col)
    placed_ref[...] = placed(select, STATE, 0)
    local_scan(value_ref, select, lam, cum_col, None, skip_ref, local_ref, False)


def row_finish_kernel(x_ref, local_ref, opening_ref, placed_ref, got_ref, wout_ref, message_ref):
    carried = carried_of(placed_ref[...], got_ref[...]) * spread_heads(opening_ref[...])
    scanned = (local_ref[...] + carried).astype(BF16)
    mixed = (x_ref[...].astype(F32) + nn(scanned, wout_ref[...])).astype(BF16)
    message_ref[...] = to_message(mixed, row_target)


def col_back_kernel(
    value_ref, sel_ref, lam_ref, skip_ref, got_ref, win_ref, gain_ref, out_ref, local_ref
):
    lam = lam_of(lam_ref)
    cum_col = cum_columns(lam)
    lam_col = columns(lam)
    select = turned_select(sel_ref)
    local_scan(value_ref, select, lam, cum_col, lam_col, skip_ref, local_ref, True)
    carried = carried_of(placed(select, 0, 1), got_ref[...])
    carried = carried * spread_heads(ending_of(cum_col, lam_col))
    scanned = (local_ref[...] + carried).astype(BF16)
    out_ref[...] = gain_ref[...] * nt(scanned, win_ref[...])


def col_grad_kernel(got_ref, y_ref, scaled_ref, x_ref, message_ref):
    x = from_message(got_ref[...], column_target)
    x_ref[...] = x.astype(BF16)
    grad = input_gradient(x, y_ref[...].astype(F32), scaled_ref[...])
    message_ref[...] = to_message(grad, column_target)


def col_value_kernel(
    x_ref, sel_ref, lam_ref, gain_ref, win_ref, rlam_ref, value_ref, part_ref, ropening_ref
):
    value = nn(normalized(x_ref[...].astype(F32), gain_ref[...]), win_ref[...]).astype(BF16)
    value_ref[...] = value
    lam = lam_of(lam_ref)
    ending = spread_heads(ending_of(cum_columns(lam), columns(lam)))
    weighted = (value.astype(F32) * ending).astype(BF16)
    part_ref[...] = state_rows(weighted, turned_select(sel_ref), 0, 1)
    ropening_ref[...] = opening_of(cum_columns(lam_of(rlam_ref)))


def row_pull_kernel(
    got_ref, sel_ref, opening_ref, wout_ref, part_ref, y_ref, pulled_ref, message_ref
):
    y = from_message(got_ref[...], row_target).astype(BF16)
    y_ref[...] = y
    pulled = nt(y, wout_ref[...]).astype(BF16)
    pulled_ref[...] = pulled
    weighted = (pulled.astype(F32) * spread_heads(opening_ref[...])).astype(BF16)
    second = state_rows(weighted, turned_select(sel_ref), STATE, 0)
    message_ref[...] = (part_ref[...] + second).astype(BF16)


def last_scan_kernel(
    value_ref, sel_ref, lam_ref, skip_ref, gain_ref, local_ref, placed_ref, factor_ref, kept_ref,
    *, backward, offset, stream,
):
    kept_ref[...] = gain_ref[...]
    lam = lam_of(lam_ref)
    select = turned_select(sel_ref)
    placed_ref[...] = placed(select, offset, stream)
    cum_col = cum_columns(lam)
    lam_col = columns(lam) if backward else None
    factor_ref[...] = ending_of(cum_col, lam_col) if backward else opening_of(cum_col)
    local_scan(value_ref, select, lam, cum_col, lam_col, skip_ref, local_ref, backward)


def end_kernel(
    got_ref, cplaced_ref, cfactor_ref, clocal_ref, cwout_ref,
    rplaced_ref, rfactor_ref, rlocal_ref, rwin_ref, gain_ref,
    cx_hbm, x_hbm, y_hbm,
    mixed_hbm, grad_hbm, cx_ref, x_ref, y_ref, mixed_ref, grad_ref, sem,
):
    def copy(a, b, i):
        return pltpu.make_async_copy(a, b, sem.at[i])

    x_in, y_in, cx_in = copy(x_hbm, x_ref, 0), copy(y_hbm, y_ref, 1), copy(cx_hbm, cx_ref, 2)
    for one in (x_in, y_in, cx_in):
        one.start()
    got = got_ref[...]
    carried = carried_of(rplaced_ref[...], got) * spread_heads(rfactor_ref[...])
    scanned = (rlocal_ref[...] + carried).astype(BF16)
    scaled = gain_ref[...] * nt(scanned, rwin_ref[...])
    x_in.wait()
    y_in.wait()
    grad_ref[...] = input_gradient(x_ref[...].astype(F32), y_ref[...].astype(F32), scaled)
    grad_out = copy(grad_ref, grad_hbm, 3)
    grad_out.start()
    carried = carried_of(cplaced_ref[...], got) * spread_heads(cfactor_ref[...])
    scanned = (clocal_ref[...] + carried).astype(BF16)
    cx_in.wait()
    mixed_ref[...] = (cx_ref[...].astype(F32) + nn(scanned, cwout_ref[...])).astype(BF16)
    mixed_out = copy(mixed_ref, mixed_hbm, 4)
    mixed_out.start()
    grad_out.wait()
    mixed_out.wait()


VM = pl.BlockSpec(memory_space=pltpu.VMEM)
SM = pl.BlockSpec(memory_space=pltpu.SMEM)
ANY = pl.BlockSpec(memory_space=pl.ANY)


class Near(tuple):
    pass


class Far(tuple):
    pass


def shaped(out):
    if isinstance(out, Near):
        return pltpu.VMEM(*out)
    if isinstance(out, Far):
        return pltpu.HBM(*out)
    return jax.ShapeDtypeStruct(*out)


def near(array):
    return pltpu.with_memory_space_constraint(array, pltpu.VMEM)


def far(array):
    return pltpu.with_memory_space_constraint(array, pltpu.HBM)


def call(kernel, name, outs, args, scalars=(), left=(), kept=(), scratch=(), flops=1e9):
    return pl.pallas_call(
        kernel,
        name=name,
        out_shape=[shaped(out) for out in outs],
        in_specs=[SM if i in scalars else ANY if i in left else VM for i in range(len(args))],
        out_specs=[ANY if i in kept else VM for i in range(len(outs))],
        scratch_shapes=list(scratch),
        compiler_params=pltpu.CompilerParams(vmem_limit_bytes=16 << 20),
        cost_estimate=pl.CostEstimate(flops=int(flops), bytes_accessed=1 << 20, transcendentals=0),
    )(*args)


TOKS = (TOK, WIDTH)
MSG = (LINES, HALF)
LOGGED = (LINES, HALF + LOGS)
PAIR = (TOK, 2 * LINES)
BIG = (2 * TOK, HALF)
FACTOR = (TOK, HEADS)
SEL = (2, 2 * STATE, 128)
LAM = (HEADS, 2, 128)


def swapped(array, axes):
    count = 1
    for axis in axes:
        count *= lax.axis_size(axis)
    split = array.reshape(count, array.shape[0] // count, array.shape[1])
    return lax.all_to_all(split, axes, split_axis=0, concat_axis=0, tiled=True).reshape(array.shape)


def body(
    tokens, row_select, row_decay, row_gain, row_skip, row_in, row_out,
    col_select, col_decay, col_gain, col_skip, col_in, col_out, cotangent,
):
    mine = (lax.axis_index("frame") * lax.axis_size("seq_0") + lax.axis_index("seq_0")).reshape(1)
    x = tokens.reshape(TOKS)
    y = cotangent.reshape(TOKS)
    rsel = row_select.reshape(2, 128, 2 * STATE).swapaxes(1, 2)
    csel = col_select.reshape(2, 128, 2 * STATE).swapaxes(1, 2)
    rlam = row_decay.reshape(HEADS, 2, 128)
    clam = col_decay.reshape(HEADS, 2, 128)
    rgain = row_gain.reshape(1, WIDTH)
    cgain = col_gain.reshape(1, WIDTH)
    rskip = row_skip.reshape(1, HEADS)
    cskip = col_skip.reshape(1, HEADS)

    rvalue, cpulled, message = call(
        start_kernel, "start", [Far((TOKS, BF16)), Far((TOKS, BF16)), Near((LOGGED, BF16))],
        [far(a) for a in (x, rsel, rlam, rgain, row_in, y, csel, clam, col_out)],
        left=range(9), kept=(0, 1),
        scratch=[
            pltpu.VMEM(TOKS, BF16), pltpu.VMEM(SEL, BF16), pltpu.VMEM(LAM, F32),
            pltpu.VMEM((1, WIDTH), F32), pltpu.VMEM((WIDTH, WIDTH), BF16),
            pltpu.VMEM(TOKS, BF16), pltpu.VMEM(SEL, BF16), pltpu.VMEM(LAM, F32),
            pltpu.VMEM((WIDTH, WIDTH), BF16), pltpu.VMEM(TOKS, BF16), pltpu.VMEM(TOKS, BF16),
            pltpu.SemaphoreType.DMA((11,)),
        ],
    )
    message, mine = lax.optimization_barrier((message, mine))
    got = swapped(message, INNER)
    before, decay, through, later, total = call(
        inner_first_kernel, "inner_first",
        [Near((MSG, F32)), Far((MSG, F32)), Near((MSG, F32)), Far((MSG, F32)), Near((LOGGED, BF16))],
        [near(got)], flops=1e7,
    )
    groups = swapped(total, OUTER)
    outer_decay, down = call(
        outer_first_kernel, "outer_first", [Far((MSG, F32)), Near((MSG, BF16))],
        [mine, near(groups), before, through], (0,), flops=1e7,
    )
    got = near(swapped(down, INNER))
    rlocal, ropening, rplaced = call(
        row_scan_kernel, "row_scan", [Near((TOKS, F32)), Near((FACTOR, F32)), Near((PAIR, BF16))],
        [far(rvalue), far(rsel), far(rlam), far(rskip)],
    )
    (sending,) = call(
        row_finish_kernel, "row_finish", [Near((BIG, BF16))],
        [near(x), rlocal, ropening, rplaced, got, near(row_out)],
    )
    arrived = swapped(sending, SEQ)
    (scaled,) = call(
        col_back_kernel, "col_back", [Near((TOKS, F32))],
        [far(cpulled), far(csel), far(clam), far(cskip), got, far(col_in), far(cgain)],
        scratch=[pltpu.VMEM(TOKS, F32)],
    )
    cx, returning = call(
        col_grad_kernel, "col_grad", [Far((TOKS, BF16)), Near((BIG, BF16))],
        [near(arrived), near(y), scaled],
    )
    landed = swapped(returning, SEQ)
    cvalue, part, ropening = call(
        col_value_kernel, "col_value",
        [Far((TOKS, BF16)), Near((MSG, F32)), Near((FACTOR, F32))],
        [far(cx), far(csel), far(clam), far(cgain), far(col_in), far(rlam)],
    )
    ry, rpulled, message = call(
        row_pull_kernel, "row_pull", [Far((TOKS, BF16)), Far((TOKS, BF16)), Near((MSG, BF16))],
        [near(landed), near(rsel), ropening, near(row_out), part],
    )
    got = swapped(message, INNER)
    before, total = call(
        inner_second_kernel, "inner_second", [Near((MSG, F32)), Near((MSG, BF16))],
        [near(got), near(decay)], flops=1e7,
    )
    groups = swapped(total, OUTER)
    (down,) = call(
        outer_second_kernel, "outer_second", [Near((MSG, BF16))],
        [mine, near(groups), before, near(later), near(outer_decay)], (0,), flops=1e7,
    )
    got = swapped(down, INNER)
    clocal, cplaced, cfactor, _ = call(
        partial(last_scan_kernel, backward=False, offset=STATE, stream=1), "col_scan",
        [Near((TOKS, F32)), Near((PAIR, BF16)), Near((FACTOR, F32)), Near(((1, WIDTH), F32))],
        [far(cvalue), far(csel), far(clam), far(cskip), far(cgain)],
    )
    rlocal, rplaced, rfactor, gain = call(
        partial(last_scan_kernel, backward=True, offset=0, stream=0), "row_scan_back",
        [Near((TOKS, F32)), Near((PAIR, BF16)), Near((FACTOR, F32)), Near(((1, WIDTH), F32))],
        [far(rpulled), far(rsel), far(rlam), far(rskip), far(rgain)],
    )
    mixed, grad = call(
        end_kernel, "end", [Far((TOKS, BF16)), Far((TOKS, BF16))],
        [near(got), cplaced, cfactor, clocal, near(col_out), rplaced, rfactor, rlocal,
         near(row_in), gain, far(cx), far(x), far(ry)],
        left=(10, 11, 12), kept=(0, 1),
        scratch=[pltpu.VMEM(TOKS, BF16)] * 5 + [pltpu.SemaphoreType.DMA((5,))],
    )
    return mixed.reshape(cotangent.shape), grad.reshape(tokens.shape)


def solution(mesh):
    torus = Mesh(
        mesh.devices.reshape(4, 8, 2, mesh.shape["frame"]), ("seq_0", "seq_1", "seq_2", "frame")
    )
    tall = P("frame", SEQ, None, None)
    flat = P("frame", None, SEQ, None)
    in_specs = (tall, tall, flat, P(), P(), P(), P(), tall, flat, P(), P(), P(), P(), tall)
    return jax.shard_map(
        body, mesh=torus, in_specs=in_specs, out_specs=(tall, tall), check_vma=False
    )
```

time: 151 us -> 127 us (0.84)
  Pallas kernels: 42.7 us -> 25.7 us
  blocking collectives: 44.3 us -> 51.7 us
  local copies, waits for them, and re-layouts: 5.61 us -> 0.04 us
  waiting for transfers between devices: 31.1 us -> 26 us
  starting transfers between devices: 26 us -> 22.4 us
    pallas_call x15 -> x14, Pallas kernels: 42.7 us -> 25.7 us  [call(): pl.pallas_call(kernel, name=name, out_shape=[shaped(out) for out in outs]...]
    all_to_all x3 -> x4, blocking collectives: 44.3 us -> 51.7 us  [swapped(): lax.all_to_all(split, axes, split_axis=0, concat_axis=0, tiled=True)]
    unnamed x14 -> x18, local copies, waits for them, and re-layouts: 5.61 us -> 0.04 us
    all_to_all x5 -> x4, waiting for transfers between devices: 31.1 us -> 26 us  [swapped(): lax.all_to_all(split, axes, split_axis=0, concat_axis=0, tiled=True)]
    all_to_all x5 -> x4, starting transfers between devices: 26 us -> 22.4 us  [swapped(): lax.all_to_all(split, axes, split_axis=0, concat_axis=0, tiled=True)]
  transfers between devices with their start and end apart: 5 -> 4, of which waited for: 5 -> 4; matrix products, arithmetic and copies ran while one was open for 0% -> 0% of each run, Pallas kernels for 12% -> 10%
where the time goes in v2:
time: 127 us
  blocking collectives  51.7 us (41%)
  waiting for transfers between devices  26 us (20%)
  Pallas kernels  25.7 us (20%)
  starting transfers between devices  22.4 us (18%)
    all_to_all x4, blocking collectives, swapped(): lax.all_to_all(split, axes, split_axis=0, concat_axis=0, tiled=True)  51.7 us
    all_to_all x4, waiting for transfers between devices, swapped(): lax.all_to_all(split, axes, split_axis=0, concat_axis=0, tiled=True)  26 us
    pallas_call x14, Pallas kernels, call(): pl.pallas_call(kernel, name=name, out_shape=[shaped(out) for out in outs]...  25.7 us
    all_to_all x4, starting transfers between devices, swapped(): lax.all_to_all(split, axes, split_axis=0, concat_axis=0, tiled=True)  22.4 us
  transfers between devices with their start and end apart: 4, of which 4 were waited for; matrix products, arithmetic and copies ran while one was open for 0% of the time, Pallas kernels for 10%

profile of v2, /device:TPU:1, one launch (start us, length us, event | category | flops | bytes accessed | tf_op | source)
XLA Modules:
  0.0 126.8 jit_solution(1537416687907805431)
XLA Ops:
  0.6 3.9 %start.1 = (bf16[256,512]{1,0:T(8,128)(2,1)}, bf16[256,512]{1,0:T(8,128)(2,1)}, bf16[128,384]{1,0:T(8,128)(2,1)S(1)}) custom-call(bf16[256,512]{1,0:T(8,128)(2,1)} %bitcast.48, bf16[2,64,128]{2,1,0:T(8,128)(2,1)} %bitcast.51, f32[8,2,128]{2,1,0:T(2,128)} %bitcast.63, f32[1,512]{1,0:T(1,128)} %bitcast.70, bf16[512,512]{1,0:T(8,128)(2,1)} %rwin_ref.1, ...), custom_call_target="tpu_custom_call" | custom-call | flops 1000000000 | bytes 1048576 | tf_op jit(solution)/shard_map/start/pallas_call | solution.py:525
  4.5 17.1 %all_to_all.40 = bf16[16,8,384]{2,1,0:T(8,128)(2,1)S(1)} all-to-all(bf16[16,8,384]{2,1,0:T(8,128)(2,1)S(1)} %bitcast.40), channel_id=1, replica_groups=mesh['seq_0'=4,'seq_1'=8,'seq_2'=2,'frame'=4] {'seq_2','seq_1'}, dimensions={0} | all-to-all | bytes 196608 | tf_op jit(solution)/shard_map/all_to_all | solution.py:552
  21.7 0.9 inner_first.1
  22.5 13.2 %all_to_all.41 = bf16[16,8,384]{2,1,0:T(8,128)(2,1)S(1)} all-to-all(bf16[16,8,384]{2,1,0:T(8,128)(2,1)S(1)} %bitcast.39), channel_id=1, replica_groups=mesh['seq_0'=4,'seq_1'=8,'seq_2'=2,'frame'=4] {'seq_0','frame'}, dimensions={0} | all-to-all | bytes 196608 | tf_op jit(solution)/shard_map/all_to_all | solution.py:552
  35.8 0.8 outer_first.1
  36.6 5.8 %all-to-all-start.2 = ((bf16[16,8,256]{2,1,0:T(8,128)(2,1)}), bf16[16,8,256]{2,1,0:T(8,128)(2,1)S(1)}, u32[]{:S(2)}, u32[]{:S(2)}) async-start(bf16[16,8,256]{2,1,0:T(8,128)(2,1)} %bitcast.16), calls=%async_computation.2 | async-start | bytes 131072 | tf_op jit(solution)/shard_map/all_to_all | solution.py:552
  42.4 0.0 copy-start.3
  42.4 0.0 copy-start.7
  42.4 2.1 %row_scan.1 = (f32[256,512]{1,0:T(8,128)S(1)}, f32[256,8]{1,0:T(8,128)S(1)}, bf16[256,256]{1,0:T(8,128)(2,1)S(1)}) custom-call(bf16[256,512]{1,0:T(8,128)(2,1)} %get-tuple-element.38.value_ref, bf16[2,64,128]{2,1,0:T(8,128)(2,1)} %bitcast.52, f32[8,2,128]{2,1,0:T(2,128)} %bitcast.64, f32[1,8]{1,0:T(1,128)} %bitcast.74), custom_call_target="tpu_custom_call" | custom-call | flops 1000000000 | bytes 1048576 | tf_op jit(solution)/shard_map/row_scan/pallas_call | solution.py:525
  44.5 5.0 %all-to-all-done.2 = bf16[16,8,256]{2,1,0:T(8,128)(2,1)S(1)} async-done(((bf16[16,8,256]{2,1,0:T(8,128)(2,1)}), bf16[16,8,256]{2,1,0:T(8,128)(2,1)S(1)}, u32[]{:S(2)}, u32[]{:S(2)}) %all-to-all-start.2) | async-done | bytes 65568 | tf_op jit(solution)/shard_map/all_to_all | solution.py:552
  49.6 0.0 copy-done.3
  49.6 0.0 copy-done.7
  49.6 1.5 %row_finish.1 = bf16[512,256]{1,0:T(8,128)(2,1)} custom-call(bf16[256,512]{1,0:T(8,128)(2,1)S(1)} %bitcast.50, f32[256,512]{1,0:T(8,128)S(1)} %get-tuple-element.39.local_ref, f32[256,8]{1,0:T(8,128)S(1)} %get-tuple-element.40.opening_ref, bf16[256,256]{1,0:T(8,128)(2,1)S(1)} %get-tuple-element.41.placed_ref, bf16[128,256]{1,0:T(8,128)(2,1)S(1)} %bitcast.42, ...), custom_call_target="tpu_custom_call" | custom-call | flops 1000000000 | bytes 1048576 | tf_op jit(solution)/shard_map/row_finish/pallas_call | solution.py:525
  51.1 4.9 %all-to-all-start.3 = ((bf16[64,8,256]{2,1,0:T(8,128)(2,1)}), bf16[64,8,256]{2,1,0:T(8,128)(2,1)S(1)}, u32[]{:S(2)}, u32[]{:S(2)}) async-start(bf16[64,8,256]{2,1,0:T(8,128)(2,1)} %bitcast.18), calls=%async_computation.3 | async-start | bytes 524288 | tf_op jit(solution)/shard_map/all_to_all | solution.py:552
  56.0 0.0 copy-start.6
  56.0 2.9 %col_back.1.scaled_ref = f32[256,512]{1,0:T(8,128)S(1)} custom-call(bf16[256,512]{1,0:T(8,128)(2,1)} %get-tuple-element.47.value_ref, bf16[2,64,128]{2,1,0:T(8,128)(2,1)} %bitcast.56, f32[8,2,128]{2,1,0:T(2,128)} %bitcast.60, f32[1,8]{1,0:T(1,128)} %bitcast.72, bf16[128,256]{1,0:T(8,128)(2,1)S(1)} %bitcast.43, bf16[512,512]{1,0:T(8,128)(2,1)} %win_ref.3, ...), custom_call_target="tpu_custom_call" | custom-call | flops 1000000000 | bytes 1048576 | tf_op jit(solution)/shard_map/col_back/pallas_call | solution.py:525
  58.9 9.1 %all-to-all-done.3 = bf16[64,8,256]{2,1,0:T(8,128)(2,1)S(1)} async-done(((bf16[64,8,256]{2,1,0:T(8,128)(2,1)}), bf16[64,8,256]{2,1,0:T(8,128)(2,1)S(1)}, u32[]{:S(2)}, u32[]{:S(2)}) %all-to-all-start.3) | async-done | bytes 262176 | tf_op jit(solution)/shard_map/all_to_all | solution.py:552
  68.0 0.0 copy-done.6
  68.0 1.5 %col_grad.1 = (bf16[256,512]{1,0:T(8,128)(2,1)}, bf16[512,256]{1,0:T(8,128)(2,1)}) custom-call(bf16[512,256]{1,0:T(8,128)(2,1)S(1)} %bitcast.38, bf16[256,512]{1,0:T(8,128)(2,1)S(1)} %bitcast.47, f32[256,512]{1,0:T(8,128)S(1)} %col_back.1.scaled_ref), custom_call_target="tpu_custom_call" | custom-call | flops 1000000000 | bytes 1048576 | tf_op jit(solution)/shard_map/col_grad/pallas_call | solution.py:525
  69.5 6.1 %all-to-all-start.4 = ((bf16[64,8,256]{2,1,0:T(8,128)(2,1)}), bf16[64,8,256]{2,1,0:T(8,128)(2,1)S(1)}, u32[]{:S(2)}, u32[]{:S(2)}) async-start(bf16[64,8,256]{2,1,0:T(8,128)(2,1)} %bitcast.23), calls=%async_computation.4 | async-start | bytes 524288 | tf_op jit(solution)/shard_map/all_to_all | solution.py:552
  75.6 0.0 copy-start.8
  75.6 2.4 %col_value.1 = (bf16[256,512]{1,0:T(8,128)(2,1)}, f32[128,256]{1,0:T(8,128)S(1)}, f32[256,8]{1,0:T(8,128)S(1)}) custom-call(bf16[256,512]{1,0:T(8,128)(2,1)} %get-tuple-element.49.x_ref.cx_hbm, bf16[2,64,128]{2,1,0:T(8,128)(2,1)} %bitcast.57, f32[8,2,128]{2,1,0:T(2,128)} %bitcast.61, f32[1,512]{1,0:T(1,128)} %bitcast.68, bf16[512,512]{1,0:T(8,128)(2,1)} %win_ref.3, ...), custom_call_target="tpu_custom_call" | custom-call | flops 1000000000 | bytes 1048576 | tf_op jit(solution)/shard_map/col_value/pallas_call | solution.py:525
  78.0 9.6 %all-to-all-done.4 = bf16[64,8,256]{2,1,0:T(8,128)(2,1)S(1)} async-done(((bf16[64,8,256]{2,1,0:T(8,128)(2,1)}), bf16[64,8,256]{2,1,0:T(8,128)(2,1)S(1)}, u32[]{:S(2)}, u32[]{:S(2)}) %all-to-all-start.4) | async-done | bytes 262176 | tf_op jit(solution)/shard_map/all_to_all | solution.py:552
  87.6 0.0 copy-done.8
  87.6 1.2 row_pull.1
  88.8 0.0 copy-start.2
  88.8 11.6 %all_to_all.42 = bf16[16,8,256]{2,1,0:T(8,128)(2,1)S(1)} all-to-all(bf16[16,8,256]{2,1,0:T(8,128)(2,1)S(1)} %bitcast.44), channel_id=1, replica_groups=mesh['seq_0'=4,'seq_1'=8,'seq_2'=2,'frame'=4] {'seq_2','seq_1'}, dimensions={0} | all-to-all | bytes 131072 | tf_op jit(solution)/shard_map/all_to_all | solution.py:552
  100.4 0.0 copy-done.2
  100.4 0.0 copy-start
  100.4 0.0 copy-start.1
  100.4 0.1 inner_second.1
  100.5 9.7 %all_to_all.43 = bf16[16,8,256]{2,1,0:T(8,128)(2,1)S(1)} all-to-all(bf16[16,8,256]{2,1,0:T(8,128)(2,1)S(1)} %bitcast.45), channel_id=1, replica_groups=mesh['seq_0'=4,'seq_1'=8,'seq_2'=2,'frame'=4] {'seq_0','frame'}, dimensions={0} | all-to-all | bytes 131072 | tf_op jit(solution)/shard_map/all_to_all | solution.py:552
  110.2 0.0 copy-done
  110.2 0.0 copy-done.1
  110.2 0.7 outer_second.1
  110.9 5.6 %all-to-all-start.7 = ((bf16[16,8,256]{2,1,0:T(8,128)(2,1)}), bf16[16,8,256]{2,1,0:T(8,128)(2,1)S(1)}, u32[]{:S(2)}, u32[]{:S(2)}) async-start(bf16[16,8,256]{2,1,0:T(8,128)(2,1)} %bitcast.29), calls=%async_computation.7 | async-start | bytes 131072 | tf_op jit(solution)/shard_map/all_to_all | solution.py:552
  116.6 2.6 %col_scan.1 = (f32[256,512]{1,0:T(8,128)S(1)}, bf16[256,256]{1,0:T(8,128)(2,1)S(1)}, f32[256,8]{1,0:T(8,128)S(1)}, f32[1,512]{1,0:T(1,128)}) custom-call(bf16[256,512]{1,0:T(8,128)(2,1)} %get-tuple-element.58.value_ref, bf16[2,64,128]{2,1,0:T(8,128)(2,1)} %bitcast.58, f32[8,2,128]{2,1,0:T(2,128)} %bitcast.62, f32[1,8]{1,0:T(1,128)} %bitcast.73, ...), custom_call_target="tpu_custom_call" | custom-call | flops 1000000000 | bytes 1048576 | tf_op jit(solution)/shard_map/col_scan/pallas_call | solution.py:525
  119.1 0.0 copy-start.4
  119.1 0.0 copy-start.5
  119.1 2.3 %row_scan_back.1 = (f32[256,512]{1,0:T(8,128)S(1)}, bf16[256,256]{1,0:T(8,128)(2,1)S(1)}, f32[256,8]{1,0:T(8,128)S(1)}, f32[1,512]{1,0:T(1,128)S(1)}) custom-call(bf16[256,512]{1,0:T(8,128)(2,1)} %get-tuple-element.62.value_ref, bf16[2,64,128]{2,1,0:T(8,128)(2,1)} %bitcast.53, f32[8,2,128]{2,1,0:T(2,128)} %bitcast.66, f32[1,8]{1,0:T(1,128)} %bitcast.75, ...), custom_call_target="tpu_custom_call" | custom-call | flops 1000000000 | bytes 1048576 | tf_op jit(solution)/shard_map/row_scan_back/pallas_call | solution.py:525
  121.5 2.3 %all-to-all-done.7 = bf16[16,8,256]{2,1,0:T(8,128)(2,1)S(1)} async-done(((bf16[16,8,256]{2,1,0:T(8,128)(2,1)}), bf16[16,8,256]{2,1,0:T(8,128)(2,1)S(1)}, u32[]{:S(2)}, u32[]{:S(2)}) %all-to-all-start.7) | async-done | bytes 65568 | tf_op jit(solution)/shard_map/all_to_all | solution.py:552
  123.8 0.0 copy-done.4
  123.8 0.0 copy-done.5
  123.8 2.9 %end.1 = (bf16[256,512]{1,0:T(8,128)(2,1)}, bf16[256,512]{1,0:T(8,128)(2,1)}) custom-call(bf16[128,256]{1,0:T(8,128)(2,1)S(1)} %bitcast.41, bf16[256,256]{1,0:T(8,128)(2,1)S(1)} %get-tuple-element.59.cplaced_ref, f32[256,8]{1,0:T(8,128)S(1)} %get-tuple-element.60.cfactor_ref, f32[256,512]{1,0:T(8,128)S(1)} %get-tuple-element.61.clocal_ref, ...), custom_call_target="tpu_custom_call" | custom-call | flops 1000000000 | bytes 1048576 | tf_op jit(solution)/shard_map/end/pallas_call | solution.py:525
Async XLA Ops:
  36.6 13.0 %all-to-all-start.2 = ((bf16[16,8,256]{2,1,0:T(8,128)(2,1)}), bf16[16,8,256]{2,1,0:T(8,128)(2,1)S(1)}, u32[]{:S(2)}, u32[]{:S(2)}) async-start(bf16[16,8,256]{2,1,0:T(8,128)(2,1)} %bitcast.16), calls=%async_computation.2 | async-start | bytes 131072 | tf_op jit(solution)/shard_map/all_to_all | solution.py:552
  42.4 7.2 %copy-start.3 = (bf16[512,512]{1,0:T(8,128)(2,1)S(1)}, bf16[512,512]{1,0:T(8,128)(2,1)}, u32[]{:S(2)}) copy-start(bf16[512,512]{1,0:T(8,128)(2,1)} %wout_ref.3) | copy-start | bytes 1572868
  42.4 7.2 %copy-start.7 = (bf16[1,2,128,512]{3,2,1,0:T(8,128)(2,1)S(1)}, bf16[1,2,128,512]{3,2,1,0:T(8,128)(2,1)}, u32[]{:S(2)}) copy-start(bf16[1,2,128,512]{3,2,1,0:T(8,128)(2,1)} %param.14) | copy-start | bytes 786436
  51.1 16.9 %all-to-all-start.3 = ((bf16[64,8,256]{2,1,0:T(8,128)(2,1)}), bf16[64,8,256]{2,1,0:T(8,128)(2,1)S(1)}, u32[]{:S(2)}, u32[]{:S(2)}) async-start(bf16[64,8,256]{2,1,0:T(8,128)(2,1)} %bitcast.18), calls=%async_computation.3 | async-start | bytes 524288 | tf_op jit(solution)/shard_map/all_to_all | solution.py:552
  56.0 12.0 %copy-start.6 = (bf16[1,2,128,512]{3,2,1,0:T(8,128)(2,1)S(1)}, bf16[1,2,128,512]{3,2,1,0:T(8,128)(2,1)}, u32[]{:S(2)}) copy-start(bf16[1,2,128,512]{3,2,1,0:T(8,128)(2,1)} %param.27) | copy-start | bytes 786436
  69.5 18.1 %all-to-all-start.4 = ((bf16[64,8,256]{2,1,0:T(8,128)(2,1)}), bf16[64,8,256]{2,1,0:T(8,128)(2,1)S(1)}, u32[]{:S(2)}, u32[]{:S(2)}) async-start(bf16[64,8,256]{2,1,0:T(8,128)(2,1)} %bitcast.23), calls=%async_computation.4 | async-start | bytes 524288 | tf_op jit(solution)/shard_map/all_to_all | solution.py:552
  75.6 12.0 %copy-start.8 = (bf16[1,2,128,64]{2,3,1,0:T(8,128)(2,1)S(1)}, bf16[1,2,128,64]{2,3,1,0:T(8,128)(2,1)}, u32[]{:S(2)}) copy-start(bf16[1,2,128,64]{2,3,1,0:T(8,128)(2,1)} %param.15) | copy-start | bytes 98308
  88.8 11.6 %copy-start.2 = (f32[128,256]{1,0:T(8,128)S(1)}, f32[128,256]{1,0:T(8,128)}, u32[]{:S(2)}) copy-start(f32[128,256]{1,0:T(8,128)} %get-tuple-element.53.decay_ref) | copy-start | bytes 393220
  100.4 9.8 %copy-start = (f32[128,256]{1,0:T(8,128)S(1)}, f32[128,256]{1,0:T(8,128)}, u32[]{:S(2)}) copy-start(f32[128,256]{1,0:T(8,128)} %get-tuple-element.56.through_ref) | copy-start | bytes 393220
  100.4 9.8 %copy-start.1 = (f32[128,256]{1,0:T(8,128)S(1)}, f32[128,256]{1,0:T(8,128)}, u32[]{:S(2)}) copy-start(f32[128,256]{1,0:T(8,128)} %get-tuple-element.57.decay_ref) | copy-start | bytes 393220
  110.9 12.8 %all-to-all-start.7 = ((bf16[16,8,256]{2,1,0:T(8,128)(2,1)}), bf16[16,8,256]{2,1,0:T(8,128)(2,1)S(1)}, u32[]{:S(2)}, u32[]{:S(2)}) async-start(bf16[16,8,256]{2,1,0:T(8,128)(2,1)} %bitcast.29), calls=%async_computation.7 | async-start | bytes 131072 | tf_op jit(solution)/shard_map/all_to_all | solution.py:552
  119.1 4.6 %copy-start.4 = (bf16[512,512]{1,0:T(8,128)(2,1)S(1)}, bf16[512,512]{1,0:T(8,128)(2,1)}, u32[]{:S(2)}) copy-start(bf16[512,512]{1,0:T(8,128)(2,1)} %rwin_ref.1) | copy-start | bytes 1572868
  119.1 4.6 %copy-start.5 = (bf16[512,512]{1,0:T(8,128)(2,1)S(1)}, bf16[512,512]{1,0:T(8,128)(2,1)}, u32[]{:S(2)}) copy-start(bf16[512,512]{1,0:T(8,128)(2,1)} %cwout_ref.1) | copy-start | bytes 1572868

commit v3 on v2

--- a/solution.py
+++ b/solution.py
@@ -210,29 +210,31 @@
 
 
 def start_kernel(
-    x_hbm, rsel_hbm, rlam_hbm, gain_hbm, win_hbm, y_hbm, csel_hbm, clam_hbm, wout_hbm,
-    value_hbm, pulled_hbm, message_ref,
-    x_ref, rsel_ref, rlam_ref, gain_ref, win_ref, y_ref, csel_ref, clam_ref, wout_ref,
-    value_ref, pulled_ref, sem,
+    x_hbm, rsel_hbm, rlam_hbm, rskip_hbm, gain_hbm, win_hbm,
+    y_hbm, csel_hbm, clam_hbm, cskip_hbm, wout_hbm,
+    rlocal_ref, rfactor_ref, rplaced_ref, clocal_ref, cfactor_ref, cplaced_ref, sent_hbm,
+    message_ref,
+    x_ref, rsel_ref, rlam_ref, rskip_ref, gain_ref, win_ref,
+    y_ref, csel_ref, clam_ref, cskip_ref, wout_ref, value_ref, pulled_ref, sent_ref, sem,
 ):
-    def copy(a, b, i):
-        return pltpu.make_async_copy(a, b, sem.at[i])
-
-    rlam_in, clam_in = copy(rlam_hbm, rlam_ref, 0), copy(clam_hbm, clam_ref, 1)
-    gain_in, x_in = copy(gain_hbm, gain_ref, 2), copy(x_hbm, x_ref, 3)
-    win_in, rsel_in = copy(win_hbm, win_ref, 4), copy(rsel_hbm, rsel_ref, 5)
-    y_in, wout_in = copy(y_hbm, y_ref, 6), copy(wout_hbm, wout_ref, 7)
-    csel_in = copy(csel_hbm, csel_ref, 8)
-    for one in (rlam_in, clam_in, gain_in, x_in, win_in, rsel_in, y_in, wout_in, csel_in):
-        one.start()
-    rlam_in.wait()
+    pairs = (
+        (rlam_hbm, rlam_ref), (clam_hbm, clam_ref), (rsel_hbm, rsel_ref), (csel_hbm, csel_ref),
+        (rskip_hbm, rskip_ref), (cskip_hbm, cskip_ref), (gain_hbm, gain_ref), (x_hbm, x_ref),
+        (win_hbm, win_ref), (y_hbm, y_ref), (wout_hbm, wout_ref), (sent_ref, sent_hbm),
+    )
+    copies = [pltpu.make_async_copy(a, b, sem.at[i]) for i, (a, b) in enumerate(pairs)]
+    for copy in copies[:11]:
+        copy.start()
+    for copy in copies[:7]:
+        copy.wait()
     rlam = lam_of(rlam_ref)
     rcum = cum_columns(rlam)
+    rsel = turned_select(rsel_ref)
     ending = spread_heads(ending_of(rcum, columns(rlam)))
-    clam_in.wait()
     clam = lam_of(clam_ref)
     ccum = cum_columns(clam)
-    opening = spread_heads(opening_of(ccum))
+    clam_col = columns(clam)
+    csel = turned_select(csel_ref)
     row = iota((8, HEADS), 0)
     head = iota((8, HEADS), 1)
     logs = jnp.where(row % 4 < 2, rcum[TOK - 1 : TOK, :], ccum[TOK - 1 : TOK, :])
@@ -245,29 +247,29 @@
     tile = tile.astype(BF16)
     for j in range(GROUP):
         message_ref[j * 8 : (j + 1) * 8, HALF:] = tile
-    gain_in.wait()
-    x_in.wait()
+    rfactor_ref[...] = opening_of(rcum)
+    cfactor_ref[...] = ending_of(ccum, clam_col)
+    rplaced_ref[...] = placed(rsel, STATE, 0)
+    cplaced_ref[...] = placed(csel, 0, 1)
+    copies[7].wait()
     normed = normalized(x_ref[...].astype(F32), gain_ref[...])
-    win_in.wait()
+    copies[8].wait()
     value = nn(normed, win_ref[...]).astype(BF16)
     value_ref[...] = value
-    value_out = copy(value_ref, value_hbm, 9)
-    value_out.start()
-    rsel_in.wait()
     weighted = (value.astype(F32) * ending).astype(BF16)
-    first = state_rows(weighted, turned_select(rsel_ref), 0, 0)
-    y_in.wait()
-    wout_in.wait()
+    first = state_rows(weighted, rsel, 0, 0)
+    copies[9].wait()
+    sent_ref[...] = to_message(y_ref[...], column_target)
+    copies[11].start()
+    local_scan(value_ref, rsel, rlam, rcum, None, rskip_ref, rlocal_ref, False)
+    copies[10].wait()
     pulled = nt(y_ref[...], wout_ref[...]).astype(BF16)
     pulled_ref[...] = pulled
-    pulled_out = copy(pulled_ref, pulled_hbm, 10)
-    pulled_out.start()
-    csel_in.wait()
-    weighted = (pulled.astype(F32) * opening).astype(BF16)
-    second = state_rows(weighted, turned_select(csel_ref), STATE, 1)
+    weighted = (pulled.astype(F32) * spread_heads(opening_of(ccum))).astype(BF16)
+    second = state_rows(weighted, csel, STATE, 1)
     message_ref[:, :HALF] = (first + second).astype(BF16)
-    value_out.wait()
-    pulled_out.wait()
+    local_scan(pulled_ref, csel, clam, ccum, clam_col, cskip_ref, clocal_ref, True)
+    copies[11].wait()
 
 
 def logs_spread(tiles):
@@ -386,111 +388,114 @@
     )
 
 
-def row_scan_kernel(value_ref, sel_ref, lam_ref, skip_ref, local_ref, opening_ref, placed_ref):
-    lam = lam_of(lam_ref)
-    cum_col = cum_columns(lam)
-    select = turned_select(sel_ref)
-    opening_ref[...] = opening_of(cum_col)
-    placed_ref[...] = placed(select, STATE, 0)
-    local_scan(value_ref, select, lam, cum_col, None, skip_ref, local_ref, False)
-
-
-def row_finish_kernel(x_ref, local_ref, opening_ref, placed_ref, got_ref, wout_ref, message_ref):
-    carried = carried_of(placed_ref[...], got_ref[...]) * spread_heads(opening_ref[...])
-    scanned = (local_ref[...] + carried).astype(BF16)
-    mixed = (x_ref[...].astype(F32) + nn(scanned, wout_ref[...])).astype(BF16)
-    message_ref[...] = to_message(mixed, row_target)
-
-
-def col_back_kernel(
-    value_ref, sel_ref, lam_ref, skip_ref, got_ref, win_ref, gain_ref, out_ref, local_ref
+def finish_kernel(
+    rlocal_ref, rfactor_ref, rplaced_ref, got_ref, wout_ref,
+    clocal_ref, cfactor_ref, cplaced_ref, win_ref, gain_hbm, x_hbm, sent_hbm,
+    mixed_ref, message_ref, gain_ref, x_ref, sem,
 ):
-    lam = lam_of(lam_ref)
-    cum_col = cum_columns(lam)
-    lam_col = columns(lam)
-    select = turned_select(sel_ref)
-    local_scan(value_ref, select, lam, cum_col, lam_col, skip_ref, local_ref, True)
-    carried = carried_of(placed(select, 0, 1), got_ref[...])
-    carried = carried * spread_heads(ending_of(cum_col, lam_col))
-    scanned = (local_ref[...] + carried).astype(BF16)
-    out_ref[...] = gain_ref[...] * nt(scanned, win_ref[...])
-
-
-def col_grad_kernel(got_ref, y_ref, scaled_ref, x_ref, message_ref):
-    x = from_message(got_ref[...], column_target)
-    x_ref[...] = x.astype(BF16)
-    grad = input_gradient(x, y_ref[...].astype(F32), scaled_ref[...])
-    message_ref[...] = to_message(grad, column_target)
-
-
-def col_value_kernel(
-    x_ref, sel_ref, lam_ref, gain_ref, win_ref, rlam_ref, value_ref, part_ref, ropening_ref
+    copies = [
+        pltpu.make_async_copy(x_hbm, x_ref, sem.at[0]),
+        pltpu.make_async_copy(gain_hbm, gain_ref, sem.at[1]),
+        pltpu.make_async_copy(sent_hbm, message_ref.at[:, HALF : 2 * HALF], sem.at[2]),
+    ]
+    for copy in copies:
+        copy.start()
+    got = got_ref[...]
+    carried = carried_of(rplaced_ref[...], got) * spread_heads(rfactor_ref[...])
+    scanned = (rlocal_ref[...] + carried).astype(BF16)
+    total = nn(scanned, wout_ref[...])
+    carried = carried_of(cplaced_ref[...], got) * spread_heads(cfactor_ref[...])
+    scanned = (clocal_ref[...] + carried).astype(BF16)
+    returned = nt(scanned, win_ref[...])
+    copies[0].wait()
+    mixed = (x_ref[...].astype(F32) + total).astype(BF16)
+    mixed_ref[...] = mixed
+    message_ref[:, :HALF] = to_message(mixed, row_target)
+    copies[1].wait()
+    scaled = (gain_ref[...] * returned).astype(BF16)
+    message_ref[:, 2 * HALF :] = to_message(scaled, column_target)
+    copies[2].wait()
+
+
+def cross_kernel(
+    got_ref, mixed_ref, rsel_ref, rfactor_ref, wout_ref, csel_ref, cfactor_ref, gain_ref, win_ref,
+    cx_ref, cvalue_ref, y_ref, pulled_ref, message_ref,
 ):
-    value = nn(normalized(x_ref[...].astype(F32), gain_ref[...]), win_ref[...]).astype(BF16)
-    value_ref[...] = value
-    lam = lam_of(lam_ref)
-    ending = spread_heads(ending_of(cum_columns(lam), columns(lam)))
-    weighted = (value.astype(F32) * ending).astype(BF16)
-    part_ref[...] = state_rows(weighted, turned_select(sel_ref), 0, 1)
-    ropening_ref[...] = opening_of(cum_columns(lam_of(rlam_ref)))
-
-
-def row_pull_kernel(
-    got_ref, sel_ref, opening_ref, wout_ref, part_ref, y_ref, pulled_ref, message_ref
-):
-    y = from_message(got_ref[...], row_target).astype(BF16)
+    y = from_message(got_ref[:, HALF : 2 * HALF], row_target)
+    scaled = from_message(got_ref[:, 2 * HALF :], row_target)
+    y = input_gradient(mixed_ref[...].astype(F32), y, scaled)
     y_ref[...] = y
     pulled = nt(y, wout_ref[...]).astype(BF16)
     pulled_ref[...] = pulled
-    weighted = (pulled.astype(F32) * spread_heads(opening_ref[...])).astype(BF16)
-    second = state_rows(weighted, turned_select(sel_ref), STATE, 0)
-    message_ref[...] = (part_ref[...] + second).astype(BF16)
-
-
-def last_scan_kernel(
-    value_ref, sel_ref, lam_ref, skip_ref, gain_ref, local_ref, placed_ref, factor_ref, kept_ref,
-    *, backward, offset, stream,
+    weighted = (pulled.astype(F32) * spread_heads(rfactor_ref[...])).astype(BF16)
+    first = state_rows(weighted, turned_select(rsel_ref), STATE, 0)
+    x = from_message(got_ref[:, :HALF], column_target)
+    cx_ref[...] = x.astype(BF16)
+    value = nn(normalized(x, gain_ref[...]), win_ref[...]).astype(BF16)
+    cvalue_ref[...] = value
+    weighted = (value.astype(F32) * spread_heads(cfactor_ref[...])).astype(BF16)
+    second = state_rows(weighted, turned_select(csel_ref), 0, 1)
+    message_ref[...] = (first + second).astype(BF16)
+
+
+def col_scan_kernel(
+    value_ref, sel_ref, lam_ref, skip_ref, x_ref, local_ref, placed_ref, factor_ref, kept_ref
+):
+    kept_ref[...] = x_ref[...]
+    lam = lam_of(lam_ref)
+    select = turned_select(sel_ref)
+    placed_ref[...] = placed(select, STATE, 1)
+    cum_col = cum_columns(lam)
+    factor_ref[...] = opening_of(cum_col)
+    local_scan(value_ref, select, lam, cum_col, None, skip_ref, local_ref, False)
+
+
+def row_scan_back_kernel(
+    value_ref, sel_ref, lam_ref, skip_ref, gain_ref, local_ref, placed_ref, factor_ref, kept_ref
 ):
     kept_ref[...] = gain_ref[...]
     lam = lam_of(lam_ref)
     select = turned_select(sel_ref)
-    placed_ref[...] = placed(select, offset, stream)
+    placed_ref[...] = placed(select, 0, 0)
     cum_col = cum_columns(lam)
-    lam_col = columns(lam) if backward else None
-    factor_ref[...] = ending_of(cum_col, lam_col) if backward else opening_of(cum_col)
-    local_scan(value_ref, select, lam, cum_col, lam_col, skip_ref, local_ref, backward)
+    lam_col = columns(lam)
+    factor_ref[...] = ending_of(cum_col, lam_col)
+    local_scan(value_ref, select, lam, cum_col, lam_col, skip_ref, local_ref, True)
 
 
 def end_kernel(
-    got_ref, cplaced_ref, cfactor_ref, clocal_ref, cwout_ref,
-    rplaced_ref, rfactor_ref, rlocal_ref, rwin_ref, gain_ref,
-    cx_hbm, x_hbm, y_hbm,
-    mixed_hbm, grad_hbm, cx_ref, x_ref, y_ref, mixed_ref, grad_ref, sem,
+    got_ref, cplaced_ref, cfactor_ref, clocal_ref, rplaced_ref, rfactor_ref, rlocal_ref, rwin_ref,
+    gain_ref, x_ref, y_ref, cx_hbm, cwout_hbm,
+    mixed_hbm, grad_hbm, cx_ref, cwout_ref, mixed_ref, grad_ref, sem,
 ):
     def copy(a, b, i):
         return pltpu.make_async_copy(a, b, sem.at[i])
 
-    x_in, y_in, cx_in = copy(x_hbm, x_ref, 0), copy(y_hbm, y_ref, 1), copy(cx_hbm, cx_ref, 2)
-    for one in (x_in, y_in, cx_in):
-        one.start()
+    cwout_in, cx_in = copy(cwout_hbm, cwout_ref, 0), copy(cx_hbm, cx_ref, 1)
+    cwout_in.start()
+    cx_in.start()
     got = got_ref[...]
     carried = carried_of(rplaced_ref[...], got) * spread_heads(rfactor_ref[...])
     scanned = (rlocal_ref[...] + carried).astype(BF16)
     scaled = gain_ref[...] * nt(scanned, rwin_ref[...])
-    x_in.wait()
-    y_in.wait()
     grad_ref[...] = input_gradient(x_ref[...].astype(F32), y_ref[...].astype(F32), scaled)
-    grad_out = copy(grad_ref, grad_hbm, 3)
+    grad_out = copy(grad_ref, grad_hbm, 2)
     grad_out.start()
     carried = carried_of(cplaced_ref[...], got) * spread_heads(cfactor_ref[...])
     scanned = (clocal_ref[...] + carried).astype(BF16)
+    cwout_in.wait()
     cx_in.wait()
-    mixed_ref[...] = (cx_ref[...].astype(F32) + nn(scanned, cwout_ref[...])).astype(BF16)
-    mixed_out = copy(mixed_ref, mixed_hbm, 4)
-    mixed_out.start()
+    outs = [copy(mixed_ref.at[rows], mixed_hbm.at[rows], 3 + k) for k, rows in enumerate(QUARTERS)]
+    for rows, out in zip(QUARTERS, outs):
+        mixed = cx_ref[rows, :].astype(F32) + nn(scanned[rows, :], cwout_ref[...])
+        mixed_ref[rows, :] = mixed.astype(BF16)
+        out.start()
     grad_out.wait()
-    mixed_out.wait()
-
+    for out in outs:
+        out.wait()
+
+
+QUARTERS = [slice(k * 64, (k + 1) * 64) for k in range(4)]
 
 VM = pl.BlockSpec(memory_space=pltpu.VMEM)
 SM = pl.BlockSpec(memory_space=pltpu.SMEM)
@@ -539,6 +544,7 @@
 LOGGED = (LINES, HALF + LOGS)
 PAIR = (TOK, 2 * LINES)
 BIG = (2 * TOK, HALF)
+WIDE = (2 * TOK, 3 * HALF)
 FACTOR = (TOK, HEADS)
 SEL = (2, 2 * STATE, 128)
 LAM = (HEADS, 2, 128)
@@ -568,16 +574,21 @@
     rskip = row_skip.reshape(1, HEADS)
     cskip = col_skip.reshape(1, HEADS)
 
-    rvalue, cpulled, message = call(
-        start_kernel, "start", [Far((TOKS, BF16)), Far((TOKS, BF16)), Near((LOGGED, BF16))],
-        [far(a) for a in (x, rsel, rlam, rgain, row_in, y, csel, clam, col_out)],
-        left=range(9), kept=(0, 1),
+    rlocal, rfactor, rplaced, clocal, cfactor, cplaced, sent, message = call(
+        start_kernel, "start",
+        [Near((TOKS, F32)), Near((FACTOR, F32)), Near((PAIR, BF16)),
+         Near((TOKS, F32)), Near((FACTOR, F32)), Near((PAIR, BF16)), Far((BIG, BF16)),
+         Near((LOGGED, BF16))],
+        [far(a) for a in
+         (x, rsel, rlam, rskip, rgain, row_in, y, csel, clam, cskip, col_out)],
+        left=range(11), kept=(6,),
         scratch=[
             pltpu.VMEM(TOKS, BF16), pltpu.VMEM(SEL, BF16), pltpu.VMEM(LAM, F32),
-            pltpu.VMEM((1, WIDTH), F32), pltpu.VMEM((WIDTH, WIDTH), BF16),
-            pltpu.VMEM(TOKS, BF16), pltpu.VMEM(SEL, BF16), pltpu.VMEM(LAM, F32),
-            pltpu.VMEM((WIDTH, WIDTH), BF16), pltpu.VMEM(TOKS, BF16), pltpu.VMEM(TOKS, BF16),
-            pltpu.SemaphoreType.DMA((11,)),
+            pltpu.VMEM((1, HEADS), F32), pltpu.VMEM((1, WIDTH), F32),
+            pltpu.VMEM((WIDTH, WIDTH), BF16), pltpu.VMEM(TOKS, BF16), pltpu.VMEM(SEL, BF16),
+            pltpu.VMEM(LAM, F32), pltpu.VMEM((1, HEADS), F32), pltpu.VMEM((WIDTH, WIDTH), BF16),
+            pltpu.VMEM(TOKS, BF16), pltpu.VMEM(TOKS, BF16), pltpu.VMEM(BIG, BF16),
+            pltpu.SemaphoreType.DMA((12,)),
         ],
     )
     message, mine = lax.optimization_barrier((message, mine))
@@ -593,33 +604,22 @@
         [mine, near(groups), before, through], (0,), flops=1e7,
     )
     got = near(swapped(down, INNER))
-    rlocal, ropening, rplaced = call(
-        row_scan_kernel, "row_scan", [Near((TOKS, F32)), Near((FACTOR, F32)), Near((PAIR, BF16))],
-        [far(rvalue), far(rsel), far(rlam), far(rskip)],
-    )
-    (sending,) = call(
-        row_finish_kernel, "row_finish", [Near((BIG, BF16))],
-        [near(x), rlocal, ropening, rplaced, got, near(row_out)],
+    rmixed, sending = call(
+        finish_kernel, "finish", [Near((TOKS, BF16)), Near((WIDE, BF16))],
+        [rlocal, rfactor, rplaced, got, near(row_out), clocal, cfactor, cplaced, near(col_in),
+         far(cgain), far(x), far(sent)],
+        left=(9, 10, 11),
+        scratch=[
+            pltpu.VMEM((1, WIDTH), F32), pltpu.VMEM(TOKS, BF16), pltpu.SemaphoreType.DMA((3,)),
+        ],
     )
     arrived = swapped(sending, SEQ)
-    (scaled,) = call(
-        col_back_kernel, "col_back", [Near((TOKS, F32))],
-        [far(cpulled), far(csel), far(clam), far(cskip), got, far(col_in), far(cgain)],
-        scratch=[pltpu.VMEM(TOKS, F32)],
-    )
-    cx, returning = call(
-        col_grad_kernel, "col_grad", [Far((TOKS, BF16)), Near((BIG, BF16))],
-        [near(arrived), near(y), scaled],
-    )
-    landed = swapped(returning, SEQ)
-    cvalue, part, ropening = call(
-        col_value_kernel, "col_value",
-        [Far((TOKS, BF16)), Near((MSG, F32)), Near((FACTOR, F32))],
-        [far(cx), far(csel), far(clam), far(cgain), far(col_in), far(rlam)],
-    )
-    ry, rpulled, message = call(
-        row_pull_kernel, "row_pull", [Far((TOKS, BF16)), Far((TOKS, BF16)), Near((MSG, BF16))],
-        [near(landed), near(rsel), ropening, near(row_out), part],
+    cx, cvalue, ry, rpulled, message = call(
+        cross_kernel, "cross",
+        [Near((TOKS, BF16)), Near((TOKS, BF16)), Near((TOKS, BF16)), Near((TOKS, BF16)),
+         Near((MSG, BF16))],
+        [near(arrived), rmixed, near(rsel), rfactor, near(row_out), near(csel), cfactor,
+         near(cgain), near(col_in)],
     )
     got = swapped(message, INNER)
     before, total = call(
@@ -632,22 +632,25 @@
         [mine, near(groups), before, near(later), near(outer_decay)], (0,), flops=1e7,
     )
     got = swapped(down, INNER)
-    clocal, cplaced, cfactor, _ = call(
-        partial(last_scan_kernel, backward=False, offset=STATE, stream=1), "col_scan",
+    clocal, cplaced, cfactor, cx = call(
+        col_scan_kernel, "col_scan",
+        [Near((TOKS, F32)), Near((PAIR, BF16)), Near((FACTOR, F32)), Far((TOKS, BF16))],
+        [cvalue, far(csel), far(clam), far(cskip), cx],
+    )
+    rlocal, rplaced, rfactor, gain = call(
+        row_scan_back_kernel, "row_scan_back",
         [Near((TOKS, F32)), Near((PAIR, BF16)), Near((FACTOR, F32)), Near(((1, WIDTH), F32))],
-        [far(cvalue), far(csel), far(clam), far(cskip), far(cgain)],
-    )
-    rlocal, rplaced, rfactor, gain = call(
-        partial(last_scan_kernel, backward=True, offset=0, stream=0), "row_scan_back",
-        [Near((TOKS, F32)), Near((PAIR, BF16)), Near((FACTOR, F32)), Near(((1, WIDTH), F32))],
-        [far(rpulled), far(rsel), far(rlam), far(rskip), far(rgain)],
+        [rpulled, far(rsel), far(rlam), far(rskip), far(rgain)],
     )
     mixed, grad = call(
         end_kernel, "end", [Far((TOKS, BF16)), Far((TOKS, BF16))],
-        [near(got), cplaced, cfactor, clocal, near(col_out), rplaced, rfactor, rlocal,
-         near(row_in), gain, far(cx), far(x), far(ry)],
-        left=(10, 11, 12), kept=(0, 1),
-        scratch=[pltpu.VMEM(TOKS, BF16)] * 5 + [pltpu.SemaphoreType.DMA((5,))],
+        [near(got), cplaced, cfactor, clocal, rplaced, rfactor, rlocal, near(row_in),
+         gain, near(x), ry, far(cx), far(col_out)],
+        left=(11, 12), kept=(0, 1),
+        scratch=[
+            pltpu.VMEM(TOKS, BF16), pltpu.VMEM((WIDTH, WIDTH), BF16), pltpu.VMEM(TOKS, BF16),
+            pltpu.VMEM(TOKS, BF16), pltpu.SemaphoreType.DMA((7,)),
+        ],
     )
     return mixed.reshape(cotangent.shape), grad.reshape(tokens.shape)
 

time: 127 us -> 121 us (0.953)
  blocking collectives: 51.7 us -> 91.3 us
  waiting for transfers between devices: 26 us -> 2.57 us
  starting transfers between devices: 22.4 us -> 5.65 us
  Pallas kernels: 25.7 us -> 19.6 us
    all_to_all x4 -> x6, blocking collectives: 51.7 us -> 91.3 us  [swapped(): lax.all_to_all(split, axes, split_axis=0, concat_axis=0, tiled=True)]
    all_to_all x4 -> x1, waiting for transfers between devices: 26 us -> 2.57 us  [swapped(): lax.all_to_all(split, axes, split_axis=0, concat_axis=0, tiled=True)]
    all_to_all x4 -> x1, starting transfers between devices: 22.4 us -> 5.65 us  [swapped(): lax.all_to_all(split, axes, split_axis=0, concat_axis=0, tiled=True)]
    pallas_call x14 -> x10, Pallas kernels: 25.7 us -> 19.6 us  [call(): pl.pallas_call(kernel, name=name, out_shape=[shaped(out) for out in outs]...]
  transfers between devices with their start and end apart: 4 -> 1, of which waited for: 4 -> 1; matrix products, arithmetic and copies ran while one was open for 0% -> 0% of each run, Pallas kernels for 10% -> 4%
where the time goes in v3:
time: 121 us
  blocking collectives  91.3 us (75%)
  Pallas kernels  19.6 us (16%)
  starting transfers between devices  5.65 us (5%)
  waiting for transfers between devices  2.57 us (2%)
    all_to_all x6, blocking collectives, swapped(): lax.all_to_all(split, axes, split_axis=0, concat_axis=0, tiled=True)  91.3 us
    pallas_call x10, Pallas kernels, call(): pl.pallas_call(kernel, name=name, out_shape=[shaped(out) for out in outs]...  19.6 us
    all_to_all x1, starting transfers between devices, swapped(): lax.all_to_all(split, axes, split_axis=0, concat_axis=0, tiled=True)  5.65 us
    all_to_all x1, waiting for transfers between devices, swapped(): lax.all_to_all(split, axes, split_axis=0, concat_axis=0, tiled=True)  2.57 us
  transfers between devices with their start and end apart: 1, of which 1 were waited for; matrix products, arithmetic and copies ran while one was open for 0% of the time, Pallas kernels for 4%

profile of v3, /device:TPU:1, one launch (start us, length us, event | category | flops | bytes accessed | tf_op | source)
XLA Modules:
  0.0 120.7 jit_solution(6987793234493218029)
XLA Ops:
  0.6 0.0 copy-start.4
  0.6 5.3 %start.1 = (f32[256,512]{1,0:T(8,128)S(1)}, f32[256,8]{1,0:T(8,128)S(1)}, bf16[256,256]{1,0:T(8,128)(2,1)S(1)}, f32[256,512]{1,0:T(8,128)S(1)}, f32[256,8]{1,0:T...) custom-call(bf16[256,512]{1,0:T(8,128)(2,1)} %bitcast.44, ...), custom_call_target="tpu_custom_call" | custom-call | flops 1000000000 | bytes 1048576 | tf_op jit(solution)/shard_map/start/pallas_call | solution.py:530
  6.0 0.0 copy-start.3
  6.0 17.3 %all_to_all.35 = bf16[16,8,384]{2,1,0:T(8,128)(2,1)S(1)} all-to-all(bf16[16,8,384]{2,1,0:T(8,128)(2,1)S(1)} %bitcast.37), channel_id=1, replica_groups=mesh['seq_0'=4,'seq_1'=8,'seq_2'=2,'frame'=4] {'seq_2','seq_1'}, dimensions={0} | all-to-all | bytes 196608 | tf_op jit(solution)/shard_map/all_to_all | solution.py:558
  23.2 0.9 inner_first.1
  24.1 13.3 %all_to_all.36 = bf16[16,8,384]{2,1,0:T(8,128)(2,1)S(1)} all-to-all(bf16[16,8,384]{2,1,0:T(8,128)(2,1)S(1)} %bitcast.38), channel_id=1, replica_groups=mesh['seq_0'=4,'seq_1'=8,'seq_2'=2,'frame'=4] {'seq_0','frame'}, dimensions={0} | all-to-all | bytes 196608 | tf_op jit(solution)/shard_map/all_to_all | solution.py:558
  37.4 0.8 outer_first.1
  38.2 12.0 %all_to_all.37 = bf16[16,8,256]{2,1,0:T(8,128)(2,1)S(1)} all-to-all(bf16[16,8,256]{2,1,0:T(8,128)(2,1)S(1)} %bitcast.42), channel_id=1, replica_groups=mesh['seq_0'=4,'seq_1'=8,'seq_2'=2,'frame'=4] {'seq_2','seq_1'}, dimensions={0} | all-to-all | bytes 131072 | tf_op jit(solution)/shard_map/all_to_all | solution.py:558
  50.2 0.0 copy-done.4
  50.2 0.0 copy-done.3
  50.2 2.6 %finish.1 = (bf16[256,512]{1,0:T(8,128)(2,1)S(1)}, bf16[512,768]{1,0:T(8,128)(2,1)S(1)}) custom-call(f32[256,512]{1,0:T(8,128)S(1)} %get-tuple-element.40.rlocal_ref, f32[256,8]{1,0:T(8,128)S(1)} %get-tuple-element.41.rfactor_ref, bf16[256,256]{1,0:T(8,128)(2,1)S(1)} %get-tuple-element.42.rplaced_ref, bf16[128,256]{1,0:T(8,128)(2,1)S(1)} %bitcast.40, ...), custom_call_target="tpu_custom_call" | custom-call | flops 1000000000 | bytes 1048576 | tf_op jit(solution)/shard_map/finish/pallas_call | solution.py:530
  52.9 0.0 copy-start.7
  52.9 0.0 copy-start.8
  52.9 27.2 %all_to_all.38 = bf16[64,8,768]{2,1,0:T(8,128)(2,1)S(1)} all-to-all(bf16[64,8,768]{2,1,0:T(8,128)(2,1)S(1)} %bitcast.32), channel_id=1, replica_groups=mesh['seq_0'=4,'seq_1'=8,'seq_2'=2,'frame'=4] {'seq_0','seq_1','seq_2'}, dimensions={0} | all-to-all | bytes 1572864 | tf_op jit(solution)/shard_map/all_to_all | solution.py:558
  80.1 0.0 copy-start.9
  80.1 0.0 copy-done.7
  80.1 0.0 copy-done.8
  80.1 0.7 copy-done.9
  80.7 2.0 %cross.1 = (bf16[256,512]{1,0:T(8,128)(2,1)S(1)}, bf16[256,512]{1,0:T(8,128)(2,1)S(1)}, bf16[256,512]{1,0:T(8,128)(2,1)S(1)}, bf16[256,512]{1,0:T(8,128)(2,1)S(1)}, bf16[128,256]{1,0:T(8,128)(2,1)S(1)}) custom-call(bf16[512,768]{1,0:T(8,128)(2,1)S(1)} %bitcast.31, bf16[256,512]{1,0:T(8,128)(2,1)S(1)} %get-tuple-element.53.mixed_ref, ...), custom_call_target="tpu_custom_call" | custom-call | flops 1000000000 | bytes 1048576 | tf_op jit(solution)/shard_map/cross/pallas_call | solution.py:530
  82.7 0.0 copy-start.2
  82.7 11.8 %all_to_all.39 = bf16[16,8,256]{2,1,0:T(8,128)(2,1)S(1)} all-to-all(bf16[16,8,256]{2,1,0:T(8,128)(2,1)S(1)} %bitcast.41), channel_id=1, replica_groups=mesh['seq_0'=4,'seq_1'=8,'seq_2'=2,'frame'=4] {'seq_2','seq_1'}, dimensions={0} | all-to-all | bytes 131072 | tf_op jit(solution)/shard_map/all_to_all | solution.py:558
  94.6 0.0 copy-done.2
  94.6 0.0 copy-start
  94.6 0.0 copy-start.1
  94.6 0.1 inner_second.1
  94.6 9.7 %all_to_all.40 = bf16[16,8,256]{2,1,0:T(8,128)(2,1)S(1)} all-to-all(bf16[16,8,256]{2,1,0:T(8,128)(2,1)S(1)} %bitcast.43), channel_id=1, replica_groups=mesh['seq_0'=4,'seq_1'=8,'seq_2'=2,'frame'=4] {'seq_0','frame'}, dimensions={0} | all-to-all | bytes 131072 | tf_op jit(solution)/shard_map/all_to_all | solution.py:558
  104.4 0.0 copy-done
  104.4 0.0 copy-done.1
  104.4 0.7 outer_second.1
  105.1 5.6 %all-to-all-start.6 = ((bf16[16,8,256]{2,1,0:T(8,128)(2,1)}), bf16[16,8,256]{2,1,0:T(8,128)(2,1)S(1)}, u32[]{:S(2)}, u32[]{:S(2)}) async-start(bf16[16,8,256]{2,1,0:T(8,128)(2,1)} %bitcast.27), calls=%async_computation.6 | async-start | bytes 131072 | tf_op jit(solution)/shard_map/all_to_all | solution.py:558
  110.7 2.0 %row_scan_back.1 = (f32[256,512]{1,0:T(8,128)S(1)}, bf16[256,256]{1,0:T(8,128)(2,1)S(1)}, f32[256,8]{1,0:T(8,128)S(1)}, f32[1,512]{1,0:T(1,128)S(1)}) custom-call(bf16[256,512]{1,0:T(8,128)(2,1)S(1)} %get-tuple-element.65.value_ref, bf16[2,64,128]{2,1,0:T(8,128)(2,1)} %bitcast.48, f32[8,2,128]{2,1,0:T(2,128)} %bitcast.57, f32[1,8]{1,0:T(1,128)} %bitcast.63, ...), custom_call_target="tpu_custom_call" | custom-call | flops 1000000000 | bytes 1048576 | tf_op jit(solution)/shard_map/row_scan_back/pallas_call | solution.py:530
  112.8 0.0 copy-start.5
  112.8 0.0 copy-start.6
  112.8 2.6 %col_scan.1 = (f32[256,512]{1,0:T(8,128)S(1)}, bf16[256,256]{1,0:T(8,128)(2,1)S(1)}, f32[256,8]{1,0:T(8,128)S(1)}, bf16[256,512]{1,0:T(8,128)(2,1)}) custom-call(bf16[256,512]{1,0:T(8,128)(2,1)S(1)} %get-tuple-element.60.value_ref, bf16[2,64,128]{2,1,0:T(8,128)(2,1)} %bitcast.51, f32[8,2,128]{2,1,0:T(2,128)} %bitcast.59, f32[1,8]{1,0:T(1,128)} %bitcast.65, ...), custom_call_target="tpu_custom_call" | custom-call | flops 1000000000 | bytes 1048576 | tf_op jit(solution)/shard_map/col_scan/pallas_call | solution.py:530
  115.4 2.6 %all-to-all-done.6 = bf16[16,8,256]{2,1,0:T(8,128)(2,1)S(1)} async-done(((bf16[16,8,256]{2,1,0:T(8,128)(2,1)}), bf16[16,8,256]{2,1,0:T(8,128)(2,1)S(1)}, u32[]{:S(2)}, u32[]{:S(2)}) %all-to-all-start.6) | async-done | bytes 65568 | tf_op jit(solution)/shard_map/all_to_all | solution.py:558
  117.9 0.0 copy-done.5
  117.9 0.0 copy-done.6
  117.9 2.7 %end.1 = (bf16[256,512]{1,0:T(8,128)(2,1)}, bf16[256,512]{1,0:T(8,128)(2,1)}) custom-call(bf16[128,256]{1,0:T(8,128)(2,1)S(1)} %bitcast.39, bf16[256,256]{1,0:T(8,128)(2,1)S(1)} %get-tuple-element.62.cplaced_ref, f32[256,8]{1,0:T(8,128)S(1)} %get-tuple-element.63.cfactor_ref, f32[256,512]{1,0:T(8,128)S(1)} %get-tuple-element.64.clocal_ref, ...), custom_call_target="tpu_custom_call" | custom-call | flops 1000000000 | bytes 1048576 | tf_op jit(solution)/shard_map/end/pallas_call | solution.py:530
Async XLA Ops:
  0.6 49.6 %copy-start.4 = (bf16[512,512]{1,0:T(8,128)(2,1)S(1)}, bf16[512,512]{1,0:T(8,128)(2,1)}, u32[]{:S(2)}) copy-start(bf16[512,512]{1,0:T(8,128)(2,1)} %win_ref.3) | copy-start | bytes 1572868
  6.0 44.3 %copy-start.3 = (bf16[512,512]{1,0:T(8,128)(2,1)S(1)}, bf16[512,512]{1,0:T(8,128)(2,1)}, u32[]{:S(2)}) copy-start(bf16[512,512]{1,0:T(8,128)(2,1)} %wout_ref.3) | copy-start | bytes 1572868
  52.9 27.2 %copy-start.7 = (bf16[1,2,128,64]{2,3,1,0:T(8,128)(2,1)S(1)}, bf16[1,2,128,64]{2,3,1,0:T(8,128)(2,1)}, u32[]{:S(2)}) copy-start(bf16[1,2,128,64]{2,3,1,0:T(8,128)(2,1)} %param.15) | copy-start | bytes 98308
  52.9 27.2 %copy-start.8 = (bf16[1,2,128,64]{2,3,1,0:T(8,128)(2,1)S(1)}, bf16[1,2,128,64]{2,3,1,0:T(8,128)(2,1)}, u32[]{:S(2)}) copy-start(bf16[1,2,128,64]{2,3,1,0:T(8,128)(2,1)} %param.21) | copy-start | bytes 98308
  80.1 0.7 copy-start.9
  82.7 11.9 %copy-start.2 = (f32[128,256]{1,0:T(8,128)S(1)}, f32[128,256]{1,0:T(8,128)}, u32[]{:S(2)}) copy-start(f32[128,256]{1,0:T(8,128)} %get-tuple-element.55.decay_ref) | copy-start | bytes 393220
  94.6 9.8 %copy-start = (f32[128,256]{1,0:T(8,128)S(1)}, f32[128,256]{1,0:T(8,128)}, u32[]{:S(2)}) copy-start(f32[128,256]{1,0:T(8,128)} %get-tuple-element.58.through_ref) | copy-start | bytes 393220
  94.6 9.8 %copy-start.1 = (f32[128,256]{1,0:T(8,128)S(1)}, f32[128,256]{1,0:T(8,128)}, u32[]{:S(2)}) copy-start(f32[128,256]{1,0:T(8,128)} %get-tuple-element.59.decay_ref) | copy-start | bytes 393220
  105.1 12.8 %all-to-all-start.6 = ((bf16[16,8,256]{2,1,0:T(8,128)(2,1)}), bf16[16,8,256]{2,1,0:T(8,128)(2,1)S(1)}, u32[]{:S(2)}, u32[]{:S(2)}) async-start(bf16[16,8,256]{2,1,0:T(8,128)(2,1)} %bitcast.27), calls=%async_computation.6 | async-start | bytes 131072 | tf_op jit(solution)/shard_map/all_to_all | solution.py:558
  112.8 5.2 %copy-start.5 = (bf16[512,512]{1,0:T(8,128)(2,1)S(1)}, bf16[512,512]{1,0:T(8,128)(2,1)}, u32[]{:S(2)}) copy-start(bf16[512,512]{1,0:T(8,128)(2,1)} %rwin_ref.1) | copy-start | bytes 1572868
  112.8 5.2 %copy-start.6 = (bf16[1,2,128,512]{3,2,1,0:T(8,128)(2,1)S(1)}, bf16[1,2,128,512]{3,2,1,0:T(8,128)(2,1)}, u32[]{:S(2)}) copy-start(bf16[1,2,128,512]{3,2,1,0:T(8,128)(2,1)} %param.14) | copy-start | bytes 786436

commit v4 on v3

--- a/solution.py
+++ b/solution.py
@@ -80,37 +80,27 @@
     return jnp.concatenate([select_ref[0], select_ref[1]], axis=1)
 
 
-def triangle():
-    return onehot(iota((TOK, TOK), 1) <= iota((TOK, TOK), 0))
-
-
-def cum_columns(lam):
-    upto = triangle()
-    return sum(nt(upto, p) for p in reversed(parts_of(lam, 3)))
-
-
-def cum_rows(lam):
-    upto = triangle()
-    return sum(nt(p, upto) for p in reversed(parts_of(lam, 3)))
-
-
-def columns(lam):
-    same = onehot(iota((TOK, TOK), 1) == iota((TOK, TOK), 0))
-    return sum(nt(same, p) for p in reversed(parts_of(lam, 3)))
-
-
-def spread_heads(values):
-    spread = onehot(iota((HEADS, WIDTH), 1) // PART == iota((HEADS, WIDTH), 0))
-    return sum(nn(p, spread) for p in reversed(parts_of(values, 2)))
-
-
-def opening_of(cum_col):
-    return jnp.exp(cum_col)
-
-
-def ending_of(cum_col, lam_col):
-    last = cum_col[TOK - 1 : TOK, :]
-    return jnp.exp(last - cum_col) * jnp.sqrt(one_minus_exp(-2.0 * lam_col))
+def block_terms(lam):
+    upto = onehot(iota((TOK, TOK), 1) <= iota((TOK, TOK), 0))
+    stacked = nt(jnp.concatenate(parts_of(lam, 3), axis=0), upto)
+    cum = stacked[:8] + stacked[8:16] + stacked[16:]
+    square = one_minus_exp(-2.0 * lam)
+    ending = jnp.exp(cum[:, TOK - 1 :] - cum) * jnp.sqrt(square)
+    log_inward = jnp.maximum(0.5 * jnp.log2(square), -500.0)
+    rows = jnp.concatenate([cum * LOG2E, log_inward - cum * LOG2E], axis=0)
+    cols = jnp.concatenate([rows, jnp.exp(cum), ending], axis=0).T
+    return cum, rows, cols
+
+
+OPENING = 16
+ENDING = 24
+
+
+def spread_heads(cols, offset):
+    spread = onehot(
+        iota((4 * HEADS, WIDTH), 1) // PART + offset == iota((4 * HEADS, WIDTH), 0)
+    )
+    return sum(nn(p, spread) for p in reversed(parts_of(cols, 2)))
 
 
 def placed(select, offset, stream):
@@ -150,42 +140,39 @@
     return (y + factor * scaled - x * (factor * factor * factor) * inner).astype(BF16)
 
 
-def local_scan(values_ref, select, lam, cum_col, lam_col, skip_ref, out_ref, backward):
-    cum_row = cum_rows(lam)
+def local_scan(values_ref, select, rows, cols, skip_ref, out_ref, backward):
     source = select[:STATE]
     target = select[STATE:]
     if backward:
         affinity = tn(source, target)
-        left = 0.5 * jnp.log2(one_minus_exp(-2.0 * lam_col)) - cum_col * LOG2E
-        right = cum_row * LOG2E
+        left, right = cols[:, HEADS : 2 * HEADS], rows[:HEADS]
     else:
         affinity = tn(target, source)
-        left = cum_col * LOG2E
-        right = 0.5 * jnp.log2(one_minus_exp(-2.0 * lam)) - cum_row * LOG2E
+        left, right = cols[:, :HEADS], rows[HEADS : 2 * HEADS]
     first = iota((128, 128), 0)
     second = iota((128, 128), 1)
     keep = second >= first if backward else second <= first
+    lower = iota((1, 2 * PART), 1) < PART
     lo, hi = slice(0, 128), slice(128, 256)
-    for h in range(HEADS):
-        span = slice(h * PART, (h + 1) * PART)
-        lc = left[:, h : h + 1]
-        rr = right[h : h + 1, :]
-
-        def tile(a, b, masked):
-            m = jnp.exp2(lc[a] + rr[:, b]) * affinity[a, b]
-            return (jnp.where(keep, m, 0.0) if masked else m).astype(BF16)
-
-        v_lo = values_ref[lo, span]
-        v_hi = values_ref[hi, span]
-        skip = skip_ref[0:1, h : h + 1]
-        if backward:
-            top = nn(tile(lo, lo, True), v_lo) + nn(tile(lo, hi, False), v_hi)
-            low = nn(tile(hi, hi, True), v_hi)
-        else:
-            top = nn(tile(lo, lo, True), v_lo)
-            low = nn(tile(hi, lo, False), v_lo) + nn(tile(hi, hi, True), v_hi)
-        out_ref[lo, span] = top + skip * v_lo.astype(F32)
-        out_ref[hi, span] = low + skip * v_hi.astype(F32)
+
+    def tile(h, a, b):
+        m = jnp.exp2(left[a, h : h + 1] + right[h : h + 1, b]) * affinity[a, b]
+        return (jnp.where(keep, m, 0.0) if a == b else m).astype(BF16)
+
+    def mixed(pair, rows, sources, parts):
+        tiles = [tile(h, rows, b) for h in pair for b in sources]
+        values = [part[b] for part in parts for b in sources]
+        return nn(jnp.concatenate(tiles, axis=1), jnp.concatenate(values, axis=0))
+
+    for h in range(0, HEADS, 2):
+        span = slice(h * PART, (h + 2) * PART)
+        v = values_ref[:, span].astype(F32)
+        parts = [jnp.where(lower, v, 0.0).astype(BF16), jnp.where(lower, 0.0, v).astype(BF16)]
+        skip = jnp.where(lower, skip_ref[0:1, h : h + 1], skip_ref[0:1, h + 1 : h + 2])
+        top = mixed((h, h + 1), lo, (lo, hi) if backward else (lo,), parts)
+        low = mixed((h, h + 1), hi, (hi,) if backward else (lo, hi), parts)
+        out_ref[lo, span] = top + skip * v[lo]
+        out_ref[hi, span] = low + skip * v[hi]
 
 
 def row_target(token):
@@ -212,8 +199,8 @@
 def start_kernel(
     x_hbm, rsel_hbm, rlam_hbm, rskip_hbm, gain_hbm, win_hbm,
     y_hbm, csel_hbm, clam_hbm, cskip_hbm, wout_hbm,
-    rlocal_ref, rfactor_ref, rplaced_ref, clocal_ref, cfactor_ref, cplaced_ref, sent_hbm,
-    message_ref,
+    rlocal_ref, rcols_ref, rrows_ref, rplaced_ref, clocal_ref, ccols_ref, crows_ref, cplaced_ref,
+    sent_hbm, message_ref,
     x_ref, rsel_ref, rlam_ref, rskip_ref, gain_ref, win_ref,
     y_ref, csel_ref, clam_ref, cskip_ref, wout_ref, value_ref, pulled_ref, sent_ref, sem,
 ):
@@ -227,17 +214,19 @@
         copy.start()
     for copy in copies[:7]:
         copy.wait()
-    rlam = lam_of(rlam_ref)
-    rcum = cum_columns(rlam)
+    rcum, rrows, rcols = block_terms(lam_of(rlam_ref))
+    ccum, crows, ccols = block_terms(lam_of(clam_ref))
+    rrows_ref[...] = rrows
+    rcols_ref[...] = rcols
+    crows_ref[...] = crows
+    ccols_ref[...] = ccols
     rsel = turned_select(rsel_ref)
-    ending = spread_heads(ending_of(rcum, columns(rlam)))
-    clam = lam_of(clam_ref)
-    ccum = cum_columns(clam)
-    clam_col = columns(clam)
     csel = turned_select(csel_ref)
     row = iota((8, HEADS), 0)
     head = iota((8, HEADS), 1)
-    logs = jnp.where(row % 4 < 2, rcum[TOK - 1 : TOK, :], ccum[TOK - 1 : TOK, :])
+    rlast = jnp.broadcast_to(rcum[:, TOK - 1 :], (HEADS, HEADS)).T
+    clast = jnp.broadcast_to(ccum[:, TOK - 1 :], (HEADS, HEADS)).T
+    logs = jnp.where(row % 4 < 2, rlast, clast)
     logs = jnp.where(head // 4 == row // 4, logs, 0.0)
     tile = None
     for k, piece in enumerate(parts_of(logs, 3)):
@@ -247,8 +236,6 @@
     tile = tile.astype(BF16)
     for j in range(GROUP):
         message_ref[j * 8 : (j + 1) * 8, HALF:] = tile
-    rfactor_ref[...] = opening_of(rcum)
-    cfactor_ref[...] = ending_of(ccum, clam_col)
     rplaced_ref[...] = placed(rsel, STATE, 0)
     cplaced_ref[...] = placed(csel, 0, 1)
     copies[7].wait()
@@ -256,19 +243,19 @@
     copies[8].wait()
     value = nn(normed, win_ref[...]).astype(BF16)
     value_ref[...] = value
-    weighted = (value.astype(F32) * ending).astype(BF16)
+    weighted = (value.astype(F32) * spread_heads(rcols, ENDING)).astype(BF16)
     first = state_rows(weighted, rsel, 0, 0)
     copies[9].wait()
     sent_ref[...] = to_message(y_ref[...], column_target)
     copies[11].start()
-    local_scan(value_ref, rsel, rlam, rcum, None, rskip_ref, rlocal_ref, False)
+    local_scan(value_ref, rsel, rrows, rcols, rskip_ref, rlocal_ref, False)
     copies[10].wait()
     pulled = nt(y_ref[...], wout_ref[...]).astype(BF16)
     pulled_ref[...] = pulled
-    weighted = (pulled.astype(F32) * spread_heads(opening_of(ccum))).astype(BF16)
+    weighted = (pulled.astype(F32) * spread_heads(ccols, OPENING)).astype(BF16)
     second = state_rows(weighted, csel, STATE, 1)
     message_ref[:, :HALF] = (first + second).astype(BF16)
-    local_scan(pulled_ref, csel, clam, ccum, clam_col, cskip_ref, clocal_ref, True)
+    local_scan(pulled_ref, csel, crows, ccols, cskip_ref, clocal_ref, True)
     copies[11].wait()
 
 
@@ -300,28 +287,31 @@
     return jnp.where(first, forward, backward) if a_forward else jnp.where(first, backward, forward)
 
 
-def inner_scan(tile, decay, a_forward, before_ref):
+def inner_pass(got_ref, logs_ref, a_forward, through_ref, before_ref, decay_ref):
+    logs = logs_spread(logs_ref[...])
+    decay_ref[...] = jnp.exp(logs)
     spots = [inner_order(j) for j in range(GROUP)]
     state = jnp.zeros((8, HALF), F32)
+    gone = jnp.zeros((8, HALF), F32)
     forward = {}
     for j in spots:
-        forward[j] = state
-        state = decay(j) * state + tile(j)
+        forward[j] = state, gone
+        state = decay_ref[tile_at(j), :] * state + got_ref[tile_at(j), :HALF].astype(F32)
+        gone = gone + logs[tile_at(j), :]
     ahead = state
     state = jnp.zeros((8, HALF), F32)
+    gone = jnp.zeros((8, HALF), F32)
     for j in reversed(spots):
-        before_ref[tile_at(j), :] = pick(a_forward, forward[j], state)
-        state = decay(j) * state + tile(j)
+        before_ref[tile_at(j), :] = pick(a_forward, forward[j][0], state)
+        through_ref[tile_at(j), :] = jnp.exp(pick(a_forward, forward[j][1], gone))
+        state = decay_ref[tile_at(j), :] * state + got_ref[tile_at(j), :HALF].astype(F32)
+        gone = gone + logs[tile_at(j), :]
     return pick(a_forward, ahead, state).astype(BF16)
 
 
-def inner_first_kernel(got_ref, before_ref, decay_ref, through_ref, later_ref, total_ref):
-    logs = logs_spread(got_ref[:, HALF:])
-    decay_ref[...] = jnp.exp(logs)
-    total = inner_scan(
-        lambda j: got_ref[tile_at(j), :HALF].astype(F32),
-        lambda j: decay_ref[tile_at(j), :], True, before_ref,
-    )
+def inner_first_kernel(got_ref, before_ref, through_ref, logs_ref, total_ref, decay_ref):
+    logs_ref[...] = got_ref[:, HALF:]
+    total = inner_pass(got_ref, logs_ref, True, through_ref, before_ref, decay_ref)
     compact = jnp.zeros((8, LOGS), F32)
     for j in range(GROUP):
         compact = compact + got_ref[tile_at(j), HALF:].astype(F32)
@@ -334,63 +324,53 @@
     for j in range(GROUP):
         total_ref[tile_at(j), :HALF] = total
         total_ref[tile_at(j), HALF:] = compact
-    spots = [inner_order(j) for j in range(GROUP)]
-    gone = jnp.zeros((8, HALF), F32)
-    earlier = {}
-    for j in spots:
-        earlier[j] = gone
-        gone = gone + logs[tile_at(j), :]
-    gone = jnp.zeros((8, HALF), F32)
-    for j in reversed(spots):
-        ahead, behind = jnp.exp(earlier[j]), jnp.exp(gone)
-        through_ref[tile_at(j), :] = pick(True, ahead, behind)
-        later_ref[tile_at(j), :] = pick(False, ahead, behind)
-        gone = gone + logs[tile_at(j), :]
-
-
-def inner_second_kernel(got_ref, decay_ref, before_ref, total_ref):
-    total = inner_scan(
-        lambda j: got_ref[tile_at(j), :].astype(F32),
-        lambda j: decay_ref[tile_at(j), :], False, before_ref,
-    )
+
+
+def inner_second_kernel(got_ref, logs_ref, before_ref, through_ref, total_ref, decay_ref):
+    total = inner_pass(got_ref, logs_ref, False, through_ref, before_ref, decay_ref)
     for j in range(GROUP):
         total_ref[tile_at(j), :] = total
 
 
-def outer_scan(mine, tile, decay, a_forward, before_ref, through_ref, out_ref):
+def outer_pass(mine, got_ref, logs, a_forward, before_ref, through_ref, out_ref, decay_ref):
+    decay_ref[...] = jnp.exp(logs_spread(logs))
+
+    def step(state, at):
+        return decay_ref[tile_at(at), :] * state + got_ref[tile_at(at), :HALF].astype(F32)
+
     state = jnp.zeros((8, HALF), F32)
     for j in range(GROUP):
-        at = outer_order(j)
-        state = jnp.where(j < mine, decay(at) * state + tile(at), state)
+        state = jnp.where(j < mine, step(state, outer_order(j)), state)
     ahead = state
     state = jnp.zeros((8, HALF), F32)
     for j in reversed(range(GROUP)):
-        at = outer_order(j)
-        state = jnp.where(j > mine, decay(at) * state + tile(at), state)
+        state = jnp.where(j > mine, step(state, outer_order(j)), state)
     both = pick(a_forward, ahead, state)
     for j in range(GROUP):
         at = tile_at(j)
         out_ref[at, :] = (through_ref[at, :] * both + before_ref[at, :]).astype(BF16)
 
 
-def outer_first_kernel(mine_ref, got_ref, before_ref, through_ref, decay_ref, out_ref):
-    decay_ref[...] = jnp.exp(logs_spread(got_ref[:, HALF:]))
-    outer_scan(
-        mine_ref[0], lambda j: got_ref[tile_at(j), :HALF].astype(F32),
-        lambda j: decay_ref[tile_at(j), :], True, before_ref, through_ref, out_ref,
-    )
-
-
-def outer_second_kernel(mine_ref, got_ref, before_ref, through_ref, decay_ref, out_ref):
-    outer_scan(
-        mine_ref[0], lambda j: got_ref[tile_at(j), :].astype(F32),
-        lambda j: decay_ref[tile_at(j), :], False, before_ref, through_ref, out_ref,
+def outer_first_kernel(
+    mine_ref, got_ref, before_ref, through_ref, logs_ref, out_ref, decay_ref
+):
+    logs_ref[...] = got_ref[:, HALF:]
+    outer_pass(
+        mine_ref[0], got_ref, got_ref[:, HALF:], True, before_ref, through_ref, out_ref, decay_ref
+    )
+
+
+def outer_second_kernel(
+    mine_ref, got_ref, before_ref, through_ref, logs_ref, out_ref, decay_ref
+):
+    outer_pass(
+        mine_ref[0], got_ref, logs_ref[...], False, before_ref, through_ref, out_ref, decay_ref
     )
 
 
 def finish_kernel(
-    rlocal_ref, rfactor_ref, rplaced_ref, got_ref, wout_ref,
-    clocal_ref, cfactor_ref, cplaced_ref, win_ref, gain_hbm, x_hbm, sent_hbm,
+    rlocal_ref, rcols_ref, rplaced_ref, got_ref, wout_ref,
+    clocal_ref, ccols_ref, cplaced_ref, win_ref, gain_hbm, x_hbm, sent_hbm,
     mixed_ref, message_ref, gain_ref, x_ref, sem,
 ):
     copies = [
@@ -401,10 +381,10 @@
     for copy in copies:
         copy.start()
     got = got_ref[...]
-    carried = carried_of(rplaced_ref[...], got) * spread_heads(rfactor_ref[...])
+    carried = carried_of(rplaced_ref[...], got) * spread_heads(rcols_ref[...], OPENING)
     scanned = (rlocal_ref[...] + carried).astype(BF16)
     total = nn(scanned, wout_ref[...])
-    carried = carried_of(cplaced_ref[...], got) * spread_heads(cfactor_ref[...])
+    carried = carried_of(cplaced_ref[...], got) * spread_heads(ccols_ref[...], ENDING)
     scanned = (clocal_ref[...] + carried).astype(BF16)
     returned = nt(scanned, win_ref[...])
     copies[0].wait()
@@ -418,7 +398,7 @@
 
 
 def cross_kernel(
-    got_ref, mixed_ref, rsel_ref, rfactor_ref, wout_ref, csel_ref, cfactor_ref, gain_ref, win_ref,
+    got_ref, mixed_ref, rsel_ref, rcols_ref, wout_ref, csel_ref, ccols_ref, gain_ref, win_ref,
     cx_ref, cvalue_ref, y_ref, pulled_ref, message_ref,
 ):
     y = from_message(got_ref[:, HALF : 2 * HALF], row_target)
@@ -427,44 +407,37 @@
     y_ref[...] = y
     pulled = nt(y, wout_ref[...]).astype(BF16)
     pulled_ref[...] = pulled
-    weighted = (pulled.astype(F32) * spread_heads(rfactor_ref[...])).astype(BF16)
+    weighted = (pulled.astype(F32) * spread_heads(rcols_ref[...], OPENING)).astype(BF16)
     first = state_rows(weighted, turned_select(rsel_ref), STATE, 0)
     x = from_message(got_ref[:, :HALF], column_target)
     cx_ref[...] = x.astype(BF16)
     value = nn(normalized(x, gain_ref[...]), win_ref[...]).astype(BF16)
     cvalue_ref[...] = value
-    weighted = (value.astype(F32) * spread_heads(cfactor_ref[...])).astype(BF16)
+    weighted = (value.astype(F32) * spread_heads(ccols_ref[...], ENDING)).astype(BF16)
     second = state_rows(weighted, turned_select(csel_ref), 0, 1)
     message_ref[...] = (first + second).astype(BF16)
 
 
 def col_scan_kernel(
-    value_ref, sel_ref, lam_ref, skip_ref, x_ref, local_ref, placed_ref, factor_ref, kept_ref
+    value_ref, sel_ref, rows_ref, cols_ref, skip_ref, x_ref, local_ref, placed_ref, kept_ref
 ):
     kept_ref[...] = x_ref[...]
-    lam = lam_of(lam_ref)
     select = turned_select(sel_ref)
     placed_ref[...] = placed(select, STATE, 1)
-    cum_col = cum_columns(lam)
-    factor_ref[...] = opening_of(cum_col)
-    local_scan(value_ref, select, lam, cum_col, None, skip_ref, local_ref, False)
+    local_scan(value_ref, select, rows_ref[...], cols_ref[...], skip_ref, local_ref, False)
 
 
 def row_scan_back_kernel(
-    value_ref, sel_ref, lam_ref, skip_ref, gain_ref, local_ref, placed_ref, factor_ref, kept_ref
+    value_ref, sel_ref, rows_ref, cols_ref, skip_ref, gain_ref, local_ref, placed_ref, kept_ref
 ):
     kept_ref[...] = gain_ref[...]
-    lam = lam_of(lam_ref)
     select = turned_select(sel_ref)
     placed_ref[...] = placed(select, 0, 0)
-    cum_col = cum_columns(lam)
-    lam_col = columns(lam)
-    factor_ref[...] = ending_of(cum_col, lam_col)
-    local_scan(value_ref, select, lam, cum_col, lam_col, skip_ref, local_ref, True)
+    local_scan(value_ref, select, rows_ref[...], cols_ref[...], skip_ref, local_ref, True)
 
 
 def end_kernel(
-    got_ref, cplaced_ref, cfactor_ref, clocal_ref, rplaced_ref, rfactor_ref, rlocal_ref, rwin_ref,
+    got_ref, cplaced_ref, ccols_ref, clocal_ref, rplaced_ref, rcols_ref, rlocal_ref, rwin_ref,
     gain_ref, x_ref, y_ref, cx_hbm, cwout_hbm,
     mixed_hbm, grad_hbm, cx_ref, cwout_ref, mixed_ref, grad_ref, sem,
 ):
@@ -475,13 +448,13 @@
     cwout_in.start()
     cx_in.start()
     got = got_ref[...]
-    carried = carried_of(rplaced_ref[...], got) * spread_heads(rfactor_ref[...])
+    carried = carried_of(rplaced_ref[...], got) * spread_heads(rcols_ref[...], ENDING)
     scanned = (rlocal_ref[...] + carried).astype(BF16)
     scaled = gain_ref[...] * nt(scanned, rwin_ref[...])
     grad_ref[...] = input_gradient(x_ref[...].astype(F32), y_ref[...].astype(F32), scaled)
     grad_out = copy(grad_ref, grad_hbm, 2)
     grad_out.start()
-    carried = carried_of(cplaced_ref[...], got) * spread_heads(cfactor_ref[...])
+    carried = carried_of(cplaced_ref[...], got) * spread_heads(ccols_ref[...], OPENING)
     scanned = (clocal_ref[...] + carried).astype(BF16)
     cwout_in.wait()
     cx_in.wait()
@@ -545,7 +518,8 @@
 PAIR = (TOK, 2 * LINES)
 BIG = (2 * TOK, HALF)
 WIDE = (2 * TOK, 3 * HALF)
-FACTOR = (TOK, HEADS)
+ROWS = (2 * HEADS, TOK)
+COLS = (TOK, 4 * HEADS)
 SEL = (2, 2 * STATE, 128)
 LAM = (HEADS, 2, 128)
 
@@ -574,14 +548,14 @@
     rskip = row_skip.reshape(1, HEADS)
     cskip = col_skip.reshape(1, HEADS)
 
-    rlocal, rfactor, rplaced, clocal, cfactor, cplaced, sent, message = call(
+    rlocal, rcols, rrows, rplaced, clocal, ccols, crows, cplaced, sent, message = call(
         start_kernel, "start",
-        [Near((TOKS, F32)), Near((FACTOR, F32)), Near((PAIR, BF16)),
-         Near((TOKS, F32)), Near((FACTOR, F32)), Near((PAIR, BF16)), Far((BIG, BF16)),
-         Near((LOGGED, BF16))],
+        [Near((TOKS, F32)), Near((COLS, F32)), Near((ROWS, F32)), Near((PAIR, BF16)),
+         Near((TOKS, F32)), Near((COLS, F32)), Near((ROWS, F32)), Near((PAIR, BF16)),
+         Far((BIG, BF16)), Near((LOGGED, BF16))],
         [far(a) for a in
          (x, rsel, rlam, rskip, rgain, row_in, y, csel, clam, cskip, col_out)],
-        left=range(11), kept=(6,),
+        left=range(11), kept=(8,),
         scratch=[
             pltpu.VMEM(TOKS, BF16), pltpu.VMEM(SEL, BF16), pltpu.VMEM(LAM, F32),
             pltpu.VMEM((1, HEADS), F32), pltpu.VMEM((1, WIDTH), F32),
@@ -593,58 +567,57 @@
     )
     message, mine = lax.optimization_barrier((message, mine))
     got = swapped(message, INNER)
-    before, decay, through, later, total = call(
+    before, through, inner_logs, total = call(
         inner_first_kernel, "inner_first",
-        [Near((MSG, F32)), Far((MSG, F32)), Near((MSG, F32)), Far((MSG, F32)), Near((LOGGED, BF16))],
-        [near(got)], flops=1e7,
+        [Near((MSG, F32)), Near((MSG, F32)), Near(((LINES, LOGS), BF16)), Near((LOGGED, BF16))],
+        [near(got)], scratch=[pltpu.VMEM(MSG, F32)], flops=1e7,
     )
     groups = swapped(total, OUTER)
-    outer_decay, down = call(
-        outer_first_kernel, "outer_first", [Far((MSG, F32)), Near((MSG, BF16))],
-        [mine, near(groups), before, through], (0,), flops=1e7,
+    outer_logs, down = call(
+        outer_first_kernel, "outer_first", [Near(((LINES, LOGS), BF16)), Near((MSG, BF16))],
+        [mine, near(groups), before, through], (0,), scratch=[pltpu.VMEM(MSG, F32)], flops=1e7,
     )
     got = near(swapped(down, INNER))
-    rmixed, sending = call(
-        finish_kernel, "finish", [Near((TOKS, BF16)), Near((WIDE, BF16))],
-        [rlocal, rfactor, rplaced, got, near(row_out), clocal, cfactor, cplaced, near(col_in),
+    rmixed, sending, gain = call(
+        finish_kernel, "finish",
+        [Near((TOKS, BF16)), Near((WIDE, BF16)), Near(((1, WIDTH), F32))],
+        [rlocal, rcols, rplaced, got, near(row_out), clocal, ccols, cplaced, near(col_in),
          far(cgain), far(x), far(sent)],
         left=(9, 10, 11),
-        scratch=[
-            pltpu.VMEM((1, WIDTH), F32), pltpu.VMEM(TOKS, BF16), pltpu.SemaphoreType.DMA((3,)),
-        ],
+        scratch=[pltpu.VMEM(TOKS, BF16), pltpu.SemaphoreType.DMA((3,))],
     )
     arrived = swapped(sending, SEQ)
     cx, cvalue, ry, rpulled, message = call(
         cross_kernel, "cross",
         [Near((TOKS, BF16)), Near((TOKS, BF16)), Near((TOKS, BF16)), Near((TOKS, BF16)),
          Near((MSG, BF16))],
-        [near(arrived), rmixed, near(rsel), rfactor, near(row_out), near(csel), cfactor,
-         near(cgain), near(col_in)],
+        [near(arrived), rmixed, near(rsel), rcols, near(row_out), near(csel), ccols,
+         gain, near(col_in)],
     )
     got = swapped(message, INNER)
-    before, total = call(
-        inner_second_kernel, "inner_second", [Near((MSG, F32)), Near((MSG, BF16))],
-        [near(got), near(decay)], flops=1e7,
+    before, through, total = call(
+        inner_second_kernel, "inner_second", [Near((MSG, F32)), Near((MSG, F32)), Near((MSG, BF16))],
+        [near(got), inner_logs], scratch=[pltpu.VMEM(MSG, F32)], flops=1e7,
     )
     groups = swapped(total, OUTER)
     (down,) = call(
         outer_second_kernel, "outer_second", [Near((MSG, BF16))],
-        [mine, near(groups), before, near(later), near(outer_decay)], (0,), flops=1e7,
+        [mine, near(groups), before, through, outer_logs], (0,),
+        scratch=[pltpu.VMEM(MSG, F32)], flops=1e7,
     )
     got = swapped(down, INNER)
-    clocal, cplaced, cfactor, cx = call(
-        col_scan_kernel, "col_scan",
-        [Near((TOKS, F32)), Near((PAIR, BF16)), Near((FACTOR, F32)), Far((TOKS, BF16))],
-        [cvalue, far(csel), far(clam), far(cskip), cx],
-    )
-    rlocal, rplaced, rfactor, gain = call(
+    clocal, cplaced, cx = call(
+        col_scan_kernel, "col_scan", [Near((TOKS, F32)), Near((PAIR, BF16)), Far((TOKS, BF16))],
+        [cvalue, far(csel), crows, ccols, far(cskip), cx],
+    )
+    rlocal, rplaced, gain = call(
         row_scan_back_kernel, "row_scan_back",
-        [Near((TOKS, F32)), Near((PAIR, BF16)), Near((FACTOR, F32)), Near(((1, WIDTH), F32))],
-        [rpulled, far(rsel), far(rlam), far(rskip), far(rgain)],
+        [Near((TOKS, F32)), Near((PAIR, BF16)), Near(((1, WIDTH), F32))],
+        [rpulled, far(rsel), rrows, rcols, far(rskip), far(rgain)],
     )
     mixed, grad = call(
         end_kernel, "end", [Far((TOKS, BF16)), Far((TOKS, BF16))],
-        [near(got), cplaced, cfactor, clocal, rplaced, rfactor, rlocal, near(row_in),
+        [near(got), cplaced, ccols, clocal, rplaced, rcols, rlocal, near(row_in),
          gain, near(x), ry, far(cx), far(col_out)],
         left=(11, 12), kept=(0, 1),
         scratch=[

time: 121 us -> 117 us (0.967)
  Pallas kernels: 19.6 us -> 15.6 us
    pallas_call x10, Pallas kernels: 19.6 us -> 15.6 us  [call(): pl.pallas_call(kernel, name=name, out_shape=[shaped(out) for out in outs]...]
  transfers between devices with their start and end apart: 1 -> 1, of which waited for: 1 -> 1; matrix products, arithmetic and copies ran while one was open for 0% -> 0% of each run, Pallas kernels for 4% -> 3%
where the time goes in v4:
time: 117 us
  blocking collectives  91.1 us (78%)
  Pallas kernels  15.6 us (13%)
  starting transfers between devices  5.65 us (5%)
  waiting for transfers between devices  3.61 us (3%)
    all_to_all x6, blocking collectives, swapped(): lax.all_to_all(split, axes, split_axis=0, concat_axis=0, tiled=True)  91.1 us
    pallas_call x10, Pallas kernels, call(): pl.pallas_call(kernel, name=name, out_shape=[shaped(out) for out in outs]...  15.6 us
    all_to_all x1, starting transfers between devices, swapped(): lax.all_to_all(split, axes, split_axis=0, concat_axis=0, tiled=True)  5.65 us
    all_to_all x1, waiting for transfers between devices, swapped(): lax.all_to_all(split, axes, split_axis=0, concat_axis=0, tiled=True)  3.61 us
  transfers between devices with their start and end apart: 1, of which 1 were waited for; matrix products, arithmetic and copies ran while one was open for 0% of the time, Pallas kernels for 3%

profile of v4, /device:TPU:1, one launch (start us, length us, event | category | flops | bytes accessed | tf_op | source)
XLA Modules:
  0.0 116.7 jit_solution(3838081986375168496)
XLA Ops:
  0.6 0.0 copy-start.1
  0.6 3.8 %start.1 = (f32[256,512]{1,0:T(8,128)S(1)}, f32[256,32]{1,0:T(8,128)S(1)}, f32[16,256]{1,0:T(8,128)S(1)}, bf16[256,256]{1,0:T(8,128)(2,1)S(1)}, f32[256,512]{1,0...) custom-call(bf16[256,512]{1,0:T(8,128)(2,1)} %bitcast.44, ...), custom_call_target="tpu_custom_call" | custom-call | flops 1000000000 | bytes 1048576 | tf_op jit(solution)/shard_map/start/pallas_call | solution.py:503
  4.4 0.0 copy-start
  4.4 17.3 %all_to_all.35 = bf16[16,8,384]{2,1,0:T(8,128)(2,1)S(1)} all-to-all(bf16[16,8,384]{2,1,0:T(8,128)(2,1)S(1)} %bitcast.37), channel_id=1, replica_groups=mesh['seq_0'=4,'seq_1'=8,'seq_2'=2,'frame'=4] {'seq_2','seq_1'}, dimensions={0} | all-to-all | bytes 196608 | tf_op jit(solution)/shard_map/all_to_all | solution.py:532
  21.7 0.2 inner_first.1
  21.9 13.3 %all_to_all.36 = bf16[16,8,384]{2,1,0:T(8,128)(2,1)S(1)} all-to-all(bf16[16,8,384]{2,1,0:T(8,128)(2,1)S(1)} %bitcast.38), channel_id=1, replica_groups=mesh['seq_0'=4,'seq_1'=8,'seq_2'=2,'frame'=4] {'seq_0','frame'}, dimensions={0} | all-to-all | bytes 196608 | tf_op jit(solution)/shard_map/all_to_all | solution.py:532
  35.1 0.2 outer_first.1
  35.4 12.0 %all_to_all.37 = bf16[16,8,256]{2,1,0:T(8,128)(2,1)S(1)} all-to-all(bf16[16,8,256]{2,1,0:T(8,128)(2,1)S(1)} %bitcast.42), channel_id=1, replica_groups=mesh['seq_0'=4,'seq_1'=8,'seq_2'=2,'frame'=4] {'seq_2','seq_1'}, dimensions={0} | all-to-all | bytes 131072 | tf_op jit(solution)/shard_map/all_to_all | solution.py:532
  47.4 0.0 copy-done.1
  47.4 0.0 copy-done
  47.4 2.7 %finish.1 = (bf16[256,512]{1,0:T(8,128)(2,1)S(1)}, bf16[512,768]{1,0:T(8,128)(2,1)S(1)}, f32[1,512]{1,0:T(1,128)S(1)}) custom-call(f32[256,512]{1,0:T(8,128)S(1)} %get-tuple-element.41.rlocal_ref, f32[256,32]{1,0:T(8,128)S(1)} %get-tuple-element.42.rcols_ref.cols_ref, bf16[256,256]{1,0:T(8,128)(2,1)S(1)} %get-tuple-element.43.rplaced_ref, ...), custom_call_target="tpu_custom_call" | custom-call | flops 1000000000 | bytes 1048576 | tf_op jit(solution)/shard_map/finish/pallas_call | solution.py:503
  50.1 0.0 copy-start.4
  50.1 0.0 copy-start.5
  50.1 27.2 %all_to_all.38 = bf16[64,8,768]{2,1,0:T(8,128)(2,1)S(1)} all-to-all(bf16[64,8,768]{2,1,0:T(8,128)(2,1)S(1)} %bitcast.31), channel_id=1, replica_groups=mesh['seq_0'=4,'seq_1'=8,'seq_2'=2,'frame'=4] {'seq_0','seq_1','seq_2'}, dimensions={0} | all-to-all | bytes 1572864 | tf_op jit(solution)/shard_map/all_to_all | solution.py:532
  77.3 0.0 copy-done.4
  77.3 0.0 copy-done.5
  77.3 2.0 %cross.1 = (bf16[256,512]{1,0:T(8,128)(2,1)S(1)}, bf16[256,512]{1,0:T(8,128)(2,1)S(1)}, bf16[256,512]{1,0:T(8,128)(2,1)S(1)}, bf16[256,512]{1,0:T(8,128)(2,1)S(1)}, bf16[128,256]{1,0:T(8,128)(2,1)S(1)}) custom-call(bf16[512,768]{1,0:T(8,128)(2,1)S(1)} %bitcast.32, bf16[256,512]{1,0:T(8,128)(2,1)S(1)} %get-tuple-element.54.mixed_ref, ...), custom_call_target="tpu_custom_call" | custom-call | flops 1000000000 | bytes 1048576 | tf_op jit(solution)/shard_map/cross/pallas_call | solution.py:503
  79.3 11.7 %all_to_all.39 = bf16[16,8,256]{2,1,0:T(8,128)(2,1)S(1)} all-to-all(bf16[16,8,256]{2,1,0:T(8,128)(2,1)S(1)} %bitcast.41), channel_id=1, replica_groups=mesh['seq_0'=4,'seq_1'=8,'seq_2'=2,'frame'=4] {'seq_2','seq_1'}, dimensions={0} | all-to-all | bytes 131072 | tf_op jit(solution)/shard_map/all_to_all | solution.py:532
  91.0 0.2 inner_second.1
  91.2 9.6 %all_to_all.40 = bf16[16,8,256]{2,1,0:T(8,128)(2,1)S(1)} all-to-all(bf16[16,8,256]{2,1,0:T(8,128)(2,1)S(1)} %bitcast.43), channel_id=1, replica_groups=mesh['seq_0'=4,'seq_1'=8,'seq_2'=2,'frame'=4] {'seq_0','frame'}, dimensions={0} | all-to-all | bytes 131072 | tf_op jit(solution)/shard_map/all_to_all | solution.py:532
  100.8 0.8 outer_second.1
  101.6 5.7 %all-to-all-start.6 = ((bf16[16,8,256]{2,1,0:T(8,128)(2,1)}), bf16[16,8,256]{2,1,0:T(8,128)(2,1)S(1)}, u32[]{:S(2)}, u32[]{:S(2)}) async-start(bf16[16,8,256]{2,1,0:T(8,128)(2,1)} %bitcast.27), calls=%async_computation.6 | async-start | bytes 131072 | tf_op jit(solution)/shard_map/all_to_all | solution.py:532
  107.3 1.4 %row_scan_back.1 = (f32[256,512]{1,0:T(8,128)S(1)}, bf16[256,256]{1,0:T(8,128)(2,1)S(1)}, f32[1,512]{1,0:T(1,128)S(1)}) custom-call(bf16[256,512]{1,0:T(8,128)(2,1)S(1)} %get-tuple-element.67.value_ref, bf16[2,64,128]{2,1,0:T(8,128)(2,1)} %bitcast.48, f32[16,256]{1,0:T(8,128)S(1)} %get-tuple-element.68.rows_ref, ...), custom_call_target="tpu_custom_call" | custom-call | flops 1000000000 | bytes 1048576 | tf_op jit(solution)/shard_map/row_scan_back/pallas_call | solution.py:503
  108.7 0.0 copy-start.2
  108.7 0.0 copy-start.3
  108.7 2.1 %col_scan.1 = (f32[256,512]{1,0:T(8,128)S(1)}, bf16[256,256]{1,0:T(8,128)(2,1)S(1)}, bf16[256,512]{1,0:T(8,128)(2,1)}) custom-call(bf16[256,512]{1,0:T(8,128)(2,1)S(1)} %get-tuple-element.62.value_ref, bf16[2,64,128]{2,1,0:T(8,128)(2,1)} %bitcast.51, f32[16,256]{1,0:T(8,128)S(1)} %get-tuple-element.63.rows_ref, ...), custom_call_target="tpu_custom_call" | custom-call | flops 1000000000 | bytes 1048576 | tf_op jit(solution)/shard_map/col_scan/pallas_call | solution.py:503
  110.8 3.6 %all-to-all-done.6 = bf16[16,8,256]{2,1,0:T(8,128)(2,1)S(1)} async-done(((bf16[16,8,256]{2,1,0:T(8,128)(2,1)}), bf16[16,8,256]{2,1,0:T(8,128)(2,1)S(1)}, u32[]{:S(2)}, u32[]{:S(2)}) %all-to-all-start.6) | async-done | bytes 65568 | tf_op jit(solution)/shard_map/all_to_all | solution.py:532
  114.5 0.0 copy-done.2
  114.5 0.0 copy-done.3
  114.5 2.3 %end.1 = (bf16[256,512]{1,0:T(8,128)(2,1)}, bf16[256,512]{1,0:T(8,128)(2,1)}) custom-call(bf16[128,256]{1,0:T(8,128)(2,1)S(1)} %bitcast.39, bf16[256,256]{1,0:T(8,128)(2,1)S(1)} %get-tuple-element.65.cplaced_ref, f32[256,32]{1,0:T(8,128)S(1)} %get-tuple-element.50.ccols_ref.cols_ref, f32[256,512]{1,0:T(8,128)S(1)} %get-tuple-element.66.clocal_ref, ...), custom_call_target="tpu_custom_call" | custom-call | flops 1000000000 | bytes 1048576 | tf_op jit(solution)/shard_map/end/pallas_call | solution.py:503
Async XLA Ops:
  0.6 46.8 %copy-start.1 = (bf16[512,512]{1,0:T(8,128)(2,1)S(1)}, bf16[512,512]{1,0:T(8,128)(2,1)}, u32[]{:S(2)}) copy-start(bf16[512,512]{1,0:T(8,128)(2,1)} %win_ref.3) | copy-start | bytes 1572868
  4.4 43.0 %copy-start = (bf16[512,512]{1,0:T(8,128)(2,1)S(1)}, bf16[512,512]{1,0:T(8,128)(2,1)}, u32[]{:S(2)}) copy-start(bf16[512,512]{1,0:T(8,128)(2,1)} %wout_ref.3) | copy-start | bytes 1572868
  50.1 27.2 %copy-start.4 = (bf16[1,2,128,64]{2,3,1,0:T(8,128)(2,1)S(1)}, bf16[1,2,128,64]{2,3,1,0:T(8,128)(2,1)}, u32[]{:S(2)}) copy-start(bf16[1,2,128,64]{2,3,1,0:T(8,128)(2,1)} %param.15) | copy-start | bytes 98308
  50.1 27.2 %copy-start.5 = (bf16[1,2,128,64]{2,3,1,0:T(8,128)(2,1)S(1)}, bf16[1,2,128,64]{2,3,1,0:T(8,128)(2,1)}, u32[]{:S(2)}) copy-start(bf16[1,2,128,64]{2,3,1,0:T(8,128)(2,1)} %param.21) | copy-start | bytes 98308
  101.6 12.8 %all-to-all-start.6 = ((bf16[16,8,256]{2,1,0:T(8,128)(2,1)}), bf16[16,8,256]{2,1,0:T(8,128)(2,1)S(1)}, u32[]{:S(2)}, u32[]{:S(2)}) async-start(bf16[16,8,256]{2,1,0:T(8,128)(2,1)} %bitcast.27), calls=%async_computation.6 | async-start | bytes 131072 | tf_op jit(solution)/shard_map/all_to_all | solution.py:532
  108.7 5.8 %copy-start.2 = (bf16[512,512]{1,0:T(8,128)(2,1)S(1)}, bf16[512,512]{1,0:T(8,128)(2,1)}, u32[]{:S(2)}) copy-start(bf16[512,512]{1,0:T(8,128)(2,1)} %rwin_ref.1) | copy-start | bytes 1572868
  108.7 5.7 %copy-start.3 = (bf16[1,2,128,512]{3,2,1,0:T(8,128)(2,1)S(1)}, bf16[1,2,128,512]{3,2,1,0:T(8,128)(2,1)}, u32[]{:S(2)}) copy-start(bf16[1,2,128,512]{3,2,1,0:T(8,128)(2,1)} %param.14) | copy-start | bytes 786436

commit v5 on v4

--- a/solution.py
+++ b/solution.py
@@ -200,17 +200,17 @@
     x_hbm, rsel_hbm, rlam_hbm, rskip_hbm, gain_hbm, win_hbm,
     y_hbm, csel_hbm, clam_hbm, cskip_hbm, wout_hbm,
     rlocal_ref, rcols_ref, rrows_ref, rplaced_ref, clocal_ref, ccols_ref, crows_ref, cplaced_ref,
-    sent_hbm, message_ref,
+    sent_ref, message_ref,
     x_ref, rsel_ref, rlam_ref, rskip_ref, gain_ref, win_ref,
-    y_ref, csel_ref, clam_ref, cskip_ref, wout_ref, value_ref, pulled_ref, sent_ref, sem,
+    y_ref, csel_ref, clam_ref, cskip_ref, wout_ref, value_ref, pulled_ref, sem,
 ):
     pairs = (
         (rlam_hbm, rlam_ref), (clam_hbm, clam_ref), (rsel_hbm, rsel_ref), (csel_hbm, csel_ref),
         (rskip_hbm, rskip_ref), (cskip_hbm, cskip_ref), (gain_hbm, gain_ref), (x_hbm, x_ref),
-        (win_hbm, win_ref), (y_hbm, y_ref), (wout_hbm, wout_ref), (sent_ref, sent_hbm),
+        (win_hbm, win_ref), (y_hbm, y_ref), (wout_hbm, wout_ref),
     )
     copies = [pltpu.make_async_copy(a, b, sem.at[i]) for i, (a, b) in enumerate(pairs)]
-    for copy in copies[:11]:
+    for copy in copies:
         copy.start()
     for copy in copies[:7]:
         copy.wait()
@@ -247,7 +247,6 @@
     first = state_rows(weighted, rsel, 0, 0)
     copies[9].wait()
     sent_ref[...] = to_message(y_ref[...], column_target)
-    copies[11].start()
     local_scan(value_ref, rsel, rrows, rcols, rskip_ref, rlocal_ref, False)
     copies[10].wait()
     pulled = nt(y_ref[...], wout_ref[...]).astype(BF16)
@@ -256,7 +255,6 @@
     second = state_rows(weighted, csel, STATE, 1)
     message_ref[:, :HALF] = (first + second).astype(BF16)
     local_scan(pulled_ref, csel, crows, ccols, cskip_ref, clocal_ref, True)
-    copies[11].wait()
 
 
 def logs_spread(tiles):
@@ -370,16 +368,12 @@
 
 def finish_kernel(
     rlocal_ref, rcols_ref, rplaced_ref, got_ref, wout_ref,
-    clocal_ref, ccols_ref, cplaced_ref, win_ref, gain_hbm, x_hbm, sent_hbm,
-    mixed_ref, message_ref, gain_ref, x_ref, sem,
-):
-    copies = [
-        pltpu.make_async_copy(x_hbm, x_ref, sem.at[0]),
-        pltpu.make_async_copy(gain_hbm, gain_ref, sem.at[1]),
-        pltpu.make_async_copy(sent_hbm, message_ref.at[:, HALF : 2 * HALF], sem.at[2]),
-    ]
-    for copy in copies:
-        copy.start()
+    clocal_ref, ccols_ref, cplaced_ref, win_ref, gain_hbm, x_ref, sent_ref,
+    mixed_ref, message_ref, gain_ref, sem,
+):
+    gain_in = pltpu.make_async_copy(gain_hbm, gain_ref, sem.at[0])
+    gain_in.start()
+    message_ref[:, HALF : 2 * HALF] = sent_ref[...]
     got = got_ref[...]
     carried = carried_of(rplaced_ref[...], got) * spread_heads(rcols_ref[...], OPENING)
     scanned = (rlocal_ref[...] + carried).astype(BF16)
@@ -387,14 +381,12 @@
     carried = carried_of(cplaced_ref[...], got) * spread_heads(ccols_ref[...], ENDING)
     scanned = (clocal_ref[...] + carried).astype(BF16)
     returned = nt(scanned, win_ref[...])
-    copies[0].wait()
     mixed = (x_ref[...].astype(F32) + total).astype(BF16)
     mixed_ref[...] = mixed
     message_ref[:, :HALF] = to_message(mixed, row_target)
-    copies[1].wait()
+    gain_in.wait()
     scaled = (gain_ref[...] * returned).astype(BF16)
     message_ref[:, 2 * HALF :] = to_message(scaled, column_target)
-    copies[2].wait()
 
 
 def cross_kernel(
@@ -419,9 +411,8 @@
 
 
 def col_scan_kernel(
-    value_ref, sel_ref, rows_ref, cols_ref, skip_ref, x_ref, local_ref, placed_ref, kept_ref
-):
-    kept_ref[...] = x_ref[...]
+    value_ref, sel_ref, rows_ref, cols_ref, skip_ref, local_ref, placed_ref
+):
     select = turned_select(sel_ref)
     placed_ref[...] = placed(select, STATE, 1)
     local_scan(value_ref, select, rows_ref[...], cols_ref[...], skip_ref, local_ref, False)
@@ -438,27 +429,25 @@
 
 def end_kernel(
     got_ref, cplaced_ref, ccols_ref, clocal_ref, rplaced_ref, rcols_ref, rlocal_ref, rwin_ref,
-    gain_ref, x_ref, y_ref, cx_hbm, cwout_hbm,
-    mixed_hbm, grad_hbm, cx_ref, cwout_ref, mixed_ref, grad_ref, sem,
+    gain_ref, x_ref, y_ref, cx_ref, cwout_hbm,
+    mixed_hbm, grad_hbm, cwout_ref, mixed_ref, grad_ref, sem,
 ):
     def copy(a, b, i):
         return pltpu.make_async_copy(a, b, sem.at[i])
 
-    cwout_in, cx_in = copy(cwout_hbm, cwout_ref, 0), copy(cx_hbm, cx_ref, 1)
+    cwout_in = copy(cwout_hbm, cwout_ref, 0)
     cwout_in.start()
-    cx_in.start()
     got = got_ref[...]
     carried = carried_of(rplaced_ref[...], got) * spread_heads(rcols_ref[...], ENDING)
     scanned = (rlocal_ref[...] + carried).astype(BF16)
     scaled = gain_ref[...] * nt(scanned, rwin_ref[...])
     grad_ref[...] = input_gradient(x_ref[...].astype(F32), y_ref[...].astype(F32), scaled)
-    grad_out = copy(grad_ref, grad_hbm, 2)
+    grad_out = copy(grad_ref, grad_hbm, 1)
     grad_out.start()
     carried = carried_of(cplaced_ref[...], got) * spread_heads(ccols_ref[...], OPENING)
     scanned = (clocal_ref[...] + carried).astype(BF16)
     cwout_in.wait()
-    cx_in.wait()
-    outs = [copy(mixed_ref.at[rows], mixed_hbm.at[rows], 3 + k) for k, rows in enumerate(QUARTERS)]
+    outs = [copy(mixed_ref.at[rows], mixed_hbm.at[rows], 2 + k) for k, rows in enumerate(QUARTERS)]
     for rows, out in zip(QUARTERS, outs):
         mixed = cx_ref[rows, :].astype(F32) + nn(scanned[rows, :], cwout_ref[...])
         mixed_ref[rows, :] = mixed.astype(BF16)
@@ -552,17 +541,16 @@
         start_kernel, "start",
         [Near((TOKS, F32)), Near((COLS, F32)), Near((ROWS, F32)), Near((PAIR, BF16)),
          Near((TOKS, F32)), Near((COLS, F32)), Near((ROWS, F32)), Near((PAIR, BF16)),
-         Far((BIG, BF16)), Near((LOGGED, BF16))],
+         Near((BIG, BF16)), Near((LOGGED, BF16))],
         [far(a) for a in
          (x, rsel, rlam, rskip, rgain, row_in, y, csel, clam, cskip, col_out)],
-        left=range(11), kept=(8,),
+        left=range(11),
         scratch=[
             pltpu.VMEM(TOKS, BF16), pltpu.VMEM(SEL, BF16), pltpu.VMEM(LAM, F32),
             pltpu.VMEM((1, HEADS), F32), pltpu.VMEM((1, WIDTH), F32),
             pltpu.VMEM((WIDTH, WIDTH), BF16), pltpu.VMEM(TOKS, BF16), pltpu.VMEM(SEL, BF16),
             pltpu.VMEM(LAM, F32), pltpu.VMEM((1, HEADS), F32), pltpu.VMEM((WIDTH, WIDTH), BF16),
-            pltpu.VMEM(TOKS, BF16), pltpu.VMEM(TOKS, BF16), pltpu.VMEM(BIG, BF16),
-            pltpu.SemaphoreType.DMA((12,)),
+            pltpu.VMEM(TOKS, BF16), pltpu.VMEM(TOKS, BF16), pltpu.SemaphoreType.DMA((11,)),
         ],
     )
     message, mine = lax.optimization_barrier((message, mine))
@@ -582,9 +570,9 @@
         finish_kernel, "finish",
         [Near((TOKS, BF16)), Near((WIDE, BF16)), Near(((1, WIDTH), F32))],
         [rlocal, rcols, rplaced, got, near(row_out), clocal, ccols, cplaced, near(col_in),
-         far(cgain), far(x), far(sent)],
-        left=(9, 10, 11),
-        scratch=[pltpu.VMEM(TOKS, BF16), pltpu.SemaphoreType.DMA((3,))],
+         far(cgain), near(x), sent],
+        left=(9,),
+        scratch=[pltpu.SemaphoreType.DMA((1,))],
     )
     arrived = swapped(sending, SEQ)
     cx, cvalue, ry, rpulled, message = call(
@@ -606,9 +594,9 @@
         scratch=[pltpu.VMEM(MSG, F32)], flops=1e7,
     )
     got = swapped(down, INNER)
-    clocal, cplaced, cx = call(
-        col_scan_kernel, "col_scan", [Near((TOKS, F32)), Near((PAIR, BF16)), Far((TOKS, BF16))],
-        [cvalue, far(csel), crows, ccols, far(cskip), cx],
+    clocal, cplaced = call(
+        col_scan_kernel, "col_scan", [Near((TOKS, F32)), Near((PAIR, BF16))],
+        [cvalue, far(csel), crows, ccols, far(cskip)],
     )
     rlocal, rplaced, gain = call(
         row_scan_back_kernel, "row_scan_back",
@@ -618,11 +606,11 @@
     mixed, grad = call(
         end_kernel, "end", [Far((TOKS, BF16)), Far((TOKS, BF16))],
         [near(got), cplaced, ccols, clocal, rplaced, rcols, rlocal, near(row_in),
-         gain, near(x), ry, far(cx), far(col_out)],
-        left=(11, 12), kept=(0, 1),
+         gain, near(x), ry, cx, far(col_out)],
+        left=(12,), kept=(0, 1),
         scratch=[
-            pltpu.VMEM(TOKS, BF16), pltpu.VMEM((WIDTH, WIDTH), BF16), pltpu.VMEM(TOKS, BF16),
-            pltpu.VMEM(TOKS, BF16), pltpu.SemaphoreType.DMA((7,)),
+            pltpu.VMEM((WIDTH, WIDTH), BF16), pltpu.VMEM(TOKS, BF16), pltpu.VMEM(TOKS, BF16),
+            pltpu.SemaphoreType.DMA((6,)),
         ],
     )
     return mixed.reshape(cotangent.shape), grad.reshape(tokens.shape)

time: 117 us -> 116 us (level)
  Pallas kernels: 15.6 us -> 14 us
    pallas_call x10, Pallas kernels: 15.6 us -> 14 us  [call(): pl.pallas_call(kernel, name=name, out_shape=[shaped(out) for out in outs]...]
  transfers between devices with their start and end apart: 1 -> 1, of which waited for: 1 -> 1; matrix products, arithmetic and copies ran while one was open for 0% -> 0% of each run, Pallas kernels for 3% -> 2%
where the time goes in v5:
time: 116 us
  blocking collectives  91.1 us (79%)
  Pallas kernels  14 us (12%)
  starting transfers between devices  5.65 us (5%)
  waiting for transfers between devices  4.28 us (4%)
    all_to_all x6, blocking collectives, swapped(): lax.all_to_all(split, axes, split_axis=0, concat_axis=0, tiled=True)  91.1 us
    pallas_call x10, Pallas kernels, call(): pl.pallas_call(kernel, name=name, out_shape=[shaped(out) for out in outs]...  14 us
    all_to_all x1, starting transfers between devices, swapped(): lax.all_to_all(split, axes, split_axis=0, concat_axis=0, tiled=True)  5.65 us
    all_to_all x1, waiting for transfers between devices, swapped(): lax.all_to_all(split, axes, split_axis=0, concat_axis=0, tiled=True)  4.28 us
  transfers between devices with their start and end apart: 1, of which 1 were waited for; matrix products, arithmetic and copies ran while one was open for 0% of the time, Pallas kernels for 2%

profile of v5, /device:TPU:1, one launch (start us, length us, event | category | flops | bytes accessed | tf_op | source)
XLA Modules:
  0.0 115.7 jit_solution(16415213007766529028)
XLA Ops:
  0.6 0.0 copy-start.1
  0.6 3.8 %start.1 = (f32[256,512]{1,0:T(8,128)S(1)}, f32[256,32]{1,0:T(8,128)S(1)}, f32[16,256]{1,0:T(8,128)S(1)}, bf16[256,256]{1,0:T(8,128)(2,1)S(1)}, f32[256,512]{1,0...) custom-call(bf16[256,512]{1,0:T(8,128)(2,1)} %bitcast.44, ...), custom_call_target="tpu_custom_call" | custom-call | flops 1000000000 | bytes 1048576 | tf_op jit(solution)/shard_map/start/pallas_call | solution.py:492
  4.4 0.0 copy-start
  4.4 17.3 %all_to_all.35 = bf16[16,8,384]{2,1,0:T(8,128)(2,1)S(1)} all-to-all(bf16[16,8,384]{2,1,0:T(8,128)(2,1)S(1)} %bitcast.37), channel_id=1, replica_groups=mesh['seq_0'=4,'seq_1'=8,'seq_2'=2,'frame'=4] {'seq_2','seq_1'}, dimensions={0} | all-to-all | bytes 196608 | tf_op jit(solution)/shard_map/all_to_all | solution.py:521
  21.7 0.2 inner_first.1
  21.9 13.3 %all_to_all.36 = bf16[16,8,384]{2,1,0:T(8,128)(2,1)S(1)} all-to-all(bf16[16,8,384]{2,1,0:T(8,128)(2,1)S(1)} %bitcast.38), channel_id=1, replica_groups=mesh['seq_0'=4,'seq_1'=8,'seq_2'=2,'frame'=4] {'seq_0','frame'}, dimensions={0} | all-to-all | bytes 196608 | tf_op jit(solution)/shard_map/all_to_all | solution.py:521
  35.1 0.0 copy-start.3
  35.1 0.2 outer_first.1
  35.3 12.1 %all_to_all.37 = bf16[16,8,256]{2,1,0:T(8,128)(2,1)S(1)} all-to-all(bf16[16,8,256]{2,1,0:T(8,128)(2,1)S(1)} %bitcast.42), channel_id=1, replica_groups=mesh['seq_0'=4,'seq_1'=8,'seq_2'=2,'frame'=4] {'seq_2','seq_1'}, dimensions={0} | all-to-all | bytes 131072 | tf_op jit(solution)/shard_map/all_to_all | solution.py:521
  47.4 0.0 copy-done.1
  47.4 0.0 copy-done
  47.4 0.0 copy-done.3
  47.4 1.7 %finish.1 = (bf16[256,512]{1,0:T(8,128)(2,1)S(1)}, bf16[512,768]{1,0:T(8,128)(2,1)S(1)}, f32[1,512]{1,0:T(1,128)S(1)}) custom-call(f32[256,512]{1,0:T(8,128)S(1)} %get-tuple-element.40.rlocal_ref, f32[256,32]{1,0:T(8,128)S(1)} %get-tuple-element.41.rcols_ref.cols_ref, bf16[256,256]{1,0:T(8,128)(2,1)S(1)} %get-tuple-element.42.rplaced_ref, ...), custom_call_target="tpu_custom_call" | custom-call | flops 1000000000 | bytes 1048576 | tf_op jit(solution)/shard_map/finish/pallas_call | solution.py:492
  49.2 0.0 copy-start.4
  49.2 0.0 copy-start.5
  49.2 27.2 %all_to_all.38 = bf16[64,8,768]{2,1,0:T(8,128)(2,1)S(1)} all-to-all(bf16[64,8,768]{2,1,0:T(8,128)(2,1)S(1)} %bitcast.31), channel_id=1, replica_groups=mesh['seq_0'=4,'seq_1'=8,'seq_2'=2,'frame'=4] {'seq_0','seq_1','seq_2'}, dimensions={0} | all-to-all | bytes 1572864 | tf_op jit(solution)/shard_map/all_to_all | solution.py:521
  76.4 0.0 copy-done.4
  76.4 0.0 copy-done.5
  76.4 2.0 %cross.1 = (bf16[256,512]{1,0:T(8,128)(2,1)S(1)}, bf16[256,512]{1,0:T(8,128)(2,1)S(1)}, bf16[256,512]{1,0:T(8,128)(2,1)S(1)}, bf16[256,512]{1,0:T(8,128)(2,1)S(1)}, bf16[128,256]{1,0:T(8,128)(2,1)S(1)}) custom-call(bf16[512,768]{1,0:T(8,128)(2,1)S(1)} %bitcast.32, bf16[256,512]{1,0:T(8,128)(2,1)S(1)} %get-tuple-element.53.mixed_ref, ...), custom_call_target="tpu_custom_call" | custom-call | flops 1000000000 | bytes 1048576 | tf_op jit(solution)/shard_map/cross/pallas_call | solution.py:492
  78.4 11.7 %all_to_all.39 = bf16[16,8,256]{2,1,0:T(8,128)(2,1)S(1)} all-to-all(bf16[16,8,256]{2,1,0:T(8,128)(2,1)S(1)} %bitcast.41), channel_id=1, replica_groups=mesh['seq_0'=4,'seq_1'=8,'seq_2'=2,'frame'=4] {'seq_2','seq_1'}, dimensions={0} | all-to-all | bytes 131072 | tf_op jit(solution)/shard_map/all_to_all | solution.py:521
  90.1 0.2 inner_second.1
  90.3 9.6 %all_to_all.40 = bf16[16,8,256]{2,1,0:T(8,128)(2,1)S(1)} all-to-all(bf16[16,8,256]{2,1,0:T(8,128)(2,1)S(1)} %bitcast.43), channel_id=1, replica_groups=mesh['seq_0'=4,'seq_1'=8,'seq_2'=2,'frame'=4] {'seq_0','frame'}, dimensions={0} | all-to-all | bytes 131072 | tf_op jit(solution)/shard_map/all_to_all | solution.py:521
  99.9 0.8 outer_second.1
  100.7 5.7 %all-to-all-start.6 = ((bf16[16,8,256]{2,1,0:T(8,128)(2,1)}), bf16[16,8,256]{2,1,0:T(8,128)(2,1)S(1)}, u32[]{:S(2)}, u32[]{:S(2)}) async-start(bf16[16,8,256]{2,1,0:T(8,128)(2,1)} %bitcast.27), calls=%async_computation.6 | async-start | bytes 131072 | tf_op jit(solution)/shard_map/all_to_all | solution.py:521
  106.4 1.4 %col_scan.1 = (f32[256,512]{1,0:T(8,128)S(1)}, bf16[256,256]{1,0:T(8,128)(2,1)S(1)}) custom-call(bf16[256,512]{1,0:T(8,128)(2,1)S(1)} %get-tuple-element.61.value_ref, bf16[2,64,128]{2,1,0:T(8,128)(2,1)} %bitcast.48, f32[16,256]{1,0:T(8,128)S(1)} %get-tuple-element.62.rows_ref, f32[256,32]{1,0:T(8,128)S(1)} %get-tuple-element.49.ccols_ref.cols_ref, ...), custom_call_target="tpu_custom_call" | custom-call | flops 1000000000 | bytes 1048576 | tf_op jit(solution)/shard_map/col_scan/pallas_call | solution.py:492
  107.8 0.0 copy-start.2
  107.8 1.5 %row_scan_back.1 = (f32[256,512]{1,0:T(8,128)S(1)}, bf16[256,256]{1,0:T(8,128)(2,1)S(1)}, f32[1,512]{1,0:T(1,128)S(1)}) custom-call(bf16[256,512]{1,0:T(8,128)(2,1)S(1)} %get-tuple-element.65.value_ref, bf16[2,64,128]{2,1,0:T(8,128)(2,1)} %bitcast.51, f32[16,256]{1,0:T(8,128)S(1)} %get-tuple-element.66.rows_ref, ...), custom_call_target="tpu_custom_call" | custom-call | flops 1000000000 | bytes 1048576 | tf_op jit(solution)/shard_map/row_scan_back/pallas_call | solution.py:492
  109.2 4.3 %all-to-all-done.6 = bf16[16,8,256]{2,1,0:T(8,128)(2,1)S(1)} async-done(((bf16[16,8,256]{2,1,0:T(8,128)(2,1)}), bf16[16,8,256]{2,1,0:T(8,128)(2,1)S(1)}, u32[]{:S(2)}, u32[]{:S(2)}) %all-to-all-start.6) | async-done | bytes 65568 | tf_op jit(solution)/shard_map/all_to_all | solution.py:521
  113.5 0.0 copy-done.2
  113.5 2.2 %end.1 = (bf16[256,512]{1,0:T(8,128)(2,1)}, bf16[256,512]{1,0:T(8,128)(2,1)}) custom-call(bf16[128,256]{1,0:T(8,128)(2,1)S(1)} %bitcast.39, bf16[256,256]{1,0:T(8,128)(2,1)S(1)} %get-tuple-element.63.cplaced_ref, f32[256,32]{1,0:T(8,128)S(1)} %get-tuple-element.49.ccols_ref.cols_ref, f32[256,512]{1,0:T(8,128)S(1)} %get-tuple-element.64.clocal_ref, ...), custom_call_target="tpu_custom_call" | custom-call | flops 1000000000 | bytes 1048576 | tf_op jit(solution)/shard_map/end/pallas_call | solution.py:492
Async XLA Ops:
  0.6 46.8 %copy-start.1 = (bf16[512,512]{1,0:T(8,128)(2,1)S(1)}, bf16[512,512]{1,0:T(8,128)(2,1)}, u32[]{:S(2)}) copy-start(bf16[512,512]{1,0:T(8,128)(2,1)} %win_ref.3) | copy-start | bytes 1572868
  4.4 43.0 %copy-start = (bf16[512,512]{1,0:T(8,128)(2,1)S(1)}, bf16[512,512]{1,0:T(8,128)(2,1)}, u32[]{:S(2)}) copy-start(bf16[512,512]{1,0:T(8,128)(2,1)} %wout_ref.3) | copy-start | bytes 1572868
  35.1 12.3 %copy-start.3 = (bf16[1,2,128,512]{3,2,1,0:T(8,128)(2,1)S(1)}, bf16[1,2,128,512]{3,2,1,0:T(8,128)(2,1)}, u32[]{:S(2)}) copy-start(bf16[1,2,128,512]{3,2,1,0:T(8,128)(2,1)} %param.14) | copy-start | bytes 786436
  49.2 27.2 %copy-start.4 = (bf16[1,2,128,64]{2,3,1,0:T(8,128)(2,1)S(1)}, bf16[1,2,128,64]{2,3,1,0:T(8,128)(2,1)}, u32[]{:S(2)}) copy-start(bf16[1,2,128,64]{2,3,1,0:T(8,128)(2,1)} %param.21) | copy-start | bytes 98308
  49.2 27.2 %copy-start.5 = (bf16[1,2,128,64]{2,3,1,0:T(8,128)(2,1)S(1)}, bf16[1,2,128,64]{2,3,1,0:T(8,128)(2,1)}, u32[]{:S(2)}) copy-start(bf16[1,2,128,64]{2,3,1,0:T(8,128)(2,1)} %param.15) | copy-start | bytes 98308
  100.7 12.8 %all-to-all-start.6 = ((bf16[16,8,256]{2,1,0:T(8,128)(2,1)}), bf16[16,8,256]{2,1,0:T(8,128)(2,1)S(1)}, u32[]{:S(2)}, u32[]{:S(2)}) async-start(bf16[16,8,256]{2,1,0:T(8,128)(2,1)} %bitcast.27), calls=%async_computation.6 | async-start | bytes 131072 | tf_op jit(solution)/shard_map/all_to_all | solution.py:521
  107.8 5.8 %copy-start.2 = (bf16[512,512]{1,0:T(8,128)(2,1)S(1)}, bf16[512,512]{1,0:T(8,128)(2,1)}, u32[]{:S(2)}) copy-start(bf16[512,512]{1,0:T(8,128)(2,1)} %rwin_ref.1) | copy-start | bytes 1572868

commit v6 on v5

--- a/solution.py
+++ b/solution.py
@@ -393,8 +393,11 @@
     got_ref, mixed_ref, rsel_ref, rcols_ref, wout_ref, csel_ref, ccols_ref, gain_ref, win_ref,
     cx_ref, cvalue_ref, y_ref, pulled_ref, message_ref,
 ):
-    y = from_message(got_ref[:, HALF : 2 * HALF], row_target)
-    scaled = from_message(got_ref[:, 2 * HALF :], row_target)
+    off = iota((TOK, 2 * TOK), 1) - row_target(iota((TOK, 1), 0))
+    low = nn(onehot(off == 0), got_ref[:, HALF:])
+    high = nn(onehot(off == 4), got_ref[:, HALF:])
+    y = jnp.concatenate([low[:, :HALF], high[:, :HALF]], axis=1)
+    scaled = jnp.concatenate([low[:, HALF:], high[:, HALF:]], axis=1)
     y = input_gradient(mixed_ref[...].astype(F32), y, scaled)
     y_ref[...] = y
     pulled = nt(y, wout_ref[...]).astype(BF16)

time: 116 us -> 116 us (level)
  no operation moved by 1% of the time
where the time goes in v6:
time: 116 us
  blocking collectives  91.1 us (79%)
  Pallas kernels  13.9 us (12%)
  starting transfers between devices  5.65 us (5%)
  waiting for transfers between devices  4.28 us (4%)
    all_to_all x6, blocking collectives, swapped(): lax.all_to_all(split, axes, split_axis=0, concat_axis=0, tiled=True)  91.1 us
    pallas_call x10, Pallas kernels, call(): pl.pallas_call(kernel, name=name, out_shape=[shaped(out) for out in outs]...  13.9 us
    all_to_all x1, starting transfers between devices, swapped(): lax.all_to_all(split, axes, split_axis=0, concat_axis=0, tiled=True)  5.65 us
    all_to_all x1, waiting for transfers between devices, swapped(): lax.all_to_all(split, axes, split_axis=0, concat_axis=0, tiled=True)  4.28 us
  transfers between devices with their start and end apart: 1, of which 1 were waited for; matrix products, arithmetic and copies ran while one was open for 0% of the time, Pallas kernels for 2%

profile of v6, /device:TPU:1, one launch (start us, length us, event | category | flops | bytes accessed | tf_op | source)
XLA Modules:
  0.0 115.7 jit_solution(12220321231272196359)
XLA Ops:
  0.6 0.0 copy-start.1
  0.6 3.8 %start.1 = (f32[256,512]{1,0:T(8,128)S(1)}, f32[256,32]{1,0:T(8,128)S(1)}, f32[16,256]{1,0:T(8,128)S(1)}, bf16[256,256]{1,0:T(8,128)(2,1)S(1)}, f32[256,512]{1,0...) custom-call(bf16[256,512]{1,0:T(8,128)(2,1)} %bitcast.44, ...), custom_call_target="tpu_custom_call" | custom-call | flops 1000000000 | bytes 1048576 | tf_op jit(solution)/shard_map/start/pallas_call | solution.py:495
  4.4 0.0 copy-start
  4.4 17.3 %all_to_all.35 = bf16[16,8,384]{2,1,0:T(8,128)(2,1)S(1)} all-to-all(bf16[16,8,384]{2,1,0:T(8,128)(2,1)S(1)} %bitcast.37), channel_id=1, replica_groups=mesh['seq_0'=4,'seq_1'=8,'seq_2'=2,'frame'=4] {'seq_2','seq_1'}, dimensions={0} | all-to-all | bytes 196608 | tf_op jit(solution)/shard_map/all_to_all | solution.py:524
  21.7 0.2 inner_first.1
  21.9 13.3 %all_to_all.36 = bf16[16,8,384]{2,1,0:T(8,128)(2,1)S(1)} all-to-all(bf16[16,8,384]{2,1,0:T(8,128)(2,1)S(1)} %bitcast.38), channel_id=1, replica_groups=mesh['seq_0'=4,'seq_1'=8,'seq_2'=2,'frame'=4] {'seq_0','frame'}, dimensions={0} | all-to-all | bytes 196608 | tf_op jit(solution)/shard_map/all_to_all | solution.py:524
  35.1 0.0 copy-start.3
  35.1 0.2 outer_first.1
  35.3 12.1 %all_to_all.37 = bf16[16,8,256]{2,1,0:T(8,128)(2,1)S(1)} all-to-all(bf16[16,8,256]{2,1,0:T(8,128)(2,1)S(1)} %bitcast.42), channel_id=1, replica_groups=mesh['seq_0'=4,'seq_1'=8,'seq_2'=2,'frame'=4] {'seq_2','seq_1'}, dimensions={0} | all-to-all | bytes 131072 | tf_op jit(solution)/shard_map/all_to_all | solution.py:524
  47.4 0.0 copy-done.1
  47.4 0.0 copy-done
  47.4 0.0 copy-done.3
  47.4 1.7 %finish.1 = (bf16[256,512]{1,0:T(8,128)(2,1)S(1)}, bf16[512,768]{1,0:T(8,128)(2,1)S(1)}, f32[1,512]{1,0:T(1,128)S(1)}) custom-call(f32[256,512]{1,0:T(8,128)S(1)} %get-tuple-element.40.rlocal_ref, f32[256,32]{1,0:T(8,128)S(1)} %get-tuple-element.41.rcols_ref.cols_ref, bf16[256,256]{1,0:T(8,128)(2,1)S(1)} %get-tuple-element.42.rplaced_ref, ...), custom_call_target="tpu_custom_call" | custom-call | flops 1000000000 | bytes 1048576 | tf_op jit(solution)/shard_map/finish/pallas_call | solution.py:495
  49.2 0.0 copy-start.4
  49.2 0.0 copy-start.5
  49.2 27.2 %all_to_all.38 = bf16[64,8,768]{2,1,0:T(8,128)(2,1)S(1)} all-to-all(bf16[64,8,768]{2,1,0:T(8,128)(2,1)S(1)} %bitcast.31), channel_id=1, replica_groups=mesh['seq_0'=4,'seq_1'=8,'seq_2'=2,'frame'=4] {'seq_0','seq_1','seq_2'}, dimensions={0} | all-to-all | bytes 1572864 | tf_op jit(solution)/shard_map/all_to_all | solution.py:524
  76.4 0.0 copy-done.4
  76.4 0.0 copy-done.5
  76.4 2.0 %cross.1 = (bf16[256,512]{1,0:T(8,128)(2,1)S(1)}, bf16[256,512]{1,0:T(8,128)(2,1)S(1)}, bf16[256,512]{1,0:T(8,128)(2,1)S(1)}, bf16[256,512]{1,0:T(8,128)(2,1)S(1)}, bf16[128,256]{1,0:T(8,128)(2,1)S(1)}) custom-call(bf16[512,768]{1,0:T(8,128)(2,1)S(1)} %bitcast.32, bf16[256,512]{1,0:T(8,128)(2,1)S(1)} %get-tuple-element.53.mixed_ref, ...), custom_call_target="tpu_custom_call" | custom-call | flops 1000000000 | bytes 1048576 | tf_op jit(solution)/shard_map/cross/pallas_call | solution.py:495
  78.4 11.7 %all_to_all.39 = bf16[16,8,256]{2,1,0:T(8,128)(2,1)S(1)} all-to-all(bf16[16,8,256]{2,1,0:T(8,128)(2,1)S(1)} %bitcast.41), channel_id=1, replica_groups=mesh['seq_0'=4,'seq_1'=8,'seq_2'=2,'frame'=4] {'seq_2','seq_1'}, dimensions={0} | all-to-all | bytes 131072 | tf_op jit(solution)/shard_map/all_to_all | solution.py:524
  90.1 0.2 inner_second.1
  90.3 9.6 %all_to_all.40 = bf16[16,8,256]{2,1,0:T(8,128)(2,1)S(1)} all-to-all(bf16[16,8,256]{2,1,0:T(8,128)(2,1)S(1)} %bitcast.43), channel_id=1, replica_groups=mesh['seq_0'=4,'seq_1'=8,'seq_2'=2,'frame'=4] {'seq_0','frame'}, dimensions={0} | all-to-all | bytes 131072 | tf_op jit(solution)/shard_map/all_to_all | solution.py:524
  99.9 0.8 outer_second.1
  100.7 5.7 %all-to-all-start.6 = ((bf16[16,8,256]{2,1,0:T(8,128)(2,1)}), bf16[16,8,256]{2,1,0:T(8,128)(2,1)S(1)}, u32[]{:S(2)}, u32[]{:S(2)}) async-start(bf16[16,8,256]{2,1,0:T(8,128)(2,1)} %bitcast.27), calls=%async_computation.6 | async-start | bytes 131072 | tf_op jit(solution)/shard_map/all_to_all | solution.py:524
  106.4 1.4 %col_scan.1 = (f32[256,512]{1,0:T(8,128)S(1)}, bf16[256,256]{1,0:T(8,128)(2,1)S(1)}) custom-call(bf16[256,512]{1,0:T(8,128)(2,1)S(1)} %get-tuple-element.61.value_ref, bf16[2,64,128]{2,1,0:T(8,128)(2,1)} %bitcast.48, f32[16,256]{1,0:T(8,128)S(1)} %get-tuple-element.62.rows_ref, f32[256,32]{1,0:T(8,128)S(1)} %get-tuple-element.49.ccols_ref.cols_ref, ...), custom_call_target="tpu_custom_call" | custom-call | flops 1000000000 | bytes 1048576 | tf_op jit(solution)/shard_map/col_scan/pallas_call | solution.py:495
  107.7 0.0 copy-start.2
  107.8 1.5 %row_scan_back.1 = (f32[256,512]{1,0:T(8,128)S(1)}, bf16[256,256]{1,0:T(8,128)(2,1)S(1)}, f32[1,512]{1,0:T(1,128)S(1)}) custom-call(bf16[256,512]{1,0:T(8,128)(2,1)S(1)} %get-tuple-element.65.value_ref, bf16[2,64,128]{2,1,0:T(8,128)(2,1)} %bitcast.51, f32[16,256]{1,0:T(8,128)S(1)} %get-tuple-element.66.rows_ref, ...), custom_call_target="tpu_custom_call" | custom-call | flops 1000000000 | bytes 1048576 | tf_op jit(solution)/shard_map/row_scan_back/pallas_call | solution.py:495
  109.2 4.3 %all-to-all-done.6 = bf16[16,8,256]{2,1,0:T(8,128)(2,1)S(1)} async-done(((bf16[16,8,256]{2,1,0:T(8,128)(2,1)}), bf16[16,8,256]{2,1,0:T(8,128)(2,1)S(1)}, u32[]{:S(2)}, u32[]{:S(2)}) %all-to-all-start.6) | async-done | bytes 65568 | tf_op jit(solution)/shard_map/all_to_all | solution.py:524
  113.5 0.0 copy-done.2
  113.5 2.2 %end.1 = (bf16[256,512]{1,0:T(8,128)(2,1)}, bf16[256,512]{1,0:T(8,128)(2,1)}) custom-call(bf16[128,256]{1,0:T(8,128)(2,1)S(1)} %bitcast.39, bf16[256,256]{1,0:T(8,128)(2,1)S(1)} %get-tuple-element.63.cplaced_ref, f32[256,32]{1,0:T(8,128)S(1)} %get-tuple-element.49.ccols_ref.cols_ref, f32[256,512]{1,0:T(8,128)S(1)} %get-tuple-element.64.clocal_ref, ...), custom_call_target="tpu_custom_call" | custom-call | flops 1000000000 | bytes 1048576 | tf_op jit(solution)/shard_map/end/pallas_call | solution.py:495
Async XLA Ops:
  0.6 46.8 %copy-start.1 = (bf16[512,512]{1,0:T(8,128)(2,1)S(1)}, bf16[512,512]{1,0:T(8,128)(2,1)}, u32[]{:S(2)}) copy-start(bf16[512,512]{1,0:T(8,128)(2,1)} %win_ref.3) | copy-start | bytes 1572868
  4.4 43.0 %copy-start = (bf16[512,512]{1,0:T(8,128)(2,1)S(1)}, bf16[512,512]{1,0:T(8,128)(2,1)}, u32[]{:S(2)}) copy-start(bf16[512,512]{1,0:T(8,128)(2,1)} %wout_ref.3) | copy-start | bytes 1572868
  35.1 12.3 %copy-start.3 = (bf16[1,2,128,512]{3,2,1,0:T(8,128)(2,1)S(1)}, bf16[1,2,128,512]{3,2,1,0:T(8,128)(2,1)}, u32[]{:S(2)}) copy-start(bf16[1,2,128,512]{3,2,1,0:T(8,128)(2,1)} %param.14) | copy-start | bytes 786436
  49.2 27.2 %copy-start.4 = (bf16[1,2,128,64]{2,3,1,0:T(8,128)(2,1)S(1)}, bf16[1,2,128,64]{2,3,1,0:T(8,128)(2,1)}, u32[]{:S(2)}) copy-start(bf16[1,2,128,64]{2,3,1,0:T(8,128)(2,1)} %param.21) | copy-start | bytes 98308
  49.2 27.2 %copy-start.5 = (bf16[1,2,128,64]{2,3,1,0:T(8,128)(2,1)S(1)}, bf16[1,2,128,64]{2,3,1,0:T(8,128)(2,1)}, u32[]{:S(2)}) copy-start(bf16[1,2,128,64]{2,3,1,0:T(8,128)(2,1)} %param.15) | copy-start | bytes 98308
  100.7 12.8 %all-to-all-start.6 = ((bf16[16,8,256]{2,1,0:T(8,128)(2,1)}), bf16[16,8,256]{2,1,0:T(8,128)(2,1)S(1)}, u32[]{:S(2)}, u32[]{:S(2)}) async-start(bf16[16,8,256]{2,1,0:T(8,128)(2,1)} %bitcast.27), calls=%async_computation.6 | async-start | bytes 131072 | tf_op jit(solution)/shard_map/all_to_all | solution.py:524
  107.7 5.8 %copy-start.2 = (bf16[512,512]{1,0:T(8,128)(2,1)S(1)}, bf16[512,512]{1,0:T(8,128)(2,1)}, u32[]{:S(2)}) copy-start(bf16[512,512]{1,0:T(8,128)(2,1)} %rwin_ref.1) | copy-start | bytes 1572868

commit v7 on v5

--- a/solution.py
+++ b/solution.py
@@ -390,9 +390,15 @@
 
 
 def cross_kernel(
-    got_ref, mixed_ref, rsel_ref, rcols_ref, wout_ref, csel_ref, ccols_ref, gain_ref, win_ref,
-    cx_ref, cvalue_ref, y_ref, pulled_ref, message_ref,
+    got_ref, mixed_ref, rsel_ref, rcols_ref, rrows_ref, rskip_hbm, wout_ref,
+    csel_ref, ccols_ref, crows_ref, cskip_hbm, gain_ref, win_ref, rgain_hbm,
+    cx_ref, y_ref, rlocal_ref, rplaced_ref, clocal_ref, cplaced_ref, rgain_ref, message_ref,
+    rskip_ref, cskip_ref, value_ref, pulled_ref, sem,
 ):
+    pairs = ((rskip_hbm, rskip_ref), (cskip_hbm, cskip_ref), (rgain_hbm, rgain_ref))
+    copies = [pltpu.make_async_copy(a, b, sem.at[i]) for i, (a, b) in enumerate(pairs)]
+    for copy in copies:
+        copy.start()
     y = from_message(got_ref[:, HALF : 2 * HALF], row_target)
     scaled = from_message(got_ref[:, 2 * HALF :], row_target)
     y = input_gradient(mixed_ref[...].astype(F32), y, scaled)
@@ -404,27 +410,18 @@
     x = from_message(got_ref[:, :HALF], column_target)
     cx_ref[...] = x.astype(BF16)
     value = nn(normalized(x, gain_ref[...]), win_ref[...]).astype(BF16)
-    cvalue_ref[...] = value
+    value_ref[...] = value
     weighted = (value.astype(F32) * spread_heads(ccols_ref[...], ENDING)).astype(BF16)
     second = state_rows(weighted, turned_select(csel_ref), 0, 1)
     message_ref[...] = (first + second).astype(BF16)
-
-
-def col_scan_kernel(
-    value_ref, sel_ref, rows_ref, cols_ref, skip_ref, local_ref, placed_ref
-):
-    select = turned_select(sel_ref)
-    placed_ref[...] = placed(select, STATE, 1)
-    local_scan(value_ref, select, rows_ref[...], cols_ref[...], skip_ref, local_ref, False)
-
-
-def row_scan_back_kernel(
-    value_ref, sel_ref, rows_ref, cols_ref, skip_ref, gain_ref, local_ref, placed_ref, kept_ref
-):
-    kept_ref[...] = gain_ref[...]
-    select = turned_select(sel_ref)
-    placed_ref[...] = placed(select, 0, 0)
-    local_scan(value_ref, select, rows_ref[...], cols_ref[...], skip_ref, local_ref, True)
+    rsel = turned_select(rsel_ref)
+    csel = turned_select(csel_ref)
+    rplaced_ref[...] = placed(rsel, 0, 0)
+    cplaced_ref[...] = placed(csel, STATE, 1)
+    for copy in copies:
+        copy.wait()
+    local_scan(pulled_ref, rsel, rrows_ref[...], rcols_ref[...], rskip_ref, rlocal_ref, True)
+    local_scan(value_ref, csel, crows_ref[...], ccols_ref[...], cskip_ref, clocal_ref, False)
 
 
 def end_kernel(
@@ -575,12 +572,17 @@
         scratch=[pltpu.SemaphoreType.DMA((1,))],
     )
     arrived = swapped(sending, SEQ)
-    cx, cvalue, ry, rpulled, message = call(
+    cx, ry, rlocal, rplaced, clocal, cplaced, gain, message = call(
         cross_kernel, "cross",
-        [Near((TOKS, BF16)), Near((TOKS, BF16)), Near((TOKS, BF16)), Near((TOKS, BF16)),
-         Near((MSG, BF16))],
-        [near(arrived), rmixed, near(rsel), rcols, near(row_out), near(csel), ccols,
-         gain, near(col_in)],
+        [Near((TOKS, BF16)), Near((TOKS, BF16)), Near((TOKS, F32)), Near((PAIR, BF16)),
+         Near((TOKS, F32)), Near((PAIR, BF16)), Near(((1, WIDTH), F32)), Near((MSG, BF16))],
+        [near(arrived), rmixed, near(rsel), rcols, rrows, far(rskip), near(row_out),
+         near(csel), ccols, crows, far(cskip), gain, near(col_in), far(rgain)],
+        left=(5, 10, 13),
+        scratch=[
+            pltpu.VMEM((1, HEADS), F32), pltpu.VMEM((1, HEADS), F32), pltpu.VMEM(TOKS, BF16),
+            pltpu.VMEM(TOKS, BF16), pltpu.SemaphoreType.DMA((3,)),
+        ],
     )
     got = swapped(message, INNER)
     before, through, total = call(
@@ -594,15 +596,6 @@
         scratch=[pltpu.VMEM(MSG, F32)], flops=1e7,
     )
     got = swapped(down, INNER)
-    clocal, cplaced = call(
-        col_scan_kernel, "col_scan", [Near((TOKS, F32)), Near((PAIR, BF16))],
-        [cvalue, far(csel), crows, ccols, far(cskip)],
-    )
-    rlocal, rplaced, gain = call(
-        row_scan_back_kernel, "row_scan_back",
-        [Near((TOKS, F32)), Near((PAIR, BF16)), Near(((1, WIDTH), F32))],
-        [rpulled, far(rsel), rrows, rcols, far(rskip), far(rgain)],
-    )
     mixed, grad = call(
         end_kernel, "end", [Far((TOKS, BF16)), Far((TOKS, BF16))],
         [near(got), cplaced, ccols, clocal, rplaced, rcols, rlocal, near(row_in),

time: 116 us -> 116 us (level)
  blocking collectives: 91.1 us -> 103 us
  starting transfers between devices: 5.65 us -> 0 us
  waiting for transfers between devices: 4.28 us -> 0 us
  Pallas kernels: 14 us -> 11.7 us
    all_to_all x6 -> x7, blocking collectives: 91.1 us -> 103 us  [swapped(): lax.all_to_all(split, axes, split_axis=0, concat_axis=0, tiled=True)]
    all_to_all x1 -> x0, starting transfers between devices: 5.65 us -> none  [swapped(): lax.all_to_all(split, axes, split_axis=0, concat_axis=0, tiled=True)]
    all_to_all x1 -> x0, waiting for transfers between devices: 4.28 us -> none  [swapped(): lax.all_to_all(split, axes, split_axis=0, concat_axis=0, tiled=True)]
    pallas_call x10 -> x8, Pallas kernels: 14 us -> 11.7 us  [call(): pl.pallas_call(kernel, name=name, out_shape=[shaped(out) for out in outs]...]
  transfers between devices with their start and end apart: 1 -> 0, of which waited for: 1 -> 0; matrix products, arithmetic and copies ran while one was open for 0% -> 0% of each run, Pallas kernels for 2% -> 0%
where the time goes in v7:
time: 116 us
  blocking collectives  103 us (89%)
  Pallas kernels  11.7 us (10%)
    all_to_all x7, blocking collectives, swapped(): lax.all_to_all(split, axes, split_axis=0, concat_axis=0, tiled=True)  103 us
    pallas_call x8, Pallas kernels, call(): pl.pallas_call(kernel, name=name, out_shape=[shaped(out) for out in outs]...  11.7 us

profile of v7, /device:TPU:1, one launch (start us, length us, event | category | flops | bytes accessed | tf_op | source)
XLA Modules:
  0.0 115.6 jit_solution(1720707646694244082)
XLA Ops:
  0.6 0.0 copy-start.1
  0.6 3.8 %start.1 = (f32[256,512]{1,0:T(8,128)S(1)}, f32[256,32]{1,0:T(8,128)S(1)}, f32[16,256]{1,0:T(8,128)S(1)}, bf16[256,256]{1,0:T(8,128)(2,1)S(1)}, f32[256,512]{1,0...) custom-call(bf16[256,512]{1,0:T(8,128)(2,1)} %bitcast.45, ...), custom_call_target="tpu_custom_call" | custom-call | flops 1000000000 | bytes 1048576 | tf_op jit(solution)/shard_map/start/pallas_call | solution.py:489
  4.4 0.0 copy-start
  4.4 17.3 %all_to_all.35 = bf16[16,8,384]{2,1,0:T(8,128)(2,1)S(1)} all-to-all(bf16[16,8,384]{2,1,0:T(8,128)(2,1)S(1)} %bitcast.38), channel_id=1, replica_groups=mesh['seq_0'=4,'seq_1'=8,'seq_2'=2,'frame'=4] {'seq_2','seq_1'}, dimensions={0} | all-to-all | bytes 196608 | tf_op jit(solution)/shard_map/all_to_all | solution.py:518
  21.7 0.2 inner_first.1
  21.9 13.3 %all_to_all.36 = bf16[16,8,384]{2,1,0:T(8,128)(2,1)S(1)} all-to-all(bf16[16,8,384]{2,1,0:T(8,128)(2,1)S(1)} %bitcast.39), channel_id=1, replica_groups=mesh['seq_0'=4,'seq_1'=8,'seq_2'=2,'frame'=4] {'seq_0','frame'}, dimensions={0} | all-to-all | bytes 196608 | tf_op jit(solution)/shard_map/all_to_all | solution.py:518
  35.1 0.0 copy-start.3
  35.1 0.2 outer_first.1
  35.3 12.1 %all_to_all.37 = bf16[16,8,256]{2,1,0:T(8,128)(2,1)S(1)} all-to-all(bf16[16,8,256]{2,1,0:T(8,128)(2,1)S(1)} %bitcast.43), channel_id=1, replica_groups=mesh['seq_0'=4,'seq_1'=8,'seq_2'=2,'frame'=4] {'seq_2','seq_1'}, dimensions={0} | all-to-all | bytes 131072 | tf_op jit(solution)/shard_map/all_to_all | solution.py:518
  47.4 0.0 copy-done.1
  47.4 0.0 copy-done
  47.4 0.0 copy-done.3
  47.4 1.7 %finish.1 = (bf16[256,512]{1,0:T(8,128)(2,1)S(1)}, bf16[512,768]{1,0:T(8,128)(2,1)S(1)}, f32[1,512]{1,0:T(1,128)S(1)}) custom-call(f32[256,512]{1,0:T(8,128)S(1)} %get-tuple-element.38.rlocal_ref, f32[256,32]{1,0:T(8,128)S(1)} %get-tuple-element.39.rcols_ref, bf16[256,256]{1,0:T(8,128)(2,1)S(1)} %get-tuple-element.40.rplaced_ref, ...), custom_call_target="tpu_custom_call" | custom-call | flops 1000000000 | bytes 1048576 | tf_op jit(solution)/shard_map/finish/pallas_call | solution.py:489
  49.1 0.0 copy-start.4
  49.1 0.0 copy-start.5
  49.2 27.2 %all_to_all.38 = bf16[64,8,768]{2,1,0:T(8,128)(2,1)S(1)} all-to-all(bf16[64,8,768]{2,1,0:T(8,128)(2,1)S(1)} %bitcast.32), channel_id=1, replica_groups=mesh['seq_0'=4,'seq_1'=8,'seq_2'=2,'frame'=4] {'seq_0','seq_1','seq_2'}, dimensions={0} | all-to-all | bytes 1572864 | tf_op jit(solution)/shard_map/all_to_all | solution.py:518
  76.4 0.0 copy-done.4
  76.4 0.0 copy-done.5
  76.4 3.2 %cross.1 = (bf16[256,512]{1,0:T(8,128)(2,1)S(1)}, bf16[256,512]{1,0:T(8,128)(2,1)S(1)}, f32[256,512]{1,0:T(8,128)S(1)}, bf16[256,256]{1,0:T(8,128)(2,1)S(1)}, f3...) custom-call(bf16[512,768]{1,0:T(8,128)(2,1)S(1)} %bitcast.31, ...), custom_call_target="tpu_custom_call" | custom-call | flops 1000000000 | bytes 1048576 | tf_op jit(solution)/shard_map/cross/pallas_call | solution.py:489
  79.6 0.0 copy-start.2
  79.6 11.9 %all_to_all.39 = bf16[16,8,256]{2,1,0:T(8,128)(2,1)S(1)} all-to-all(bf16[16,8,256]{2,1,0:T(8,128)(2,1)S(1)} %bitcast.40), channel_id=1, replica_groups=mesh['seq_0'=4,'seq_1'=8,'seq_2'=2,'frame'=4] {'seq_2','seq_1'}, dimensions={0} | all-to-all | bytes 131072 | tf_op jit(solution)/shard_map/all_to_all | solution.py:518
  91.4 0.2 inner_second.1
  91.7 9.6 %all_to_all.40 = bf16[16,8,256]{2,1,0:T(8,128)(2,1)S(1)} all-to-all(bf16[16,8,256]{2,1,0:T(8,128)(2,1)S(1)} %bitcast.44), channel_id=1, replica_groups=mesh['seq_0'=4,'seq_1'=8,'seq_2'=2,'frame'=4] {'seq_0','frame'}, dimensions={0} | all-to-all | bytes 131072 | tf_op jit(solution)/shard_map/all_to_all | solution.py:518
  101.2 0.2 outer_second.1
  101.4 11.9 %all_to_all.41 = bf16[16,8,256]{2,1,0:T(8,128)(2,1)S(1)} all-to-all(bf16[16,8,256]{2,1,0:T(8,128)(2,1)S(1)} %bitcast.37), channel_id=1, replica_groups=mesh['seq_0'=4,'seq_1'=8,'seq_2'=2,'frame'=4] {'seq_2','seq_1'}, dimensions={0} | all-to-all | bytes 131072 | tf_op jit(solution)/shard_map/all_to_all | solution.py:518
  113.4 0.0 copy-done.2
  113.4 2.2 %end.1 = (bf16[256,512]{1,0:T(8,128)(2,1)}, bf16[256,512]{1,0:T(8,128)(2,1)}) custom-call(bf16[128,256]{1,0:T(8,128)(2,1)S(1)} %bitcast.41, bf16[256,256]{1,0:T(8,128)(2,1)S(1)} %get-tuple-element.61.cplaced_ref, f32[256,32]{1,0:T(8,128)S(1)} %get-tuple-element.47.ccols_ref, f32[256,512]{1,0:T(8,128)S(1)} %get-tuple-element.62.clocal_ref, ...), custom_call_target="tpu_custom_call" | custom-call | flops 1000000000 | bytes 1048576 | tf_op jit(solution)/shard_map/end/pallas_call | solution.py:489
Async XLA Ops:
  0.6 46.8 %copy-start.1 = (bf16[512,512]{1,0:T(8,128)(2,1)S(1)}, bf16[512,512]{1,0:T(8,128)(2,1)}, u32[]{:S(2)}) copy-start(bf16[512,512]{1,0:T(8,128)(2,1)} %win_ref.3) | copy-start | bytes 1572868
  4.4 43.0 %copy-start = (bf16[512,512]{1,0:T(8,128)(2,1)S(1)}, bf16[512,512]{1,0:T(8,128)(2,1)}, u32[]{:S(2)}) copy-start(bf16[512,512]{1,0:T(8,128)(2,1)} %wout_ref.3) | copy-start | bytes 1572868
  35.1 12.3 %copy-start.3 = (bf16[1,2,128,512]{3,2,1,0:T(8,128)(2,1)S(1)}, bf16[1,2,128,512]{3,2,1,0:T(8,128)(2,1)}, u32[]{:S(2)}) copy-start(bf16[1,2,128,512]{3,2,1,0:T(8,128)(2,1)} %param.14) | copy-start | bytes 786436
  49.1 27.2 %copy-start.4 = (bf16[1,2,128,64]{2,3,1,0:T(8,128)(2,1)S(1)}, bf16[1,2,128,64]{2,3,1,0:T(8,128)(2,1)}, u32[]{:S(2)}) copy-start(bf16[1,2,128,64]{2,3,1,0:T(8,128)(2,1)} %param.15) | copy-start | bytes 98308
  49.1 27.2 %copy-start.5 = (bf16[1,2,128,64]{2,3,1,0:T(8,128)(2,1)S(1)}, bf16[1,2,128,64]{2,3,1,0:T(8,128)(2,1)}, u32[]{:S(2)}) copy-start(bf16[1,2,128,64]{2,3,1,0:T(8,128)(2,1)} %param.21) | copy-start | bytes 98308
  79.6 33.8 %copy-start.2 = (bf16[512,512]{1,0:T(8,128)(2,1)S(1)}, bf16[512,512]{1,0:T(8,128)(2,1)}, u32[]{:S(2)}) copy-start(bf16[512,512]{1,0:T(8,128)(2,1)} %rwin_ref.1) | copy-start | bytes 1572868
